TPU v7x, 128 devices: a whole 4x4x4 slice. The times are simulated.
128 devices in a mesh: segment: 2 (over core), grp: 64 (over x, z, y).
Axes of the slice: x: 4, y: 4, z: 4, core: 2. Of those that a mesh axis runs over, the one named last changes fastest.
Arguments:
- monomer_density: bfloat16 [512, 9216], P('grp'), may hold values from -3 to 3
- monomer_centers: float32 [3, 512], replicated, may hold values from 0 to 8
- dimer_pairs: int32 [2, 1024], replicated, may hold values from 0 to 511, as said below
- basis_sizes: int32 [512], replicated, may hold values from 48 to 96
- dimer_core: float32 [1024, 36864], P('grp')
- esp_map: float32 [96, 192], replicated, may hold values from -0.1875 to 0.1875
- repulsion: float32 [36864], replicated, may hold values from 0.005 to 0.05
Outputs:
- section_out: float32 [2, 1024, 36864], P('segment', 'grp')
- window_energy: float32 [], replicated
Inputs may be any that keep to these rules, and one draw needn't show every extreme that they name: `dimer_pairs`: the two monomers of a dimer differ.
All inputs are finite; a program needn't handle non-finite values. Where the computation divides by a largest or mean magnitude, that divisor is 1e-20 or more.
Results may differ from a plain program's by a relative error of at most 0.00045.
Values may be sent and summed in bfloat16 or wider, within the bound.
No kernel may reach another device: no remote copies, remote signals or barrier semaphores. Data moves between devices by JAX's collectives and lax.ppermute only.
A program may use at most 128 MiB of HBM per device.

v0:
```python
import jax
import jax.numpy as jnp
from jax import lax
from jax.experimental import pallas as pl
from jax.experimental.pallas import tpu as pltpu
from jax.sharding import Mesh
from jax.sharding import PartitionSpec as P


PURIFY = 8
SINGLE = (8, 4)
MIB = 1024 * 1024
GRP = ("grp_0", "grp_1", "grp_2")
ALL = ("segment", "grp_0", "grp_1", "grp_2")
STRIDES = ((1, 4, 16), (4, 16, 1))

BM = 96
BD = 192
FLAT = BD * BD
TILES = FLAT // 128
HALF = BM * BM // 2
LOCAL = 8
PITCH = 292
FPITCH = 73
epsilon = 1e-06
highest = lax.Precision.HIGHEST
f32 = jnp.float32
bf16 = jnp.bfloat16


def phase_shift(value, phase, step):
    pairs = []
    for core in range(2):
        stride = STRIDES[core][phase]
        for chip in range(64):
            place = (chip // stride) % 4
            target = chip + (((place + step) % 4) - place) * stride
            pairs.append((core * 64 + chip, core * 64 + target))
    return lax.ppermute(value, ALL, pairs)


def shifts(shift, *args):
    arrived = []
    for step in (1, 2, 3):
        arrived.append(shift(*args, step))
    return arrived


def axis_shift(value, axis, step):
    return lax.ppermute(value, axis, [(i, (i + step) % 4) for i in range(4)])


def swap_cores(value):
    return lax.ppermute(value, "segment", [(0, 1), (1, 0)])


def split_two(value):
    high = value.astype(bf16)
    low = (value - high.astype(f32)).astype(bf16)
    return high, low


def dot(left, right):
    return jnp.dot(left, right, preferred_element_type=f32)


def dot_three(left, right):
    (lh, ll), (rh, rl) = left, right
    return dot(lh, rh) + (dot(ll, rh) + dot(lh, rl))


def lane_index(rows):
    return lax.broadcasted_iota(jnp.int32, (rows, 128), 1)


def unflatten_kernel(segment_ref, core_ref, first_ref, second_ref, flat):
    for tile in range(TILES):
        flat[pl.ds(tile, LOCAL, stride=PITCH), :] = core_ref[:, tile * 128 : tile * 128 + 128]
    low_half = lane_index(BM) < 64
    for d in range(LOCAL):
        a = flat[pl.ds(d * PITCH, BM, stride=3), :]
        b = flat[pl.ds(d * PITCH + 1, BM, stride=3), :]
        c = flat[pl.ds(d * PITCH + 2, BM, stride=3), :]
        b_rolled = pltpu.roll(b, 64, 1)
        c_rolled = pltpu.roll(c, 64, 1)
        first_ref[pl.ds(d * BD, BM, stride=2), :] = a
        second_ref[pl.ds(d * BD, BM, stride=2), :] = b
        first_ref[pl.ds(d * BD + 1, BM, stride=2), :] = jnp.where(low_half, b_rolled, c_rolled)
        second_ref[pl.ds(d * BD + 1, BM, stride=2), :] = c_rolled


def unflatten(segment, core):
    return pl.pallas_call(
        unflatten_kernel,
        name="unflatten",
        grid_spec=pltpu.PrefetchScalarGridSpec(
            num_scalar_prefetch=1,
            grid=(1,),
            in_specs=[pl.BlockSpec((LOCAL, FLAT), lambda i, s: (s[0], 0))],
            out_specs=[pl.BlockSpec((LOCAL * BD, 128), lambda i, s: (0, 0))] * 2,
            scratch_shapes=[pltpu.VMEM((LOCAL * PITCH, 128), f32)],
        ),
        out_shape=[jax.ShapeDtypeStruct((LOCAL * BD, 128), f32)] * 2,
        cost_estimate=pl.CostEstimate(flops=20000000, bytes_accessed=3000000, transcendentals=0),
    )(segment, core)


def flatten_kernel(place_ref, square_ref, out_ref, first, second, flat):
    low_half = lane_index(BM) < 64
    for d in range(LOCAL):
        first[...] = square_ref[0, d, :, 0:128]
        second[:, 0:64] = square_ref[0, d, :, 128:192]
        even_a = first[pl.ds(0, BM, stride=2), :]
        even_b = second[pl.ds(0, BM, stride=2), :]
        odd_a = pltpu.roll(first[pl.ds(1, BM, stride=2), :], 64, 1)
        odd_b = pltpu.roll(second[pl.ds(1, BM, stride=2), :], 64, 1)
        flat[pl.ds(d * PITCH, BM, stride=3), :] = even_a
        flat[pl.ds(d * PITCH + 1, BM, stride=3), :] = jnp.where(low_half, even_b, odd_a)
        flat[pl.ds(d * PITCH + 2, BM, stride=3), :] = jnp.where(low_half, odd_a, odd_b)
    for tile in range(TILES):
        out_ref[:, tile * 128 : tile * 128 + 128] = flat[pl.ds(tile, LOCAL, stride=PITCH), :]


def flatten(place, stack, rows):
    return pl.pallas_call(
        flatten_kernel,
        name="flatten",
        grid_spec=pltpu.PrefetchScalarGridSpec(
            num_scalar_prefetch=1,
            grid=(1,),
            in_specs=[pl.BlockSpec((1, LOCAL, BD, BD), lambda i, p: (p[0], 0, 0, 0))],
            out_specs=pl.BlockSpec((LOCAL, FLAT), lambda i, p: (p[1], 0)),
            scratch_shapes=[
                pltpu.VMEM((BD, 128), f32),
                pltpu.VMEM((BD, 128), f32),
                pltpu.VMEM((LOCAL * PITCH, 128), f32),
            ],
        ),
        out_shape=jax.ShapeDtypeStruct((rows, FLAT), f32),
        cost_estimate=pl.CostEstimate(flops=20000000, bytes_accessed=3000000, transcendentals=0),
    )(place, stack)


def partial_kernel(weight_ref, b0, b1, b2, b3, o0, o1, o2, o3):
    for start in range(0, HALF, 512):
        columns = slice(start, start + 512)
        rows = jnp.concatenate([b[:, columns] for b in (b0, b1, b2, b3)], axis=0)
        total = dot(weight_ref[...], rows)
        for k, out in enumerate((o0, o1, o2, o3)):
            out[:, columns] = total[16 * k : 16 * k + 16]


def partial_fields(weights, blocks):
    return pl.pallas_call(
        partial_kernel,
        name="partial_fields",
        out_shape=[pltpu.HBM((16, HALF), f32)] * 4,
        compiler_params=pltpu.CompilerParams(vmem_limit_bytes=12 * MIB),
        cost_estimate=pl.CostEstimate(flops=80000000, bytes_accessed=2400000, transcendentals=0),
    )(weights, *blocks)


def live_square(n_first, n_second):
    row = lax.broadcasted_iota(jnp.int32, (BD, BD), 0)
    column = lax.broadcasted_iota(jnp.int32, (BD, BD), 1)

    def inside(position):
        limit = jnp.where(position < BM, n_first, n_second + BM)
        return position < limit

    live = jnp.logical_and(inside(row), inside(column))
    return live, row == column


def solve_kernel(
    segment_ref, sizes_ref, mine_any, theirs_any, first_any, second_any, esp_any, rep_any,
    stack, energy_out,
    mine_ref, theirs_ref, first_ref, second_ref, esp_ref, rep_ref, arrivals,
    flat, field, fock, work, work_h, work_l, square_h, square_l, diagonals,
):
    places = (
        (mine_any, mine_ref), (theirs_any, theirs_ref), (esp_any, esp_ref),
        (first_any, first_ref), (second_any, second_ref), (rep_any, rep_ref),
    )
    copies = [
        pltpu.make_async_copy(source, target, arrivals.at[i])
        for i, (source, target) in enumerate(places)
    ]
    for copy in copies:
        copy.start()
    copies[0].wait()
    copies[1].wait()
    core_out = stack.at[0]
    density_out = stack.at[1]
    segment = segment_ref[0]
    own_start = 36 * segment
    other_start = 36 - own_start
    for tile in range(36):
        columns = slice(tile * 128, tile * 128 + 128)
        flat[pl.ds(own_start + tile, LOCAL, stride=FPITCH), :] = mine_ref[:, columns]
        flat[pl.ds(other_start + tile, LOCAL, stride=FPITCH), :] = theirs_ref[:, columns]
    for copy in copies[2:]:
        copy.wait()
    esp = split_two(esp_ref[...])
    esp_t = split_two(esp_ref[...].T)
    repulsion = 0.5 * (rep_ref[...] + rep_ref[...].T)
    lane = lane_index(24)
    for d in range(LOCAL):
        a = flat[pl.ds(d * FPITCH, 24, stride=3), :]
        b = flat[pl.ds(d * FPITCH + 1, 24, stride=3), :]
        c = flat[pl.ds(d * FPITCH + 2, 24, stride=3), :]
        base = d * BM
        field[pl.ds(base, 24, stride=4), :] = a
        field[pl.ds(base + 1, 24, stride=4), :] = jnp.where(
            lane < 32, pltpu.roll(a, 32, 1), pltpu.roll(b, 32, 1)
        )
        field[pl.ds(base + 2, 24, stride=4), :] = jnp.where(
            lane < 64, pltpu.roll(b, 64, 1), pltpu.roll(c, 64, 1)
        )
        field[pl.ds(base + 3, 24, stride=4), :] = pltpu.roll(c, 96, 1)
    for d in range(LOCAL):
        left = dot_three(esp_t, split_two(field[d * BM : d * BM + BM, 0:BM]))
        potential = dot_three(split_two(left), esp)
        rows = slice(d * BD, d * BD + BD)
        core = jnp.concatenate([first_ref[rows, :], second_ref[rows, 0:64]], axis=1)
        total = core + potential
        core_out[d] = 0.5 * (total + total.T)

    def live_count(d):
        n_first = jnp.clip(sizes_ref[0, d], 0, BM)
        n_second = jnp.clip(sizes_ref[1, d], 0, BM)
        return n_first, n_second, (n_first + n_second).astype(f32)

    def purify(source, singles):
        for d in range(LOCAL):
            n_first, n_second, count = live_count(d)
            live, diagonal = live_square(n_first, n_second)
            masked = jnp.where(live, source[d], 0.0)
            on_diagonal = jnp.logical_and(live, diagonal)
            chemical = jnp.sum(jnp.where(diagonal, masked, 0.0)) / count
            shifted = masked - jnp.where(on_diagonal, chemical, 0.0)
            radius = jnp.max(jnp.sum(jnp.abs(shifted), axis=0, keepdims=True))
            work[d] = shifted * (-0.5 / (radius + epsilon))

        def single(_, carry):
            for d in range(LOCAL):
                high = work[d].astype(bf16)
                work_h[d] = high
                square_h[d] = dot(high, high).astype(bf16)
            for d in range(LOCAL):
                work[d] = 1.5 * work[d] - 2.0 * dot(square_h[d], work_h[d])
            return carry

        def triple(_, carry):
            for d in range(LOCAL):
                high, low = split_two(work[d])
                work_h[d] = high
                work_l[d] = low
                squared = dot_three((high, low), (high, low))
                square_h[d], square_l[d] = split_two(squared)
            for d in range(LOCAL):
                cubed = dot_three((square_h[d], square_l[d]), (work_h[d], work_l[d]))
                work[d] = 1.5 * work[d] - 2.0 * cubed
            return carry

        if singles > 0:
            lax.fori_loop(0, singles, single, 0)
        if singles < PURIFY:
            lax.fori_loop(singles, PURIFY, triple, 0)

    def density_of(d):
        n_first, n_second, count = live_count(d)
        live, diagonal = live_square(n_first, n_second)
        return work[d] + jnp.where(jnp.logical_and(live, diagonal), 0.5, 0.0), diagonal, count

    purify(core_out, SINGLE[0])
    for d in range(LOCAL):
        density, diagonal, _ = density_of(d)
        diagonals[d : d + 1, :] = jnp.sum(jnp.where(diagonal, density, 0.0), axis=0, keepdims=True)
    coulomb = jnp.dot(diagonals[...], repulsion, precision=highest, preferred_element_type=f32)
    for d in range(LOCAL):
        density, diagonal, _ = density_of(d)
        fock[d] = (
            core_out[d]
            + jnp.where(diagonal, coulomb[d : d + 1, :], 0.0)
            - 0.5 * (repulsion * density)
        )
    purify(fock, SINGLE[1])
    energy = jnp.zeros((1, BD), f32)
    for d in range(LOCAL):
        density, _, count = density_of(d)
        density_out[d] = density
        terms = jnp.sum(density * (core_out[d] + fock[d]), axis=0, keepdims=True)
        energy = energy + terms * (0.5 / count)
    energy_out[...] = jnp.full((8, 128), jnp.sum(energy), f32)


def solve(segment, sizes, mine, theirs, first, second, esp_map, repulsion):
    vmem = pl.BlockSpec(memory_space=pltpu.VMEM)
    smem = pl.BlockSpec(memory_space=pltpu.SMEM)
    square = (LOCAL, BD, BD)
    return pl.pallas_call(
        solve_kernel,
        name="solve",
        in_specs=[smem, smem] + [pl.BlockSpec(memory_space=pltpu.HBM)] * 6,
        out_specs=[vmem] * 2,
        out_shape=[
            jax.ShapeDtypeStruct((2,) + square, f32),
            jax.ShapeDtypeStruct((8, 128), f32),
        ],
        scratch_shapes=[
            pltpu.VMEM((LOCAL, HALF), f32),
            pltpu.VMEM((LOCAL, HALF), f32),
            pltpu.VMEM((LOCAL * BD, 128), f32),
            pltpu.VMEM((LOCAL * BD, 128), f32),
            pltpu.VMEM((BM, BD), f32),
            pltpu.VMEM((BD, BD), f32),
            pltpu.SemaphoreType.DMA((6,)),
            pltpu.VMEM((LOCAL * FPITCH, 128), f32),
            pltpu.VMEM((LOCAL * BM, 128), f32),
            pltpu.VMEM(square, f32),
            pltpu.VMEM(square, f32),
            pltpu.VMEM(square, bf16),
            pltpu.VMEM(square, bf16),
            pltpu.VMEM(square, bf16),
            pltpu.VMEM(square, bf16),
            pltpu.VMEM((LOCAL, BD), f32),
        ],
        cost_estimate=pl.CostEstimate(
            flops=11000000000, bytes_accessed=6000000, transcendentals=0
        ),
    )(segment, sizes, mine, theirs, first, second, esp_map, repulsion)


def esp_weights(first_ids, second_ids, centers, labels):
    middle = 0.5 * (centers[:, first_ids] + centers[:, second_ids])
    nearby = centers[:, labels]
    distance = jnp.zeros((first_ids.shape[0], labels.shape[0]), f32)
    for axis_pos in range(3):
        axis_gap = middle[axis_pos][:, None] - nearby[axis_pos][None, :]
        distance = distance + axis_gap * axis_gap
    weights = 1.0 / jnp.sqrt(distance + 1.0)
    excluded = (labels[None, :] == first_ids[:, None]) | (labels[None, :] == second_ids[:, None])
    return jnp.where(excluded, 0.0, weights)


def after(values, anchor):
    return lax.optimization_barrier((values, anchor))[0]


def on_device(
    monomer_density, monomer_centers, dimer_pairs, basis_sizes, dimer_core, esp_map, repulsion
):
    chip = lax.axis_index(GRP)
    segment = lax.axis_index("segment")

    own = lax.dynamic_slice_in_dim(monomer_density, segment * HALF, HALF, 1)
    gathered = jnp.concatenate([own] + shifts(phase_shift, own, 0), axis=0)
    blocks = [gathered] + shifts(phase_shift, gathered, 1)

    pair_ids, centers = after((dimer_pairs, monomer_centers), gathered)
    strides = [jnp.where(segment == 0, STRIDES[0][p], STRIDES[1][p]) for p in range(3)]
    places = [(chip // strides[p]) % 4 for p in range(3)]

    def moved(chips, phase, step):
        return chips + ((places[phase] + step + 4) % 4 - places[phase]) * strides[phase]

    steps = jnp.arange(4, dtype=jnp.int32)
    targets = moved(chip, 2, steps)
    rows = (jnp.arange(16, dtype=jnp.int32) + 8 * segment) % 16
    dimers = (targets[:, None] * 16 + rows[None, :]).reshape(64)
    sources = moved(moved(chip, 0, -steps)[None, :], 1, -steps[:, None])
    labels = (sources[:, :, None] * 8 + jnp.arange(8, dtype=jnp.int32)).reshape(128)
    pairs = pair_ids[:, dimers]
    weights = esp_weights(pairs[0], pairs[1], centers, labels).astype(bf16)
    parts = partial_fields(weights, blocks)

    segment_array = segment.reshape(1).astype(jnp.int32)
    core_rows, sizes_all, esp, rep = after((dimer_core, basis_sizes, esp_map, repulsion), parts[0])
    first, second = unflatten(segment_array, core_rows)
    sizes = sizes_all[pairs.reshape(2, 4, 16)[:, 0, 0:8]]
    square_repulsion = rep.reshape(BD, BD)

    r0 = parts[0]
    r1, r2, r3 = shifts(lambda step: phase_shift(parts[step], 2, step))
    r1, r2, r3, first, second, sizes, esp, square_repulsion = lax.optimization_barrier(
        (r1, r2, r3, first, second, sizes, esp, square_repulsion)
    )
    own_sum, other_sum = [(r0[h] + r1[h]) + (r2[h] + r3[h]) for h in (slice(0, 8), slice(8, 16))]
    theirs = swap_cores(other_sum)
    stack, energy = solve(
        segment_array, sizes, own_sum, theirs, first, second, esp, square_repulsion
    )

    for axis in GRP:
        one, two, three = shifts(axis_shift, energy, axis)
        energy = (energy + two) + (one + three)
    energy = energy + swap_cores(energy)
    window_energy = energy[0, 0] / 1024.0

    sent = flatten(jnp.stack([1 - segment, 0 * segment]).astype(jnp.int32), stack, LOCAL)
    arrived = swap_cores(sent)
    kept = flatten(jnp.stack([segment, segment]).astype(jnp.int32), stack, 2 * LOCAL)
    combined = lax.dynamic_update_slice_in_dim(kept, arrived, (1 - segment) * LOCAL, 0)
    return (combined[None], window_energy)


def solution(mesh):
    split = Mesh(
        mesh.devices.reshape(mesh.shape["segment"], 4, 4, 4), ("segment", "grp_0", "grp_1", "grp_2")
    )
    return jax.shard_map(
        on_device,
        mesh=split,
        in_specs=(P(GRP, None), P(), P(), P(), P(GRP, None), P(), P()),
        out_specs=(P("segment", GRP, None), P()),
        check_vma=False,
    )
```

profile of v0, /device:TPU:0, one launch (start us, length us, event | category | flops | bytes accessed | tf_op | source)
XLA Modules:
  0.0 98.7 jit_solution(7216187018719687699)
XLA Ops:
  1.6 3.1 %collective-permute-start.2 = (bf16[8,4608]{1,0:T(8,128)(2,1)S(1)}, bf16[8,4608]{1,0:T(8,128)(2,1)S(1)}, u32[]{:S(2)}, u32[]{:S(2)}) collective-permute-start(bf16[8,4608]{1,0:T(8,128)(2,1)S(1)} %constant_dynamic-slice_fusion), channel_id=1, source_target_pairs={{0,3},{1,0},{2,1},{3,2},{4,7},{5,4},{6,5},{7,6},{8,11},{9,8},{10,9... | collective-permute-start | bytes 221192 | tf_op jit(solution)/shard_map/ppermute | solution.py:39
  6.9 3.7 %collective-permute-done.1 = bf16[8,4608]{1,0:T(8,128)(2,1)S(1)} collective-permute-done((bf16[8,4608]{1,0:T(8,128)(2,1)S(1)}, bf16[8,4608]{1,0:T(8,128)(2,1)S(1)}, u32[]{:S(2)}, u32[]{:S(2)}) %collective-permute-start.1) | collective-permute-done | bytes 73760 | tf_op jit(solution)/shard_map/ppermute | solution.py:39
  11.4 4.1 %collective-permute-start.5 = (bf16[32,4608]{1,0:T(8,128)(2,1)S(1)}, bf16[32,4608]{1,0:T(8,128)(2,1)S(1)}, u32[]{:S(2)}, u32[]{:S(2)}) collective-permute-start(bf16[32,4608]{1,0:T(8,128)(2,1)S(1)} %pad_maximum_fusion.b0), channel_id=1, source_target_pairs={{0,12},{1,13},{2,14},{3,15},{4,0},{5,1},{6,2},{7,3},{8,4},{9,5},{1... | collective-permute-start | bytes 884744 | tf_op jit(solution)/shard_map/ppermute | solution.py:39
  15.5 1.3 %collective-permute-start.3 = (bf16[32,4608]{1,0:T(8,128)(2,1)S(1)}, bf16[32,4608]{1,0:T(8,128)(2,1)S(1)}, u32[]{:S(2)}, u32[]{:S(2)}) collective-permute-start(bf16[32,4608]{1,0:T(8,128)(2,1)S(1)} %pad_maximum_fusion.b0), channel_id=1, source_target_pairs={{0,4},{1,5},{2,6},{3,7},{4,8},{5,9},{6,10},{7,11},{8,12},{9,13},{1... | collective-permute-start | bytes 884744 | tf_op jit(solution)/shard_map/ppermute | solution.py:39
  23.8 2.8 %collective-permute-done.3.b1 = bf16[32,4608]{1,0:T(8,128)(2,1)S(1)} collective-permute-done((bf16[32,4608]{1,0:T(8,128)(2,1)S(1)}, bf16[32,4608]{1,0:T(8,128)(2,1)S(1)}, u32[]{:S(2)}, u32[]{:S(2)}) %collective-permute-start.3) | collective-permute-done | bytes 294944 | tf_op jit(solution)/shard_map/ppermute | solution.py:39
  26.6 1.3 %partial_fields.1 = (f32[16,4608]{1,0:T(8,128)}, f32[16,4608]{1,0:T(8,128)}, f32[16,4608]{1,0:T(8,128)}, f32[16,4608]{1,0:T(8,128)}) custom-call(bf16[64,128]{1,0:T(8,128)(2,1)S(1)} %select_convert_fusion.weight_ref, bf16[32,4608]{1,0:T(8,128)(2,1)S(1)} %pad_maximum_fusion.b0, bf16[32,4608]{1,0:T(8,128)(2,1)S(1)} %collective-permute-done.3.b1, ...), custom_call_target="tpu_custom_call" | custom-call | flops 80000000 | bytes 2400000 | tf_op jit(solution)/shard_map/partial_fields/pallas_call | solution.py:154
  27.9 1.5 %collective-permute-start.6 = (f32[16,4608]{1,0:T(8,128)}, f32[16,4608]{1,0:T(8,128)S(1)}, u32[]{:S(2)}, u32[]{:S(2)}) collective-permute-start(f32[16,4608]{1,0:T(8,128)} %get-tuple-element.26), channel_id=1, source_target_pairs={{0,16},{1,17},{2,18},{3,19},{4,20},{5,21},{6,22},{7,23},{8,24},{9,... | collective-permute-start | bytes 884744 | tf_op jit(solution)/shard_map/ppermute | solution.py:39
  29.4 2.7 %collective-permute-start.7 = (f32[16,4608]{1,0:T(8,128)}, f32[16,4608]{1,0:T(8,128)S(1)}, u32[]{:S(2)}, u32[]{:S(2)}) collective-permute-start(f32[16,4608]{1,0:T(8,128)} %get-tuple-element.27), channel_id=1, source_target_pairs={{0,32},{1,33},{2,34},{3,35},{4,36},{5,37},{6,38},{7,39},{8,40},{9,... | collective-permute-start | bytes 884744 | tf_op jit(solution)/shard_map/ppermute | solution.py:39
  32.1 1.4 %collective-permute-start.8 = (f32[16,4608]{1,0:T(8,128)}, f32[16,4608]{1,0:T(8,128)S(1)}, u32[]{:S(2)}, u32[]{:S(2)}) collective-permute-start(f32[16,4608]{1,0:T(8,128)} %get-tuple-element.28), channel_id=1, source_target_pairs={{0,48},{1,49},{2,50},{3,51},{4,52},{5,53},{6,54},{7,55},{8,56},{9,... | collective-permute-start | bytes 884744 | tf_op jit(solution)/shard_map/ppermute | solution.py:39
  35.8 2.7 %unflatten.1 = (f32[1536,128]{1,0:T(8,128)}, f32[1536,128]{1,0:T(8,128)}) custom-call(s32[1]{0:T(128)} %bitcast.segment_ref, f32[16,36864]{1,0:T(8,128)} %core_ref), custom_call_target="tpu_custom_call" | custom-call | flops 20000000 | bytes 3000000 | tf_op jit(solution)/shard_map/unflatten/pallas_call | solution.py:93
  38.5 1.7 %collective-permute-done.7 = f32[16,4608]{1,0:T(8,128)S(1)} collective-permute-done((f32[16,4608]{1,0:T(8,128)}, f32[16,4608]{1,0:T(8,128)S(1)}, u32[]{:S(2)}, u32[]{:S(2)}) %collective-permute-start.7) | collective-permute-done | bytes 294944 | tf_op jit(solution)/shard_map/ppermute | solution.py:39
  42.9 22.7 %solve.1 = (f32[2,8,192,192]{3,2,1,0:T(8,128)}, f32[8,128]{1,0:T(8,128)}) custom-call(s32[1]{0:T(128)} %bitcast.segment_ref, s32[2,8]{1,0:T(2,128)} %reshape.328.sizes_ref, f32[8,4608]{1,0:T(8,128)} %get-tuple-element.55.mine_any, f32[8,4608]{1,0:T(8,128)} %copy-done.5, f32[1536,128]{1,0:T(8,128)} %get-tuple-element.40.first_any, ...), custom_call_target="tpu_custom_call" | custom-call | flops 11000000512 | bytes 6000000 | tf_op jit(solution)/shard_map/solve/pallas_call | solution.py:302
  65.6 3.5 %flatten.3 = f32[8,36864]{1,0:T(8,128)} custom-call(s32[2]{0:T(128)} %pad_add_fusion.1.place_ref, f32[2,8,192,192]{3,2,1,0:T(8,128)} %get-tuple-element.44.square_ref), custom_call_target="tpu_custom_call" | custom-call | flops 20000000 | bytes 3000000 | tf_op jit(solution)/shard_map/flatten/pallas_call | solution.py:125
  69.3 2.5 %collective-permute-start.13 = (f32[8,128]{1,0:T(8,128)S(1)}, f32[8,128]{1,0:T(8,128)S(1)}, u32[]{:S(2)}, u32[]{:S(2)}) collective-permute-start(f32[8,128]{1,0:T(8,128)S(1)} %copy-done.4), channel_id=1, source_target_pairs={{0,48},{16,0},{32,16},{48,32},{1,49},{17,1},{33,17},{49,33},{2,50}... | collective-permute-start | bytes 12296 | tf_op jit(solution)/shard_map/ppermute | solution.py:50
  71.8 2.4 %collective-permute-start.11 = (f32[8,128]{1,0:T(8,128)S(1)}, f32[8,128]{1,0:T(8,128)S(1)}, u32[]{:S(2)}, u32[]{:S(2)}) collective-permute-start(f32[8,128]{1,0:T(8,128)S(1)} %copy-done.4), channel_id=1, source_target_pairs={{0,32},{16,48},{32,0},{48,16},{1,33},{17,49},{33,1},{49,17},{2,34}... | collective-permute-start | bytes 12296 | tf_op jit(solution)/shard_map/ppermute | solution.py:50
  74.2 2.4 %collective-permute-done.12 = f32[8,128]{1,0:T(8,128)S(1)} collective-permute-done((f32[8,128]{1,0:T(8,128)S(1)}, f32[8,128]{1,0:T(8,128)S(1)}, u32[]{:S(2)}, u32[]{:S(2)}) %collective-permute-start.12) | collective-permute-done | bytes 4128 | tf_op jit(solution)/shard_map/ppermute | solution.py:50
  79.4 1.2 %collective-permute-done.16 = f32[8,128]{1,0:T(8,128)S(1)} collective-permute-done((f32[8,128]{1,0:T(8,128)S(1)}, f32[8,128]{1,0:T(8,128)S(1)}, u32[]{:S(2)}, u32[]{:S(2)}) %collective-permute-start.16) | collective-permute-done | bytes 4128 | tf_op jit(solution)/shard_map/ppermute | solution.py:50
  80.5 2.1 %collective-permute-done.15 = f32[8,128]{1,0:T(8,128)S(1)} collective-permute-done((f32[8,128]{1,0:T(8,128)S(1)}, f32[8,128]{1,0:T(8,128)S(1)}, u32[]{:S(2)}, u32[]{:S(2)}) %collective-permute-start.15) | collective-permute-done | bytes 4128 | tf_op jit(solution)/shard_map/ppermute | solution.py:50
  82.6 1.4 %collective-permute-done.14 = f32[8,128]{1,0:T(8,128)S(1)} collective-permute-done((f32[8,128]{1,0:T(8,128)S(1)}, f32[8,128]{1,0:T(8,128)S(1)}, u32[]{:S(2)}, u32[]{:S(2)}) %collective-permute-start.14) | collective-permute-done | bytes 4128 | tf_op jit(solution)/shard_map/ppermute | solution.py:50
  84.6 1.5 %collective-permute-start.18 = (f32[8,128]{1,0:T(8,128)S(1)}, f32[8,128]{1,0:T(8,128)S(1)}, u32[]{:S(2)}, u32[]{:S(2)}) collective-permute-start(f32[8,128]{1,0:T(8,128)S(1)} %add_add_fusion.3), channel_id=1, source_target_pairs={{0,1},{1,2},{2,3},{3,0},{4,5},{5,6},{6,7},{7,4},{8,9},{9,10},{10,1... | collective-permute-start | bytes 12296 | tf_op jit(solution)/shard_map/ppermute | solution.py:50
  86.1 1.2 %collective-permute-start.17 = (f32[8,128]{1,0:T(8,128)S(1)}, f32[8,128]{1,0:T(8,128)S(1)}, u32[]{:S(2)}, u32[]{:S(2)}) collective-permute-start(f32[8,128]{1,0:T(8,128)S(1)} %add_add_fusion.3), channel_id=1, source_target_pairs={{0,2},{1,3},{2,0},{3,1},{4,6},{5,7},{6,4},{7,5},{8,10},{9,11},{10,... | collective-permute-start | bytes 12296 | tf_op jit(solution)/shard_map/ppermute | solution.py:50
  87.7 1.8 %collective-permute-done.18 = f32[8,128]{1,0:T(8,128)S(1)} collective-permute-done((f32[8,128]{1,0:T(8,128)S(1)}, f32[8,128]{1,0:T(8,128)S(1)}, u32[]{:S(2)}, u32[]{:S(2)}) %collective-permute-start.18) | collective-permute-done | bytes 4128 | tf_op jit(solution)/shard_map/ppermute | solution.py:50
  89.5 1.7 %collective-permute-done.17 = f32[8,128]{1,0:T(8,128)S(1)} collective-permute-done((f32[8,128]{1,0:T(8,128)S(1)}, f32[8,128]{1,0:T(8,128)S(1)}, u32[]{:S(2)}, u32[]{:S(2)}) %collective-permute-start.17) | collective-permute-done | bytes 4128 | tf_op jit(solution)/shard_map/ppermute | solution.py:50
  91.9 3.5 %flatten.2 = f32[16,36864]{1,0:T(8,128)} custom-call(s32[2]{0:T(128)} %pad_add_fusion.place_ref, f32[2,8,192,192]{3,2,1,0:T(8,128)} %get-tuple-element.44.square_ref), custom_call_target="tpu_custom_call" | custom-call | flops 20000000 | bytes 3000000 | tf_op jit(solution)/shard_map/flatten/pallas_call | solution.py:125
  (81 shorter events, 21.8 us)
Async XLA Ops:
  0.6 34.3 %copy-start.3 = (f32[36864]{0:T(1024)S(1)}, f32[36864]{0:T(1024)}, u32[]{:S(2)}) copy-start(f32[36864]{0:T(1024)} %param.13) | copy-start | bytes 442372
  0.7 33.0 %copy-start.1 = (s32[512]{0:T(512)S(1)}, s32[512]{0:T(512)}, u32[]{:S(2)}) copy-start(s32[512]{0:T(512)} %param.10) | copy-start | bytes 6148
  1.6 5.3 %collective-permute-start.2 = (bf16[8,4608]{1,0:T(8,128)(2,1)S(1)}, bf16[8,4608]{1,0:T(8,128)(2,1)S(1)}, u32[]{:S(2)}, u32[]{:S(2)}) collective-permute-start(bf16[8,4608]{1,0:T(8,128)(2,1)S(1)} %constant_dynamic-slice_fusion), channel_id=1, source_target_pairs={{0,3},{1,0},{2,1},{3,2},{4,7},{5,4},{6,5},{7,6},{8,11},{9,8},{10,9... | collective-permute-start | bytes 221192 | tf_op jit(solution)/shard_map/ppermute | solution.py:39
  4.7 5.9 %collective-permute-start.1 = (bf16[8,4608]{1,0:T(8,128)(2,1)S(1)}, bf16[8,4608]{1,0:T(8,128)(2,1)S(1)}, u32[]{:S(2)}, u32[]{:S(2)}) collective-permute-start(bf16[8,4608]{1,0:T(8,128)(2,1)S(1)} %constant_dynamic-slice_fusion), channel_id=1, source_target_pairs={{0,2},{1,3},{2,0},{3,1},{4,6},{5,7},{6,4},{7,5},{8,10},{9,11},{10,... | collective-permute-start | bytes 221192 | tf_op jit(solution)/shard_map/ppermute | solution.py:39
  5.3 6.0 %collective-permute-start = (bf16[8,4608]{1,0:T(8,128)(2,1)S(1)}, bf16[8,4608]{1,0:T(8,128)(2,1)S(1)}, u32[]{:S(2)}, u32[]{:S(2)}) collective-permute-start(bf16[8,4608]{1,0:T(8,128)(2,1)S(1)} %constant_dynamic-slice_fusion), channel_id=1, source_target_pairs={{0,1},{1,2},{2,3},{3,0},{4,5},{5,6},{6,7},{7,4},{8,9},{9,10},{10,1... | collective-permute-start | bytes 221192 | tf_op jit(solution)/shard_map/ppermute | solution.py:39
  11.4 11.5 %collective-permute-start.5 = (bf16[32,4608]{1,0:T(8,128)(2,1)S(1)}, bf16[32,4608]{1,0:T(8,128)(2,1)S(1)}, u32[]{:S(2)}, u32[]{:S(2)}) collective-permute-start(bf16[32,4608]{1,0:T(8,128)(2,1)S(1)} %pad_maximum_fusion.b0), channel_id=1, source_target_pairs={{0,12},{1,13},{2,14},{3,15},{4,0},{5,1},{6,2},{7,3},{8,4},{9,5},{1... | collective-permute-start | bytes 884744 | tf_op jit(solution)/shard_map/ppermute | solution.py:39
  15.5 8.3 %collective-permute-start.4 = (bf16[32,4608]{1,0:T(8,128)(2,1)S(1)}, bf16[32,4608]{1,0:T(8,128)(2,1)S(1)}, u32[]{:S(2)}, u32[]{:S(2)}) collective-permute-start(bf16[32,4608]{1,0:T(8,128)(2,1)S(1)} %pad_maximum_fusion.b0), channel_id=1, source_target_pairs={{0,8},{1,9},{2,10},{3,11},{4,12},{5,13},{6,14},{7,15},{8,0},{9,1},... | collective-permute-start | bytes 884744 | tf_op jit(solution)/shard_map/ppermute | solution.py:39
  15.5 11.1 %collective-permute-start.3 = (bf16[32,4608]{1,0:T(8,128)(2,1)S(1)}, bf16[32,4608]{1,0:T(8,128)(2,1)S(1)}, u32[]{:S(2)}, u32[]{:S(2)}) collective-permute-start(bf16[32,4608]{1,0:T(8,128)(2,1)S(1)} %pad_maximum_fusion.b0), channel_id=1, source_target_pairs={{0,4},{1,5},{2,6},{3,7},{4,8},{5,9},{6,10},{7,11},{8,12},{9,13},{1... | collective-permute-start | bytes 884744 | tf_op jit(solution)/shard_map/ppermute | solution.py:39
  27.9 12.3 %copy-start.2 = (f32[16,4608]{1,0:T(8,128)S(1)}, f32[16,4608]{1,0:T(8,128)}, u32[]{:S(2)}) copy-start(f32[16,4608]{1,0:T(8,128)} %get-tuple-element.29) | copy-start | bytes 884740
  27.9 10.6 %collective-permute-start.6 = (f32[16,4608]{1,0:T(8,128)}, f32[16,4608]{1,0:T(8,128)S(1)}, u32[]{:S(2)}, u32[]{:S(2)}) collective-permute-start(f32[16,4608]{1,0:T(8,128)} %get-tuple-element.26), channel_id=1, source_target_pairs={{0,16},{1,17},{2,18},{3,19},{4,20},{5,21},{6,22},{7,23},{8,24},{9,... | collective-permute-start | bytes 884744 | tf_op jit(solution)/shard_map/ppermute | solution.py:39
  29.4 10.8 %collective-permute-start.7 = (f32[16,4608]{1,0:T(8,128)}, f32[16,4608]{1,0:T(8,128)S(1)}, u32[]{:S(2)}, u32[]{:S(2)}) collective-permute-start(f32[16,4608]{1,0:T(8,128)} %get-tuple-element.27), channel_id=1, source_target_pairs={{0,32},{1,33},{2,34},{3,35},{4,36},{5,37},{6,38},{7,39},{8,40},{9,... | collective-permute-start | bytes 884744 | tf_op jit(solution)/shard_map/ppermute | solution.py:39
  32.1 8.1 %collective-permute-start.8 = (f32[16,4608]{1,0:T(8,128)}, f32[16,4608]{1,0:T(8,128)S(1)}, u32[]{:S(2)}, u32[]{:S(2)}) collective-permute-start(f32[16,4608]{1,0:T(8,128)} %get-tuple-element.28), channel_id=1, source_target_pairs={{0,48},{1,49},{2,50},{3,51},{4,52},{5,53},{6,54},{7,55},{8,56},{9,... | collective-permute-start | bytes 884744 | tf_op jit(solution)/shard_map/ppermute | solution.py:39
  40.9 1.4 %collective-permute-start.9 = (f32[8,4608]{1,0:T(8,128)S(1)}, f32[8,4608]{1,0:T(8,128)S(1)}, u32[]{:S(2)}, u32[]{:S(2)}) collective-permute-start(f32[8,4608]{1,0:T(8,128)S(1)} %get-tuple-element.54), channel_id=1, source_target_pairs={{0,64},{64,0},{1,65},{65,1},{2,66},{66,2},{3,67},{67,3},{4,68},{68... | collective-permute-start | bytes 442376 | tf_op jit(solution)/shard_map/ppermute | solution.py:54
  69.1 27.4 %collective-permute-start.10 = (f32[8,36864]{1,0:T(8,128)}, f32[8,36864]{1,0:T(8,128)S(1)}, u32[]{:S(2)}, u32[]{:S(2)}) collective-permute-start(f32[8,36864]{1,0:T(8,128)} %flatten.3), channel_id=1, source_target_pairs={{0,64},{64,0},{1,65},{65,1},{2,66},{66,2},{3,67},{67,3},{4,68},{68... | collective-permute-start | bytes 3538952 | tf_op jit(solution)/shard_map/ppermute | solution.py:54
  69.3 5.0 %collective-permute-start.13 = (f32[8,128]{1,0:T(8,128)S(1)}, f32[8,128]{1,0:T(8,128)S(1)}, u32[]{:S(2)}, u32[]{:S(2)}) collective-permute-start(f32[8,128]{1,0:T(8,128)S(1)} %copy-done.4), channel_id=1, source_target_pairs={{0,48},{16,0},{32,16},{48,32},{1,49},{17,1},{33,17},{49,33},{2,50}... | collective-permute-start | bytes 12296 | tf_op jit(solution)/shard_map/ppermute | solution.py:50
  71.8 4.8 %collective-permute-start.12 = (f32[8,128]{1,0:T(8,128)S(1)}, f32[8,128]{1,0:T(8,128)S(1)}, u32[]{:S(2)}, u32[]{:S(2)}) collective-permute-start(f32[8,128]{1,0:T(8,128)S(1)} %copy-done.4), channel_id=1, source_target_pairs={{0,16},{16,32},{32,48},{48,0},{1,17},{17,33},{33,49},{49,1},{2,18}... | collective-permute-start | bytes 12296 | tf_op jit(solution)/shard_map/ppermute | solution.py:50
  71.8 5.1 %collective-permute-start.11 = (f32[8,128]{1,0:T(8,128)S(1)}, f32[8,128]{1,0:T(8,128)S(1)}, u32[]{:S(2)}, u32[]{:S(2)}) collective-permute-start(f32[8,128]{1,0:T(8,128)S(1)} %copy-done.4), channel_id=1, source_target_pairs={{0,32},{16,48},{32,0},{48,16},{1,33},{17,49},{33,1},{49,17},{2,34}... | collective-permute-start | bytes 12296 | tf_op jit(solution)/shard_map/ppermute | solution.py:50
  76.9 3.6 %collective-permute-start.16 = (f32[8,128]{1,0:T(8,128)S(1)}, f32[8,128]{1,0:T(8,128)S(1)}, u32[]{:S(2)}, u32[]{:S(2)}) collective-permute-start(f32[8,128]{1,0:T(8,128)S(1)} %add_add_fusion.4), channel_id=1, source_target_pairs={{0,12},{4,0},{8,4},{12,8},{1,13},{5,1},{9,5},{13,9},{2,14},{6,2},{... | collective-permute-start | bytes 12296 | tf_op jit(solution)/shard_map/ppermute | solution.py:50
  77.8 4.8 %collective-permute-start.15 = (f32[8,128]{1,0:T(8,128)S(1)}, f32[8,128]{1,0:T(8,128)S(1)}, u32[]{:S(2)}, u32[]{:S(2)}) collective-permute-start(f32[8,128]{1,0:T(8,128)S(1)} %add_add_fusion.4), channel_id=1, source_target_pairs={{0,4},{4,8},{8,12},{12,0},{1,5},{5,9},{9,13},{13,1},{2,6},{6,10},{... | collective-permute-start | bytes 12296 | tf_op jit(solution)/shard_map/ppermute | solution.py:50
  79.0 5.1 %collective-permute-start.14 = (f32[8,128]{1,0:T(8,128)S(1)}, f32[8,128]{1,0:T(8,128)S(1)}, u32[]{:S(2)}, u32[]{:S(2)}) collective-permute-start(f32[8,128]{1,0:T(8,128)S(1)} %add_add_fusion.4), channel_id=1, source_target_pairs={{0,8},{4,12},{8,0},{12,4},{1,9},{5,13},{9,1},{13,5},{2,10},{6,14},... | collective-permute-start | bytes 12296 | tf_op jit(solution)/shard_map/ppermute | solution.py:50
  84.1 3.6 %collective-permute-start.19 = (f32[8,128]{1,0:T(8,128)S(1)}, f32[8,128]{1,0:T(8,128)S(1)}, u32[]{:S(2)}, u32[]{:S(2)}) collective-permute-start(f32[8,128]{1,0:T(8,128)S(1)} %add_add_fusion.3), channel_id=1, source_target_pairs={{0,3},{1,0},{2,1},{3,2},{4,7},{5,4},{6,5},{7,6},{8,11},{9,8},{10,9... | collective-permute-start | bytes 12296 | tf_op jit(solution)/shard_map/ppermute | solution.py:50
  84.6 4.8 %collective-permute-start.18 = (f32[8,128]{1,0:T(8,128)S(1)}, f32[8,128]{1,0:T(8,128)S(1)}, u32[]{:S(2)}, u32[]{:S(2)}) collective-permute-start(f32[8,128]{1,0:T(8,128)S(1)} %add_add_fusion.3), channel_id=1, source_target_pairs={{0,1},{1,2},{2,3},{3,0},{4,5},{5,6},{6,7},{7,4},{8,9},{9,10},{10,1... | collective-permute-start | bytes 12296 | tf_op jit(solution)/shard_map/ppermute | solution.py:50
  86.1 5.1 %collective-permute-start.17 = (f32[8,128]{1,0:T(8,128)S(1)}, f32[8,128]{1,0:T(8,128)S(1)}, u32[]{:S(2)}, u32[]{:S(2)}) collective-permute-start(f32[8,128]{1,0:T(8,128)S(1)} %add_add_fusion.3), channel_id=1, source_target_pairs={{0,2},{1,3},{2,0},{3,1},{4,6},{5,7},{6,4},{7,5},{8,10},{9,11},{10,... | collective-permute-start | bytes 12296 | tf_op jit(solution)/shard_map/ppermute | solution.py:50
  91.2 4.1 %collective-permute-start.20 = (f32[8,128]{1,0:T(8,128)S(1)}, f32[8,128]{1,0:T(8,128)S(1)}, u32[]{:S(2)}, u32[]{:S(2)}) collective-permute-start(f32[8,128]{1,0:T(8,128)S(1)} %add_add_fusion.2), channel_id=1, source_target_pairs={{0,64},{64,0},{1,65},{65,1},{2,66},{66,2},{3,67},{67,3},{4,68},{68... | collective-permute-start | bytes 12296 | tf_op jit(solution)/shard_map/ppermute | solution.py:54
  (3 other events, 5.2 us)
where the time goes:
time: 101 us; the launch traced here: 98.7 us
  Pallas kernels  33.7 us (33%)
  starting transfers between devices  26.6 us (26%)
  waiting for transfers between devices  22.9 us (23%)
  local copies, waits for them, and re-layouts  10.5 us (10%)
  between operations  2.62 us (3%)
  other arithmetic  2.49 us (2%)
    pallas_call x1, Pallas kernels, solve(): pl.pallas_call(solve_kernel, name='solve', in_specs=[smem, smem] + [pl.Bl...  22.7 us
    ppermute x9, starting transfers between devices, phase_shift(): return lax.ppermute(value, ALL, pairs)  15.8 us
    ppermute x9, waiting for transfers between devices, axis_shift(): return lax.ppermute(value, axis, [(i, (i + step) % 4) for i in range(4)])  11.2 us
    ppermute x9, waiting for transfers between devices, phase_shift(): return lax.ppermute(value, ALL, pairs)  10.9 us
    ppermute x9, starting transfers between devices, axis_shift(): return lax.ppermute(value, axis, [(i, (i + step) % 4) for i in range(4)])  10.7 us
    pallas_call x2, Pallas kernels, flatten(): pl.pallas_call(flatten_kernel, name='flatten', grid_spec=pltpu.PrefetchSc...  6.95 us
    pallas_call x1, Pallas kernels, unflatten(): pl.pallas_call(unflatten_kernel, name='unflatten', grid_spec=pltpu.Prefet...  2.72 us
  transfers between devices with their start and end apart: 21, of which 15 were waited for; matrix products, arithmetic and copies ran while one was open for 10% of the time, Pallas kernels for 6%

commit v1 on v0

--- a/solution.py
+++ b/solution.py
@@ -8,8 +8,8 @@
 
 
 PURIFY = 8
+MIB = 1024 * 1024
 SINGLE = (8, 4)
-MIB = 1024 * 1024
 GRP = ("grp_0", "grp_1", "grp_2")
 ALL = ("segment", "grp_0", "grp_1", "grp_2")
 STRIDES = ((1, 4, 16), (4, 16, 1))
@@ -23,7 +23,6 @@
 PITCH = 292
 FPITCH = 73
 epsilon = 1e-06
-highest = lax.Precision.HIGHEST
 f32 = jnp.float32
 bf16 = jnp.bfloat16
 
@@ -73,7 +72,12 @@
     return lax.broadcasted_iota(jnp.int32, (rows, 128), 1)
 
 
-def unflatten_kernel(segment_ref, core_ref, first_ref, second_ref, flat):
+def unflatten_kernel(segment_ref, core_ref, esp_ref, first_ref, second_ref, left_ref, flat):
+    half = BM // 2
+    own = pl.multiple_of(half * segment_ref[0], 8)
+    other = pl.multiple_of(half - own, 8)
+    left_ref[0:half, :] = esp_ref[pl.ds(own, half), :]
+    left_ref[half:BM, :] = esp_ref[pl.ds(other, half), :]
     for tile in range(TILES):
         flat[pl.ds(tile, LOCAL, stride=PITCH), :] = core_ref[:, tile * 128 : tile * 128 + 128]
     low_half = lane_index(BM) < 64
@@ -89,20 +93,25 @@
         second_ref[pl.ds(d * BD + 1, BM, stride=2), :] = c_rolled
 
 
-def unflatten(segment, core):
+def unflatten(segment, core, esp_map):
     return pl.pallas_call(
         unflatten_kernel,
         name="unflatten",
         grid_spec=pltpu.PrefetchScalarGridSpec(
             num_scalar_prefetch=1,
             grid=(1,),
-            in_specs=[pl.BlockSpec((LOCAL, FLAT), lambda i, s: (s[0], 0))],
-            out_specs=[pl.BlockSpec((LOCAL * BD, 128), lambda i, s: (0, 0))] * 2,
+            in_specs=[
+                pl.BlockSpec((LOCAL, FLAT), lambda i, s: (s[0], 0)),
+                pl.BlockSpec((BM, BD), lambda i, s: (0, 0)),
+            ],
+            out_specs=[pl.BlockSpec((LOCAL * BD, 128), lambda i, s: (0, 0))] * 2
+            + [pl.BlockSpec((BM, BD), lambda i, s: (0, 0))],
             scratch_shapes=[pltpu.VMEM((LOCAL * PITCH, 128), f32)],
         ),
-        out_shape=[jax.ShapeDtypeStruct((LOCAL * BD, 128), f32)] * 2,
+        out_shape=[jax.ShapeDtypeStruct((LOCAL * BD, 128), f32)] * 2
+        + [jax.ShapeDtypeStruct((BM, BD), f32)],
         cost_estimate=pl.CostEstimate(flops=20000000, bytes_accessed=3000000, transcendentals=0),
-    )(segment, core)
+    )(segment, core, esp_map)
 
 
 def flatten_kernel(place_ref, square_ref, out_ref, first, second, flat):
@@ -136,7 +145,7 @@
                 pltpu.VMEM((LOCAL * PITCH, 128), f32),
             ],
         ),
-        out_shape=jax.ShapeDtypeStruct((rows, FLAT), f32),
+        out_shape=pltpu.HBM((rows, FLAT), f32),
         cost_estimate=pl.CostEstimate(flops=20000000, bytes_accessed=3000000, transcendentals=0),
     )(place, stack)
 
@@ -160,27 +169,17 @@
     )(weights, *blocks)
 
 
-def live_square(n_first, n_second):
-    row = lax.broadcasted_iota(jnp.int32, (BD, BD), 0)
-    column = lax.broadcasted_iota(jnp.int32, (BD, BD), 1)
-
-    def inside(position):
-        limit = jnp.where(position < BM, n_first, n_second + BM)
-        return position < limit
-
-    live = jnp.logical_and(inside(row), inside(column))
-    return live, row == column
-
-
 def solve_kernel(
-    segment_ref, sizes_ref, mine_any, theirs_any, first_any, second_any, esp_any, rep_any,
+    sizes_any, mine_any, theirs_any, first_any, second_any, esp_any, left_any, rep_any,
     stack, energy_out,
-    mine_ref, theirs_ref, first_ref, second_ref, esp_ref, rep_ref, arrivals,
-    flat, field, fock, work, work_h, work_l, square_h, square_l, diagonals,
+    sizes_ref, mine_ref, theirs_ref, first_ref, second_ref, esp_ref, left_ref, rep_ref, arrivals,
+    fock, density, departures, flat, field, eye, masked, offset, work, work_h, work_l, square_h, square_l,
+    alive, diagonal, others, scale, shift, occupied, extra,
 ):
     places = (
-        (mine_any, mine_ref), (theirs_any, theirs_ref), (esp_any, esp_ref),
-        (first_any, first_ref), (second_any, second_ref), (rep_any, rep_ref),
+        (sizes_any, sizes_ref), (mine_any, mine_ref), (theirs_any, theirs_ref), (esp_any, esp_ref),
+        (left_any, left_ref), (rep_any, rep_ref),
+        (first_any, first_ref), (second_any, second_ref),
     )
     copies = [
         pltpu.make_async_copy(source, target, arrivals.at[i])
@@ -188,22 +187,27 @@
     ]
     for copy in copies:
         copy.start()
+
+    row = lax.broadcasted_iota(jnp.int32, (BM, BD), 0)
+    eye[...] = jnp.where(
+        lax.broadcasted_iota(jnp.int32, (128, 128), 0) == lax.broadcasted_iota(jnp.int32, (128, 128), 1),
+        1.0,
+        0.0,
+    )
     copies[0].wait()
-    copies[1].wait()
-    core_out = stack.at[0]
-    density_out = stack.at[1]
-    segment = segment_ref[0]
-    own_start = 36 * segment
-    other_start = 36 - own_start
+    limits = [jnp.broadcast_to(sizes_ref[:, k : k + 1], (LOCAL, BD)) for k in (0, 1)]
+    position = lax.broadcasted_iota(jnp.int32, (LOCAL, BD), 1)
+    limit = jnp.where(position < BM, limits[0], limits[1] + BM)
+    live = jnp.where(position < limit, 1.0, 0.0)
+    alive[...] = live
+    count = jnp.sum(live, axis=1, keepdims=True)
+
+    for copy in copies[1:6]:
+        copy.wait()
     for tile in range(36):
         columns = slice(tile * 128, tile * 128 + 128)
-        flat[pl.ds(own_start + tile, LOCAL, stride=FPITCH), :] = mine_ref[:, columns]
-        flat[pl.ds(other_start + tile, LOCAL, stride=FPITCH), :] = theirs_ref[:, columns]
-    for copy in copies[2:]:
-        copy.wait()
-    esp = split_two(esp_ref[...])
-    esp_t = split_two(esp_ref[...].T)
-    repulsion = 0.5 * (rep_ref[...] + rep_ref[...].T)
+        flat[pl.ds(tile, LOCAL, stride=FPITCH), :] = mine_ref[:, columns]
+        flat[pl.ds(36 + tile, LOCAL, stride=FPITCH), :] = theirs_ref[:, columns]
     lane = lane_index(24)
     for d in range(LOCAL):
         a = flat[pl.ds(d * FPITCH, 24, stride=3), :]
@@ -218,118 +222,178 @@
             lane < 64, pltpu.roll(b, 64, 1), pltpu.roll(c, 64, 1)
         )
         field[pl.ds(base + 3, 24, stride=4), :] = pltpu.roll(c, 96, 1)
-    for d in range(LOCAL):
-        left = dot_three(esp_t, split_two(field[d * BM : d * BM + BM, 0:BM]))
-        potential = dot_three(split_two(left), esp)
+
+    esp = split_two(esp_ref[...])
+    esp_t = split_two(left_ref[...].T)
+    repulsion = 0.5 * (rep_ref[...] + rep_ref[...].T)
+    half_repulsion = 0.5 * repulsion
+    right = split_two(dot_three(split_two(field[...][:, 0:BM]), esp))
+
+    def blocks(value):
+        return value[0:128, 0:128], value[128:BD, 128:BD]
+
+    def eyes():
+        return eye[...], eye[0:64, 0:64]
+
+    def diagonal_of(value):
+        first_part, second_part = (
+            jnp.sum(b * e, axis=0, keepdims=True) for b, e in zip(blocks(value), eyes())
+        )
+        return jnp.concatenate([first_part, second_part], axis=1)
+
+    def with_diagonal(value, vector):
+        (a, b), (eye_a, eye_b) = blocks(value), eyes()
+        a = a + eye_a * vector[:, 0:128]
+        b = b + eye_b * vector[:, 128:BD]
+        return jnp.concatenate(
+            [
+                jnp.concatenate([a, value[0:128, 128:BD]], axis=1),
+                jnp.concatenate([value[128:BD, 0:128], b], axis=1),
+            ],
+            axis=0,
+        )
+
+    def columns_of(value, d):
+        (a, b), (eye_a, eye_b) = blocks(value), eyes()
+        on_a, on_b = a * eye_a, b * eye_b
+        diagonal[d : d + 1, 0:128] = jnp.sum(on_a, axis=0, keepdims=True)
+        diagonal[d : d + 1, 128:BD] = jnp.sum(on_b, axis=0, keepdims=True)
+
+        def total(part):
+            return jnp.sum(jnp.abs(part), axis=0, keepdims=True)
+
+        others[d : d + 1, 0:128] = total(a - on_a) + total(value[128:BD, 0:128])
+        others[d : d + 1, 128:BD] = total(b - on_b) + total(value[0:128, 128:BD])
+
+    copies[6].wait()
+    copies[7].wait()
+    for d in range(LOCAL):
+        rows = slice(d * BM, d * BM + BM)
+        potential = dot_three(esp_t, (right[0][rows], right[1][rows]))
         rows = slice(d * BD, d * BD + BD)
         core = jnp.concatenate([first_ref[rows, :], second_ref[rows, 0:64]], axis=1)
         total = core + potential
-        core_out[d] = 0.5 * (total + total.T)
-
-    def live_count(d):
-        n_first = jnp.clip(sizes_ref[0, d], 0, BM)
-        n_second = jnp.clip(sizes_ref[1, d], 0, BM)
-        return n_first, n_second, (n_first + n_second).astype(f32)
-
-    def purify(source, singles):
+        total = 0.5 * (total + total.T)
+        fock[d] = total
+        total = total * alive[d : d + 1, :]
+        total = jnp.concatenate(
+            [
+                jnp.where(row < limits[0][d : d + 1, :], total[0:BM], 0.0),
+                jnp.where(row < limits[1][d : d + 1, :], total[BM:BD], 0.0),
+            ],
+            axis=0,
+        )
+        masked[d] = total
+        columns_of(total, d)
+
+    leaving = [pltpu.make_async_copy(fock, stack.at[0], departures.at[LOCAL])]
+    leaving[0].start()
+
+    def start(source, added):
+        on_diagonal = diagonal[...] + added
+        chemical = jnp.sum(on_diagonal, axis=1, keepdims=True) / count
+        lowered = chemical * live
+        sums = others[...] + jnp.abs(on_diagonal - lowered)
+        radius = jnp.max(sums, axis=1, keepdims=True)
+        scale[...] = jnp.broadcast_to(-0.5 / (radius + epsilon), (LOCAL, BD))
+        shift[...] = added - lowered
         for d in range(LOCAL):
-            n_first, n_second, count = live_count(d)
-            live, diagonal = live_square(n_first, n_second)
-            masked = jnp.where(live, source[d], 0.0)
-            on_diagonal = jnp.logical_and(live, diagonal)
-            chemical = jnp.sum(jnp.where(diagonal, masked, 0.0)) / count
-            shifted = masked - jnp.where(on_diagonal, chemical, 0.0)
-            radius = jnp.max(jnp.sum(jnp.abs(shifted), axis=0, keepdims=True))
-            work[d] = shifted * (-0.5 / (radius + epsilon))
-
-        def single(_, carry):
-            for d in range(LOCAL):
-                high = work[d].astype(bf16)
-                work_h[d] = high
-                square_h[d] = dot(high, high).astype(bf16)
-            for d in range(LOCAL):
-                work[d] = 1.5 * work[d] - 2.0 * dot(square_h[d], work_h[d])
-            return carry
-
-        def triple(_, carry):
-            for d in range(LOCAL):
-                high, low = split_two(work[d])
-                work_h[d] = high
-                work_l[d] = low
-                squared = dot_three((high, low), (high, low))
-                square_h[d], square_l[d] = split_two(squared)
-            for d in range(LOCAL):
-                cubed = dot_three((square_h[d], square_l[d]), (work_h[d], work_l[d]))
-                work[d] = 1.5 * work[d] - 2.0 * cubed
-            return carry
-
+            work[d] = with_diagonal(source[d], shift[d : d + 1, :]) * scale[d : d + 1, :]
+
+    def single(_, carry):
+        for d in range(LOCAL):
+            high = work[d].astype(bf16)
+            work_h[d] = high
+            square_h[d] = dot(high, high).astype(bf16)
+        for d in range(LOCAL):
+            work[d] = 1.5 * work[d] - 2.0 * dot(square_h[d], work_h[d])
+        return carry
+
+    def triple(_, carry):
+        for d in range(LOCAL):
+            high, low = split_two(work[d])
+            work_h[d] = high
+            work_l[d] = low
+            squared = dot_three((high, low), (high, low))
+            square_h[d], square_l[d] = split_two(squared)
+        for d in range(LOCAL):
+            cubed = dot_three((square_h[d], square_l[d]), (work_h[d], work_l[d]))
+            work[d] = 1.5 * work[d] - 2.0 * cubed
+        return carry
+
+    def purify(singles):
         if singles > 0:
             lax.fori_loop(0, singles, single, 0)
         if singles < PURIFY:
             lax.fori_loop(singles, PURIFY, triple, 0)
 
-    def density_of(d):
-        n_first, n_second, count = live_count(d)
-        live, diagonal = live_square(n_first, n_second)
-        return work[d] + jnp.where(jnp.logical_and(live, diagonal), 0.5, 0.0), diagonal, count
-
-    purify(core_out, SINGLE[0])
-    for d in range(LOCAL):
-        density, diagonal, _ = density_of(d)
-        diagonals[d : d + 1, :] = jnp.sum(jnp.where(diagonal, density, 0.0), axis=0, keepdims=True)
-    coulomb = jnp.dot(diagonals[...], repulsion, precision=highest, preferred_element_type=f32)
-    for d in range(LOCAL):
-        density, diagonal, _ = density_of(d)
-        fock[d] = (
-            core_out[d]
-            + jnp.where(diagonal, coulomb[d : d + 1, :], 0.0)
-            - 0.5 * (repulsion * density)
-        )
-    purify(fock, SINGLE[1])
-    energy = jnp.zeros((1, BD), f32)
-    for d in range(LOCAL):
-        density, _, count = density_of(d)
-        density_out[d] = density
-        terms = jnp.sum(density * (core_out[d] + fock[d]), axis=0, keepdims=True)
-        energy = energy + terms * (0.5 / count)
-    energy_out[...] = jnp.full((8, 128), jnp.sum(energy), f32)
-
-
-def solve(segment, sizes, mine, theirs, first, second, esp_map, repulsion):
+    start(masked, jnp.zeros((LOCAL, BD), f32))
+    purify(SINGLE[0])
+    for d in range(LOCAL):
+        occupied[d : d + 1, :] = diagonal_of(work[d])
+    coulomb = dot_three(split_two(occupied[...] + 0.5 * live), split_two(repulsion))
+    own_repulsion = diagonal_of(half_repulsion)
+    extra[...] = live * (coulomb - 0.5 * own_repulsion)
+    for d in range(LOCAL):
+        changed = masked[d] - half_repulsion * work[d]
+        offset[d] = changed
+        columns_of(changed, d)
+    start(offset, extra[...])
+    purify(SINGLE[1])
+    for d in range(LOCAL):
+        solved = with_diagonal(work[d], 0.5 * alive[d : d + 1, :])
+        density[d] = solved
+        leaving.append(pltpu.make_async_copy(density.at[d], stack.at[1, d], departures.at[d]))
+        leaving[-1].start()
+        both = with_diagonal(masked[d] + offset[d], extra[d : d + 1, :])
+        diagonal[d : d + 1, :] = jnp.sum(solved * both, axis=0, keepdims=True)
+    energy = jnp.sum(diagonal[...], axis=1, keepdims=True) * (0.5 / count)
+    energy_out[...] = jnp.broadcast_to(jnp.sum(energy, axis=0, keepdims=True), (8, 128))
+    for copy in leaving:
+        copy.wait()
+
+
+def solve(sizes, mine, theirs, first, second, esp_map, esp_left, repulsion):
     vmem = pl.BlockSpec(memory_space=pltpu.VMEM)
-    smem = pl.BlockSpec(memory_space=pltpu.SMEM)
     square = (LOCAL, BD, BD)
     return pl.pallas_call(
         solve_kernel,
         name="solve",
-        in_specs=[smem, smem] + [pl.BlockSpec(memory_space=pltpu.HBM)] * 6,
-        out_specs=[vmem] * 2,
+        in_specs=[pl.BlockSpec(memory_space=pltpu.HBM)] * 8,
+        out_specs=[pl.BlockSpec(memory_space=pltpu.HBM), vmem],
         out_shape=[
             jax.ShapeDtypeStruct((2,) + square, f32),
             jax.ShapeDtypeStruct((8, 128), f32),
         ],
         scratch_shapes=[
+            pltpu.VMEM((LOCAL, 2), jnp.int32),
             pltpu.VMEM((LOCAL, HALF), f32),
             pltpu.VMEM((LOCAL, HALF), f32),
             pltpu.VMEM((LOCAL * BD, 128), f32),
             pltpu.VMEM((LOCAL * BD, 128), f32),
             pltpu.VMEM((BM, BD), f32),
+            pltpu.VMEM((BM, BD), f32),
             pltpu.VMEM((BD, BD), f32),
-            pltpu.SemaphoreType.DMA((6,)),
+            pltpu.SemaphoreType.DMA((8,)),
+            pltpu.VMEM(square, f32),
+            pltpu.VMEM(square, f32),
+            pltpu.SemaphoreType.DMA((LOCAL + 1,)),
             pltpu.VMEM((LOCAL * FPITCH, 128), f32),
             pltpu.VMEM((LOCAL * BM, 128), f32),
+            pltpu.VMEM((128, 128), f32),
+            pltpu.VMEM(square, f32),
             pltpu.VMEM(square, f32),
             pltpu.VMEM(square, f32),
             pltpu.VMEM(square, bf16),
             pltpu.VMEM(square, bf16),
             pltpu.VMEM(square, bf16),
             pltpu.VMEM(square, bf16),
-            pltpu.VMEM((LOCAL, BD), f32),
-        ],
+        ]
+        + [pltpu.VMEM((LOCAL, BD), f32)] * 7,
         cost_estimate=pl.CostEstimate(
             flops=11000000000, bytes_accessed=6000000, transcendentals=0
         ),
-    )(segment, sizes, mine, theirs, first, second, esp_map, repulsion)
+    )(sizes, mine, theirs, first, second, esp_map, esp_left, repulsion)
 
 
 def esp_weights(first_ids, second_ids, centers, labels):
@@ -377,19 +441,19 @@
 
     segment_array = segment.reshape(1).astype(jnp.int32)
     core_rows, sizes_all, esp, rep = after((dimer_core, basis_sizes, esp_map, repulsion), parts[0])
-    first, second = unflatten(segment_array, core_rows)
-    sizes = sizes_all[pairs.reshape(2, 4, 16)[:, 0, 0:8]]
+    first, second, left = unflatten(segment_array, core_rows, esp)
+    sizes = jnp.clip(sizes_all[pairs.reshape(2, 4, 16)[:, 0, 0:8]], 0, BM).T
     square_repulsion = rep.reshape(BD, BD)
 
     r0 = parts[0]
     r1, r2, r3 = shifts(lambda step: phase_shift(parts[step], 2, step))
-    r1, r2, r3, first, second, sizes, esp, square_repulsion = lax.optimization_barrier(
-        (r1, r2, r3, first, second, sizes, esp, square_repulsion)
+    r1, r2, r3, first, second, sizes, esp, left, square_repulsion = lax.optimization_barrier(
+        (r1, r2, r3, first, second, sizes, esp, left, square_repulsion)
     )
     own_sum, other_sum = [(r0[h] + r1[h]) + (r2[h] + r3[h]) for h in (slice(0, 8), slice(8, 16))]
     theirs = swap_cores(other_sum)
     stack, energy = solve(
-        segment_array, sizes, own_sum, theirs, first, second, esp, square_repulsion
+        sizes, own_sum, theirs, first, second, esp, left, square_repulsion
     )
 
     for axis in GRP:

time: 101 us -> 97.2 us (0.962)
  Pallas kernels: 33.7 us -> 30.4 us
    pallas_call x1, Pallas kernels: 22.7 us -> 19.4 us  [solve(): pl.pallas_call(solve_kernel, name='solve', in_specs=[pl.BlockSpec(memory_...]
  transfers between devices with their start and end apart: 21 -> 21, of which waited for: 15 -> 15; matrix products, arithmetic and copies ran while one was open for 10% -> 10% of each run, Pallas kernels for 6% -> 7%
where the time goes in v1:
time: 97.2 us; the launch traced here: 95.5 us
  Pallas kernels  30.4 us (31%)
  starting transfers between devices  26.6 us (27%)
  waiting for transfers between devices  22.8 us (23%)
  local copies, waits for them, and re-layouts  10.6 us (11%)
  between operations  2.63 us (3%)
  other arithmetic  2.48 us (3%)
    pallas_call x1, Pallas kernels, solve(): pl.pallas_call(solve_kernel, name='solve', in_specs=[pl.BlockSpec(memory_...  19.4 us
    ppermute x9, starting transfers between devices, phase_shift(): return lax.ppermute(value, ALL, pairs)  15.8 us
    ppermute x9, waiting for transfers between devices, axis_shift(): return lax.ppermute(value, axis, [(i, (i + step) % 4) for i in range(4)])  11.3 us
    ppermute x9, waiting for transfers between devices, phase_shift(): return lax.ppermute(value, ALL, pairs)  10.8 us
    ppermute x9, starting transfers between devices, axis_shift(): return lax.ppermute(value, axis, [(i, (i + step) % 4) for i in range(4)])  10.7 us
    pallas_call x2, Pallas kernels, flatten(): pl.pallas_call(flatten_kernel, name='flatten', grid_spec=pltpu.PrefetchSc...  6.95 us
    pallas_call x1, Pallas kernels, unflatten(): pl.pallas_call(unflatten_kernel, name='unflatten', grid_spec=pltpu.Prefet...  2.75 us
  transfers between devices with their start and end apart: 21, of which 15 were waited for; matrix products, arithmetic and copies ran while one was open for 10% of the time, Pallas kernels for 7%

profile of v1, /device:TPU:0, one launch (start us, length us, event | category | flops | bytes accessed | tf_op | source)
XLA Modules:
  0.0 95.5 jit_solution(11611973112959345794)
XLA Ops:
  1.6 3.1 %collective-permute-start.2 = (bf16[8,4608]{1,0:T(8,128)(2,1)S(1)}, bf16[8,4608]{1,0:T(8,128)(2,1)S(1)}, u32[]{:S(2)}, u32[]{:S(2)}) collective-permute-start(bf16[8,4608]{1,0:T(8,128)(2,1)S(1)} %constant_dynamic-slice_fusion), channel_id=1, source_target_pairs={{0,3},{1,0},{2,1},{3,2},{4,7},{5,4},{6,5},{7,6},{8,11},{9,8},{10,9... | collective-permute-start | bytes 221192 | tf_op jit(solution)/shard_map/ppermute | solution.py:38
  6.9 3.7 %collective-permute-done.1 = bf16[8,4608]{1,0:T(8,128)(2,1)S(1)} collective-permute-done((bf16[8,4608]{1,0:T(8,128)(2,1)S(1)}, bf16[8,4608]{1,0:T(8,128)(2,1)S(1)}, u32[]{:S(2)}, u32[]{:S(2)}) %collective-permute-start.1) | collective-permute-done | bytes 73760 | tf_op jit(solution)/shard_map/ppermute | solution.py:38
  11.4 4.1 %collective-permute-start.5 = (bf16[32,4608]{1,0:T(8,128)(2,1)S(1)}, bf16[32,4608]{1,0:T(8,128)(2,1)S(1)}, u32[]{:S(2)}, u32[]{:S(2)}) collective-permute-start(bf16[32,4608]{1,0:T(8,128)(2,1)S(1)} %pad_maximum_fusion.b0), channel_id=1, source_target_pairs={{0,12},{1,13},{2,14},{3,15},{4,0},{5,1},{6,2},{7,3},{8,4},{9,5},{1... | collective-permute-start | bytes 884744 | tf_op jit(solution)/shard_map/ppermute | solution.py:38
  15.5 1.3 %collective-permute-start.3 = (bf16[32,4608]{1,0:T(8,128)(2,1)S(1)}, bf16[32,4608]{1,0:T(8,128)(2,1)S(1)}, u32[]{:S(2)}, u32[]{:S(2)}) collective-permute-start(bf16[32,4608]{1,0:T(8,128)(2,1)S(1)} %pad_maximum_fusion.b0), channel_id=1, source_target_pairs={{0,4},{1,5},{2,6},{3,7},{4,8},{5,9},{6,10},{7,11},{8,12},{9,13},{1... | collective-permute-start | bytes 884744 | tf_op jit(solution)/shard_map/ppermute | solution.py:38
  23.8 2.8 %collective-permute-done.3.b1 = bf16[32,4608]{1,0:T(8,128)(2,1)S(1)} collective-permute-done((bf16[32,4608]{1,0:T(8,128)(2,1)S(1)}, bf16[32,4608]{1,0:T(8,128)(2,1)S(1)}, u32[]{:S(2)}, u32[]{:S(2)}) %collective-permute-start.3) | collective-permute-done | bytes 294944 | tf_op jit(solution)/shard_map/ppermute | solution.py:38
  26.6 1.3 %partial_fields.1 = (f32[16,4608]{1,0:T(8,128)}, f32[16,4608]{1,0:T(8,128)}, f32[16,4608]{1,0:T(8,128)}, f32[16,4608]{1,0:T(8,128)}) custom-call(bf16[64,128]{1,0:T(8,128)(2,1)S(1)} %select_convert_fusion.weight_ref, bf16[32,4608]{1,0:T(8,128)(2,1)S(1)} %pad_maximum_fusion.b0, bf16[32,4608]{1,0:T(8,128)(2,1)S(1)} %collective-permute-done.3.b1, ...), custom_call_target="tpu_custom_call" | custom-call | flops 80000000 | bytes 2400000 | tf_op jit(solution)/shard_map/partial_fields/pallas_call | solution.py:163
  27.9 1.5 %collective-permute-start.6 = (f32[16,4608]{1,0:T(8,128)}, f32[16,4608]{1,0:T(8,128)S(1)}, u32[]{:S(2)}, u32[]{:S(2)}) collective-permute-start(f32[16,4608]{1,0:T(8,128)} %get-tuple-element.28), channel_id=1, source_target_pairs={{0,16},{1,17},{2,18},{3,19},{4,20},{5,21},{6,22},{7,23},{8,24},{9,... | collective-permute-start | bytes 884744 | tf_op jit(solution)/shard_map/ppermute | solution.py:38
  29.4 2.7 %collective-permute-start.7 = (f32[16,4608]{1,0:T(8,128)}, f32[16,4608]{1,0:T(8,128)S(1)}, u32[]{:S(2)}, u32[]{:S(2)}) collective-permute-start(f32[16,4608]{1,0:T(8,128)} %get-tuple-element.29), channel_id=1, source_target_pairs={{0,32},{1,33},{2,34},{3,35},{4,36},{5,37},{6,38},{7,39},{8,40},{9,... | collective-permute-start | bytes 884744 | tf_op jit(solution)/shard_map/ppermute | solution.py:38
  32.1 1.4 %collective-permute-start.8 = (f32[16,4608]{1,0:T(8,128)}, f32[16,4608]{1,0:T(8,128)S(1)}, u32[]{:S(2)}, u32[]{:S(2)}) collective-permute-start(f32[16,4608]{1,0:T(8,128)} %get-tuple-element.30), channel_id=1, source_target_pairs={{0,48},{1,49},{2,50},{3,51},{4,52},{5,53},{6,54},{7,55},{8,56},{9,... | collective-permute-start | bytes 884744 | tf_op jit(solution)/shard_map/ppermute | solution.py:38
  35.8 2.7 %unflatten.1 = (f32[1536,128]{1,0:T(8,128)}, f32[1536,128]{1,0:T(8,128)}, f32[96,192]{1,0:T(8,128)}) custom-call(s32[1]{0:T(128)} %bitcast.segment_ref, f32[16,36864]{1,0:T(8,128)} %core_ref, f32[96,192]{1,0:T(8,128)} %esp_any), custom_call_target="tpu_custom_call" | custom-call | flops 20000000 | bytes 3000000 | tf_op jit(solution)/shard_map/unflatten/pallas_call | solution.py:97
  38.5 1.7 %collective-permute-done.7 = f32[16,4608]{1,0:T(8,128)S(1)} collective-permute-done((f32[16,4608]{1,0:T(8,128)}, f32[16,4608]{1,0:T(8,128)S(1)}, u32[]{:S(2)}, u32[]{:S(2)}) %collective-permute-start.7) | collective-permute-done | bytes 294944 | tf_op jit(solution)/shard_map/ppermute | solution.py:38
  42.9 19.4 %solve.1 = (f32[2,8,192,192]{3,2,1,0:T(8,128)}, f32[8,128]{1,0:T(8,128)}) custom-call(s32[8,2]{1,0:T(8,128)} %bitcast.32, f32[8,4608]{1,0:T(8,128)} %get-tuple-element.59.mine_any, f32[8,4608]{1,0:T(8,128)} %copy-done.5, f32[1536,128]{1,0:T(8,128)} %get-tuple-element.43.first_any, f32[1536,128]{1,0:T(8,128)} %get-tuple-element.44.second_any, ...), custom_call_target="tpu_custom_call" | custom-call | flops 11000000512 | bytes 6000000 | tf_op jit(solution)/shard_map/solve/pallas_call | solution.py:359
  62.4 3.5 %flatten.3 = f32[8,36864]{1,0:T(8,128)} custom-call(s32[2]{0:T(128)} %pad_add_fusion.1.place_ref, f32[2,8,192,192]{3,2,1,0:T(8,128)} %get-tuple-element.48.square_ref), custom_call_target="tpu_custom_call" | custom-call | flops 20000000 | bytes 3000000 | tf_op jit(solution)/shard_map/flatten/pallas_call | solution.py:134
  66.0 2.5 %collective-permute-start.13 = (f32[8,128]{1,0:T(8,128)S(1)}, f32[8,128]{1,0:T(8,128)S(1)}, u32[]{:S(2)}, u32[]{:S(2)}) collective-permute-start(f32[8,128]{1,0:T(8,128)S(1)} %copy-done.4), channel_id=1, source_target_pairs={{0,48},{16,0},{32,16},{48,32},{1,49},{17,1},{33,17},{49,33},{2,50}... | collective-permute-start | bytes 12296 | tf_op jit(solution)/shard_map/ppermute | solution.py:49
  68.6 2.4 %collective-permute-start.11 = (f32[8,128]{1,0:T(8,128)S(1)}, f32[8,128]{1,0:T(8,128)S(1)}, u32[]{:S(2)}, u32[]{:S(2)}) collective-permute-start(f32[8,128]{1,0:T(8,128)S(1)} %copy-done.4), channel_id=1, source_target_pairs={{0,32},{16,48},{32,0},{48,16},{1,33},{17,49},{33,1},{49,17},{2,34}... | collective-permute-start | bytes 12296 | tf_op jit(solution)/shard_map/ppermute | solution.py:49
  71.0 2.4 %collective-permute-done.12 = f32[8,128]{1,0:T(8,128)S(1)} collective-permute-done((f32[8,128]{1,0:T(8,128)S(1)}, f32[8,128]{1,0:T(8,128)S(1)}, u32[]{:S(2)}, u32[]{:S(2)}) %collective-permute-start.12) | collective-permute-done | bytes 4128 | tf_op jit(solution)/shard_map/ppermute | solution.py:49
  76.1 1.2 %collective-permute-done.16 = f32[8,128]{1,0:T(8,128)S(1)} collective-permute-done((f32[8,128]{1,0:T(8,128)S(1)}, f32[8,128]{1,0:T(8,128)S(1)}, u32[]{:S(2)}, u32[]{:S(2)}) %collective-permute-start.16) | collective-permute-done | bytes 4128 | tf_op jit(solution)/shard_map/ppermute | solution.py:49
  77.3 2.1 %collective-permute-done.15 = f32[8,128]{1,0:T(8,128)S(1)} collective-permute-done((f32[8,128]{1,0:T(8,128)S(1)}, f32[8,128]{1,0:T(8,128)S(1)}, u32[]{:S(2)}, u32[]{:S(2)}) %collective-permute-start.15) | collective-permute-done | bytes 4128 | tf_op jit(solution)/shard_map/ppermute | solution.py:49
  79.4 1.4 %collective-permute-done.14 = f32[8,128]{1,0:T(8,128)S(1)} collective-permute-done((f32[8,128]{1,0:T(8,128)S(1)}, f32[8,128]{1,0:T(8,128)S(1)}, u32[]{:S(2)}, u32[]{:S(2)}) %collective-permute-start.14) | collective-permute-done | bytes 4128 | tf_op jit(solution)/shard_map/ppermute | solution.py:49
  81.4 1.5 %collective-permute-start.18 = (f32[8,128]{1,0:T(8,128)S(1)}, f32[8,128]{1,0:T(8,128)S(1)}, u32[]{:S(2)}, u32[]{:S(2)}) collective-permute-start(f32[8,128]{1,0:T(8,128)S(1)} %add_add_fusion.3), channel_id=1, source_target_pairs={{0,1},{1,2},{2,3},{3,0},{4,5},{5,6},{6,7},{7,4},{8,9},{9,10},{10,1... | collective-permute-start | bytes 12296 | tf_op jit(solution)/shard_map/ppermute | solution.py:49
  82.8 1.2 %collective-permute-start.17 = (f32[8,128]{1,0:T(8,128)S(1)}, f32[8,128]{1,0:T(8,128)S(1)}, u32[]{:S(2)}, u32[]{:S(2)}) collective-permute-start(f32[8,128]{1,0:T(8,128)S(1)} %add_add_fusion.3), channel_id=1, source_target_pairs={{0,2},{1,3},{2,0},{3,1},{4,6},{5,7},{6,4},{7,5},{8,10},{9,11},{10,... | collective-permute-start | bytes 12296 | tf_op jit(solution)/shard_map/ppermute | solution.py:49
  84.4 1.8 %collective-permute-done.18 = f32[8,128]{1,0:T(8,128)S(1)} collective-permute-done((f32[8,128]{1,0:T(8,128)S(1)}, f32[8,128]{1,0:T(8,128)S(1)}, u32[]{:S(2)}, u32[]{:S(2)}) %collective-permute-start.18) | collective-permute-done | bytes 4128 | tf_op jit(solution)/shard_map/ppermute | solution.py:49
  86.2 1.7 %collective-permute-done.17 = f32[8,128]{1,0:T(8,128)S(1)} collective-permute-done((f32[8,128]{1,0:T(8,128)S(1)}, f32[8,128]{1,0:T(8,128)S(1)}, u32[]{:S(2)}, u32[]{:S(2)}) %collective-permute-start.17) | collective-permute-done | bytes 4128 | tf_op jit(solution)/shard_map/ppermute | solution.py:49
  88.6 3.5 %flatten.2 = f32[16,36864]{1,0:T(8,128)} custom-call(s32[2]{0:T(128)} %pad_add_fusion.place_ref, f32[2,8,192,192]{3,2,1,0:T(8,128)} %get-tuple-element.48.square_ref), custom_call_target="tpu_custom_call" | custom-call | flops 20000000 | bytes 3000000 | tf_op jit(solution)/shard_map/flatten/pallas_call | solution.py:134
  (83 shorter events, 21.9 us)
Async XLA Ops:
  0.6 34.4 %copy-start.3 = (f32[36864]{0:T(1024)S(1)}, f32[36864]{0:T(1024)}, u32[]{:S(2)}) copy-start(f32[36864]{0:T(1024)} %param.13) | copy-start | bytes 442372
  0.7 32.9 %copy-start.1 = (s32[512]{0:T(512)S(1)}, s32[512]{0:T(512)}, u32[]{:S(2)}) copy-start(s32[512]{0:T(512)} %param.10) | copy-start | bytes 6148
  1.6 5.3 %collective-permute-start.2 = (bf16[8,4608]{1,0:T(8,128)(2,1)S(1)}, bf16[8,4608]{1,0:T(8,128)(2,1)S(1)}, u32[]{:S(2)}, u32[]{:S(2)}) collective-permute-start(bf16[8,4608]{1,0:T(8,128)(2,1)S(1)} %constant_dynamic-slice_fusion), channel_id=1, source_target_pairs={{0,3},{1,0},{2,1},{3,2},{4,7},{5,4},{6,5},{7,6},{8,11},{9,8},{10,9... | collective-permute-start | bytes 221192 | tf_op jit(solution)/shard_map/ppermute | solution.py:38
  4.7 5.9 %collective-permute-start.1 = (bf16[8,4608]{1,0:T(8,128)(2,1)S(1)}, bf16[8,4608]{1,0:T(8,128)(2,1)S(1)}, u32[]{:S(2)}, u32[]{:S(2)}) collective-permute-start(bf16[8,4608]{1,0:T(8,128)(2,1)S(1)} %constant_dynamic-slice_fusion), channel_id=1, source_target_pairs={{0,2},{1,3},{2,0},{3,1},{4,6},{5,7},{6,4},{7,5},{8,10},{9,11},{10,... | collective-permute-start | bytes 221192 | tf_op jit(solution)/shard_map/ppermute | solution.py:38
  5.3 6.0 %collective-permute-start = (bf16[8,4608]{1,0:T(8,128)(2,1)S(1)}, bf16[8,4608]{1,0:T(8,128)(2,1)S(1)}, u32[]{:S(2)}, u32[]{:S(2)}) collective-permute-start(bf16[8,4608]{1,0:T(8,128)(2,1)S(1)} %constant_dynamic-slice_fusion), channel_id=1, source_target_pairs={{0,1},{1,2},{2,3},{3,0},{4,5},{5,6},{6,7},{7,4},{8,9},{9,10},{10,1... | collective-permute-start | bytes 221192 | tf_op jit(solution)/shard_map/ppermute | solution.py:38
  11.4 11.5 %collective-permute-start.5 = (bf16[32,4608]{1,0:T(8,128)(2,1)S(1)}, bf16[32,4608]{1,0:T(8,128)(2,1)S(1)}, u32[]{:S(2)}, u32[]{:S(2)}) collective-permute-start(bf16[32,4608]{1,0:T(8,128)(2,1)S(1)} %pad_maximum_fusion.b0), channel_id=1, source_target_pairs={{0,12},{1,13},{2,14},{3,15},{4,0},{5,1},{6,2},{7,3},{8,4},{9,5},{1... | collective-permute-start | bytes 884744 | tf_op jit(solution)/shard_map/ppermute | solution.py:38
  15.5 8.3 %collective-permute-start.4 = (bf16[32,4608]{1,0:T(8,128)(2,1)S(1)}, bf16[32,4608]{1,0:T(8,128)(2,1)S(1)}, u32[]{:S(2)}, u32[]{:S(2)}) collective-permute-start(bf16[32,4608]{1,0:T(8,128)(2,1)S(1)} %pad_maximum_fusion.b0), channel_id=1, source_target_pairs={{0,8},{1,9},{2,10},{3,11},{4,12},{5,13},{6,14},{7,15},{8,0},{9,1},... | collective-permute-start | bytes 884744 | tf_op jit(solution)/shard_map/ppermute | solution.py:38
  15.5 11.1 %collective-permute-start.3 = (bf16[32,4608]{1,0:T(8,128)(2,1)S(1)}, bf16[32,4608]{1,0:T(8,128)(2,1)S(1)}, u32[]{:S(2)}, u32[]{:S(2)}) collective-permute-start(bf16[32,4608]{1,0:T(8,128)(2,1)S(1)} %pad_maximum_fusion.b0), channel_id=1, source_target_pairs={{0,4},{1,5},{2,6},{3,7},{4,8},{5,9},{6,10},{7,11},{8,12},{9,13},{1... | collective-permute-start | bytes 884744 | tf_op jit(solution)/shard_map/ppermute | solution.py:38
  27.9 12.3 %copy-start.2 = (f32[16,4608]{1,0:T(8,128)S(1)}, f32[16,4608]{1,0:T(8,128)}, u32[]{:S(2)}) copy-start(f32[16,4608]{1,0:T(8,128)} %get-tuple-element.31) | copy-start | bytes 884740
  27.9 10.6 %collective-permute-start.6 = (f32[16,4608]{1,0:T(8,128)}, f32[16,4608]{1,0:T(8,128)S(1)}, u32[]{:S(2)}, u32[]{:S(2)}) collective-permute-start(f32[16,4608]{1,0:T(8,128)} %get-tuple-element.28), channel_id=1, source_target_pairs={{0,16},{1,17},{2,18},{3,19},{4,20},{5,21},{6,22},{7,23},{8,24},{9,... | collective-permute-start | bytes 884744 | tf_op jit(solution)/shard_map/ppermute | solution.py:38
  29.4 10.8 %collective-permute-start.7 = (f32[16,4608]{1,0:T(8,128)}, f32[16,4608]{1,0:T(8,128)S(1)}, u32[]{:S(2)}, u32[]{:S(2)}) collective-permute-start(f32[16,4608]{1,0:T(8,128)} %get-tuple-element.29), channel_id=1, source_target_pairs={{0,32},{1,33},{2,34},{3,35},{4,36},{5,37},{6,38},{7,39},{8,40},{9,... | collective-permute-start | bytes 884744 | tf_op jit(solution)/shard_map/ppermute | solution.py:38
  32.1 8.1 %collective-permute-start.8 = (f32[16,4608]{1,0:T(8,128)}, f32[16,4608]{1,0:T(8,128)S(1)}, u32[]{:S(2)}, u32[]{:S(2)}) collective-permute-start(f32[16,4608]{1,0:T(8,128)} %get-tuple-element.30), channel_id=1, source_target_pairs={{0,48},{1,49},{2,50},{3,51},{4,52},{5,53},{6,54},{7,55},{8,56},{9,... | collective-permute-start | bytes 884744 | tf_op jit(solution)/shard_map/ppermute | solution.py:38
  40.9 1.4 %collective-permute-start.9 = (f32[8,4608]{1,0:T(8,128)S(1)}, f32[8,4608]{1,0:T(8,128)S(1)}, u32[]{:S(2)}, u32[]{:S(2)}) collective-permute-start(f32[8,4608]{1,0:T(8,128)S(1)} %get-tuple-element.58), channel_id=1, source_target_pairs={{0,64},{64,0},{1,65},{65,1},{2,66},{66,2},{3,67},{67,3},{4,68},{68... | collective-permute-start | bytes 442376 | tf_op jit(solution)/shard_map/ppermute | solution.py:53
  65.9 27.4 %collective-permute-start.10 = (f32[8,36864]{1,0:T(8,128)}, f32[8,36864]{1,0:T(8,128)S(1)}, u32[]{:S(2)}, u32[]{:S(2)}) collective-permute-start(f32[8,36864]{1,0:T(8,128)} %flatten.3), channel_id=1, source_target_pairs={{0,64},{64,0},{1,65},{65,1},{2,66},{66,2},{3,67},{67,3},{4,68},{68... | collective-permute-start | bytes 3538952 | tf_op jit(solution)/shard_map/ppermute | solution.py:53
  66.0 5.0 %collective-permute-start.13 = (f32[8,128]{1,0:T(8,128)S(1)}, f32[8,128]{1,0:T(8,128)S(1)}, u32[]{:S(2)}, u32[]{:S(2)}) collective-permute-start(f32[8,128]{1,0:T(8,128)S(1)} %copy-done.4), channel_id=1, source_target_pairs={{0,48},{16,0},{32,16},{48,32},{1,49},{17,1},{33,17},{49,33},{2,50}... | collective-permute-start | bytes 12296 | tf_op jit(solution)/shard_map/ppermute | solution.py:49
  68.5 4.8 %collective-permute-start.12 = (f32[8,128]{1,0:T(8,128)S(1)}, f32[8,128]{1,0:T(8,128)S(1)}, u32[]{:S(2)}, u32[]{:S(2)}) collective-permute-start(f32[8,128]{1,0:T(8,128)S(1)} %copy-done.4), channel_id=1, source_target_pairs={{0,16},{16,32},{32,48},{48,0},{1,17},{17,33},{33,49},{49,1},{2,18}... | collective-permute-start | bytes 12296 | tf_op jit(solution)/shard_map/ppermute | solution.py:49
  68.6 5.1 %collective-permute-start.11 = (f32[8,128]{1,0:T(8,128)S(1)}, f32[8,128]{1,0:T(8,128)S(1)}, u32[]{:S(2)}, u32[]{:S(2)}) collective-permute-start(f32[8,128]{1,0:T(8,128)S(1)} %copy-done.4), channel_id=1, source_target_pairs={{0,32},{16,48},{32,0},{48,16},{1,33},{17,49},{33,1},{49,17},{2,34}... | collective-permute-start | bytes 12296 | tf_op jit(solution)/shard_map/ppermute | solution.py:49
  73.7 3.6 %collective-permute-start.16 = (f32[8,128]{1,0:T(8,128)S(1)}, f32[8,128]{1,0:T(8,128)S(1)}, u32[]{:S(2)}, u32[]{:S(2)}) collective-permute-start(f32[8,128]{1,0:T(8,128)S(1)} %add_add_fusion.4), channel_id=1, source_target_pairs={{0,12},{4,0},{8,4},{12,8},{1,13},{5,1},{9,5},{13,9},{2,14},{6,2},{... | collective-permute-start | bytes 12296 | tf_op jit(solution)/shard_map/ppermute | solution.py:49
  74.6 4.8 %collective-permute-start.15 = (f32[8,128]{1,0:T(8,128)S(1)}, f32[8,128]{1,0:T(8,128)S(1)}, u32[]{:S(2)}, u32[]{:S(2)}) collective-permute-start(f32[8,128]{1,0:T(8,128)S(1)} %add_add_fusion.4), channel_id=1, source_target_pairs={{0,4},{4,8},{8,12},{12,0},{1,5},{5,9},{9,13},{13,1},{2,6},{6,10},{... | collective-permute-start | bytes 12296 | tf_op jit(solution)/shard_map/ppermute | solution.py:49
  75.7 5.1 %collective-permute-start.14 = (f32[8,128]{1,0:T(8,128)S(1)}, f32[8,128]{1,0:T(8,128)S(1)}, u32[]{:S(2)}, u32[]{:S(2)}) collective-permute-start(f32[8,128]{1,0:T(8,128)S(1)} %add_add_fusion.4), channel_id=1, source_target_pairs={{0,8},{4,12},{8,0},{12,4},{1,9},{5,13},{9,1},{13,5},{2,10},{6,14},... | collective-permute-start | bytes 12296 | tf_op jit(solution)/shard_map/ppermute | solution.py:49
  80.8 3.6 %collective-permute-start.19 = (f32[8,128]{1,0:T(8,128)S(1)}, f32[8,128]{1,0:T(8,128)S(1)}, u32[]{:S(2)}, u32[]{:S(2)}) collective-permute-start(f32[8,128]{1,0:T(8,128)S(1)} %add_add_fusion.3), channel_id=1, source_target_pairs={{0,3},{1,0},{2,1},{3,2},{4,7},{5,4},{6,5},{7,6},{8,11},{9,8},{10,9... | collective-permute-start | bytes 12296 | tf_op jit(solution)/shard_map/ppermute | solution.py:49
  81.4 4.8 %collective-permute-start.18 = (f32[8,128]{1,0:T(8,128)S(1)}, f32[8,128]{1,0:T(8,128)S(1)}, u32[]{:S(2)}, u32[]{:S(2)}) collective-permute-start(f32[8,128]{1,0:T(8,128)S(1)} %add_add_fusion.3), channel_id=1, source_target_pairs={{0,1},{1,2},{2,3},{3,0},{4,5},{5,6},{6,7},{7,4},{8,9},{9,10},{10,1... | collective-permute-start | bytes 12296 | tf_op jit(solution)/shard_map/ppermute | solution.py:49
  82.8 5.1 %collective-permute-start.17 = (f32[8,128]{1,0:T(8,128)S(1)}, f32[8,128]{1,0:T(8,128)S(1)}, u32[]{:S(2)}, u32[]{:S(2)}) collective-permute-start(f32[8,128]{1,0:T(8,128)S(1)} %add_add_fusion.3), channel_id=1, source_target_pairs={{0,2},{1,3},{2,0},{3,1},{4,6},{5,7},{6,4},{7,5},{8,10},{9,11},{10,... | collective-permute-start | bytes 12296 | tf_op jit(solution)/shard_map/ppermute | solution.py:49
  88.0 4.1 %collective-permute-start.20 = (f32[8,128]{1,0:T(8,128)S(1)}, f32[8,128]{1,0:T(8,128)S(1)}, u32[]{:S(2)}, u32[]{:S(2)}) collective-permute-start(f32[8,128]{1,0:T(8,128)S(1)} %add_add_fusion.2), channel_id=1, source_target_pairs={{0,64},{64,0},{1,65},{65,1},{2,66},{66,2},{3,67},{67,3},{4,68},{68... | collective-permute-start | bytes 12296 | tf_op jit(solution)/shard_map/ppermute | solution.py:53
  (3 other events, 5.2 us)

commit v2 on v1

--- a/solution.py
+++ b/solution.py
@@ -325,7 +325,7 @@
         if singles > 0:
             lax.fori_loop(0, singles, single, 0)
         if singles < PURIFY:
-            lax.fori_loop(singles, PURIFY, triple, 0)
+            lax.fori_loop(singles, PURIFY, triple, 0, unroll=True)
 
     start(masked, jnp.zeros((LOCAL, BD), f32))
     purify(SINGLE[0])
@@ -347,7 +347,7 @@
         leaving[-1].start()
         both = with_diagonal(masked[d] + offset[d], extra[d : d + 1, :])
         diagonal[d : d + 1, :] = jnp.sum(solved * both, axis=0, keepdims=True)
-    energy = jnp.sum(diagonal[...], axis=1, keepdims=True) * (0.5 / count)
+    energy = jnp.sum(diagonal[...], axis=1, keepdims=True) * (0.5 / (1024.0 * count))
     energy_out[...] = jnp.broadcast_to(jnp.sum(energy, axis=0, keepdims=True), (8, 128))
     for copy in leaving:
         copy.wait()
@@ -446,11 +446,15 @@
     square_repulsion = rep.reshape(BD, BD)
 
     r0 = parts[0]
-    r1, r2, r3 = shifts(lambda step: phase_shift(parts[step], 2, step))
+    narrow = [part.astype(jnp.float16) for part in parts]
+    r1, r2, r3 = shifts(lambda step: phase_shift(narrow[step], 2, step))
     r1, r2, r3, first, second, sizes, esp, left, square_repulsion = lax.optimization_barrier(
         (r1, r2, r3, first, second, sizes, esp, left, square_repulsion)
     )
-    own_sum, other_sum = [(r0[h] + r1[h]) + (r2[h] + r3[h]) for h in (slice(0, 8), slice(8, 16))]
+    own_sum, other_sum = [
+        (r0[h] + r1[h].astype(f32)) + (r2[h].astype(f32) + r3[h].astype(f32))
+        for h in (slice(0, 8), slice(8, 16))
+    ]
     theirs = swap_cores(other_sum)
     stack, energy = solve(
         sizes, own_sum, theirs, first, second, esp, left, square_repulsion
@@ -460,7 +464,7 @@
         one, two, three = shifts(axis_shift, energy, axis)
         energy = (energy + two) + (one + three)
     energy = energy + swap_cores(energy)
-    window_energy = energy[0, 0] / 1024.0
+    window_energy = energy[0, 0]
 
     sent = flatten(jnp.stack([1 - segment, 0 * segment]).astype(jnp.int32), stack, LOCAL)
     arrived = swap_cores(sent)

time: 97.2 us -> 96 us (0.988)
  starting transfers between devices: 26.6 us -> 23.3 us
  other arithmetic: 2.48 us -> 5.46 us
  between operations: 2.63 us -> 0.85 us
  waiting for transfers between devices: 22.8 us -> 24.3 us
    convert_element_type x0 -> x3, other arithmetic: none -> 2.98 us  [on_device(): narrow = [part.astype(jnp.float16) for part in parts]]
    ppermute x9, starting transfers between devices: 10.7 us -> 8.52 us  [axis_shift(): return lax.ppermute(value, axis, [(i, (i + step) % 4) for i in range(4)])]
    ppermute x9, waiting for transfers between devices: 11.3 us -> 12.9 us  [axis_shift(): return lax.ppermute(value, axis, [(i, (i + step) % 4) for i in range(4)])]
    ppermute x9, starting transfers between devices: 15.8 us -> 14.6 us  [phase_shift(): return lax.ppermute(value, ALL, pairs)]
  transfers between devices with their start and end apart: 21 -> 21, of which waited for: 15 -> 17; matrix products, arithmetic and copies ran while one was open for 10% -> 10% of each run, Pallas kernels for 7% -> 7%
where the time goes in v2:
time: 96 us; the launch traced here: 94.2 us
  Pallas kernels  29.8 us (31%)
  waiting for transfers between devices  24.3 us (25%)
  starting transfers between devices  23.3 us (24%)
  local copies, waits for them, and re-layouts  10.6 us (11%)
  other arithmetic  5.46 us (6%)
    pallas_call x1, Pallas kernels, solve(): pl.pallas_call(solve_kernel, name='solve', in_specs=[pl.BlockSpec(memory_...  18.8 us
    ppermute x9, starting transfers between devices, phase_shift(): return lax.ppermute(value, ALL, pairs)  14.6 us
    ppermute x9, waiting for transfers between devices, axis_shift(): return lax.ppermute(value, axis, [(i, (i + step) % 4) for i in range(4)])  12.9 us
    ppermute x9, waiting for transfers between devices, phase_shift(): return lax.ppermute(value, ALL, pairs)  10.7 us
    ppermute x9, starting transfers between devices, axis_shift(): return lax.ppermute(value, axis, [(i, (i + step) % 4) for i in range(4)])  8.52 us
    pallas_call x2, Pallas kernels, flatten(): pl.pallas_call(flatten_kernel, name='flatten', grid_spec=pltpu.PrefetchSc...  6.95 us
    convert_element_type x3, other arithmetic, on_device(): narrow = [part.astype(jnp.float16) for part in parts]  2.98 us
    pallas_call x1, Pallas kernels, unflatten(): pl.pallas_call(unflatten_kernel, name='unflatten', grid_spec=pltpu.Prefet...  2.75 us
  transfers between devices with their start and end apart: 21, of which 17 were waited for; matrix products, arithmetic and copies ran while one was open for 10% of the time, Pallas kernels for 7%

profile of v2, /device:TPU:0, one launch (start us, length us, event | category | flops | bytes accessed | tf_op | source)
XLA Modules:
  0.0 94.2 jit_solution(10413105642527080229)
XLA Ops:
  1.6 3.1 %collective-permute-start.2 = (bf16[8,4608]{1,0:T(8,128)(2,1)S(1)}, bf16[8,4608]{1,0:T(8,128)(2,1)S(1)}, u32[]{:S(2)}, u32[]{:S(2)}) collective-permute-start(bf16[8,4608]{1,0:T(8,128)(2,1)S(1)} %constant_dynamic-slice_fusion), channel_id=1, source_target_pairs={{0,3},{1,0},{2,1},{3,2},{4,7},{5,4},{6,5},{7,6},{8,11},{9,8},{10,9... | collective-permute-start | bytes 221192 | tf_op jit(solution)/shard_map/ppermute | solution.py:38
  6.9 3.7 %collective-permute-done.1 = bf16[8,4608]{1,0:T(8,128)(2,1)S(1)} collective-permute-done((bf16[8,4608]{1,0:T(8,128)(2,1)S(1)}, bf16[8,4608]{1,0:T(8,128)(2,1)S(1)}, u32[]{:S(2)}, u32[]{:S(2)}) %collective-permute-start.1) | collective-permute-done | bytes 73760 | tf_op jit(solution)/shard_map/ppermute | solution.py:38
  11.3 4.1 %collective-permute-start.5 = (bf16[32,4608]{1,0:T(8,128)(2,1)S(1)}, bf16[32,4608]{1,0:T(8,128)(2,1)S(1)}, u32[]{:S(2)}, u32[]{:S(2)}) collective-permute-start(bf16[32,4608]{1,0:T(8,128)(2,1)S(1)} %pad_maximum_fusion.b0), channel_id=1, source_target_pairs={{0,12},{1,13},{2,14},{3,15},{4,0},{5,1},{6,2},{7,3},{8,4},{9,5},{1... | collective-permute-start | bytes 884744 | tf_op jit(solution)/shard_map/ppermute | solution.py:38
  15.5 1.3 %collective-permute-start.3 = (bf16[32,4608]{1,0:T(8,128)(2,1)S(1)}, bf16[32,4608]{1,0:T(8,128)(2,1)S(1)}, u32[]{:S(2)}, u32[]{:S(2)}) collective-permute-start(bf16[32,4608]{1,0:T(8,128)(2,1)S(1)} %pad_maximum_fusion.b0), channel_id=1, source_target_pairs={{0,4},{1,5},{2,6},{3,7},{4,8},{5,9},{6,10},{7,11},{8,12},{9,13},{1... | collective-permute-start | bytes 884744 | tf_op jit(solution)/shard_map/ppermute | solution.py:38
  23.8 2.8 %collective-permute-done.3.b1 = bf16[32,4608]{1,0:T(8,128)(2,1)S(1)} collective-permute-done((bf16[32,4608]{1,0:T(8,128)(2,1)S(1)}, bf16[32,4608]{1,0:T(8,128)(2,1)S(1)}, u32[]{:S(2)}, u32[]{:S(2)}) %collective-permute-start.3) | collective-permute-done | bytes 294944 | tf_op jit(solution)/shard_map/ppermute | solution.py:38
  26.6 1.3 %partial_fields.1 = (f32[16,4608]{1,0:T(8,128)}, f32[16,4608]{1,0:T(8,128)}, f32[16,4608]{1,0:T(8,128)}, f32[16,4608]{1,0:T(8,128)}) custom-call(bf16[64,128]{1,0:T(8,128)(2,1)S(1)} %select_convert_fusion.weight_ref, bf16[32,4608]{1,0:T(8,128)(2,1)S(1)} %pad_maximum_fusion.b0, bf16[32,4608]{1,0:T(8,128)(2,1)S(1)} %collective-permute-done.3.b1, ...), custom_call_target="tpu_custom_call" | custom-call | flops 80000000 | bytes 2400000 | tf_op jit(solution)/shard_map/partial_fields/pallas_call | solution.py:163
  30.8 2.8 %collective-permute-start.8 = (f16[16,4608]{1,0:T(8,128)(2,1)S(1)}, f16[16,4608]{1,0:T(8,128)(2,1)S(1)}, u32[]{:S(2)}, u32[]{:S(2)}) collective-permute-start(f16[16,4608]{1,0:T(8,128)(2,1)S(1)} %convert_element_type.33), channel_id=1, source_target_pairs={{0,48},{1,49},{2,50},{3,51},{4,52},{5,53},{6,54},{7,55},{8,56},{9,... | collective-permute-start | bytes 442376 | tf_op jit(solution)/shard_map/ppermute | solution.py:38
  37.6 2.7 %unflatten.1 = (f32[1536,128]{1,0:T(8,128)}, f32[1536,128]{1,0:T(8,128)}, f32[96,192]{1,0:T(8,128)}) custom-call(s32[1]{0:T(128)} %bitcast.segment_ref, f32[16,36864]{1,0:T(8,128)} %core_ref, f32[96,192]{1,0:T(8,128)} %esp_any), custom_call_target="tpu_custom_call" | custom-call | flops 20000000 | bytes 3000000 | tf_op jit(solution)/shard_map/unflatten/pallas_call | solution.py:97
  40.4 1.5 %collective-permute-done.6 = f16[16,4608]{1,0:T(8,128)(2,1)S(1)} collective-permute-done((f16[16,4608]{1,0:T(8,128)(2,1)S(1)}, f16[16,4608]{1,0:T(8,128)(2,1)S(1)}, u32[]{:S(2)}, u32[]{:S(2)}) %collective-permute-start.6) | collective-permute-done | bytes 147488 | tf_op jit(solution)/shard_map/ppermute | solution.py:38
  44.7 18.8 %solve.1 = (f32[2,8,192,192]{3,2,1,0:T(8,128)}, f32[8,128]{1,0:T(8,128)}) custom-call(s32[8,2]{1,0:T(8,128)} %bitcast.32, f32[8,4608]{1,0:T(8,128)} %get-tuple-element.59.mine_any, f32[8,4608]{1,0:T(8,128)} %copy-done.5, f32[1536,128]{1,0:T(8,128)} %get-tuple-element.43.first_any, f32[1536,128]{1,0:T(8,128)} %get-tuple-element.44.second_any, ...), custom_call_target="tpu_custom_call" | custom-call | flops 11000000512 | bytes 6000000 | tf_op jit(solution)/shard_map/solve/pallas_call | solution.py:359
  63.4 3.5 %flatten.3 = f32[8,36864]{1,0:T(8,128)} custom-call(s32[2]{0:T(128)} %pad_add_fusion.1.place_ref, f32[2,8,192,192]{3,2,1,0:T(8,128)} %get-tuple-element.48.square_ref), custom_call_target="tpu_custom_call" | custom-call | flops 20000000 | bytes 3000000 | tf_op jit(solution)/shard_map/flatten/pallas_call | solution.py:134
  67.9 1.2 %collective-permute-start.12 = (f32[8,128]{1,0:T(8,128)S(1)}, f32[8,128]{1,0:T(8,128)S(1)}, u32[]{:S(2)}, u32[]{:S(2)}) collective-permute-start(f32[8,128]{1,0:T(8,128)S(1)} %copy-done.4), channel_id=1, source_target_pairs={{0,16},{16,32},{32,48},{48,0},{1,17},{17,33},{33,49},{49,1},{2,18}... | collective-permute-start | bytes 12296 | tf_op jit(solution)/shard_map/ppermute | solution.py:49
  70.7 2.0 %collective-permute-done.12 = f32[8,128]{1,0:T(8,128)S(1)} collective-permute-done((f32[8,128]{1,0:T(8,128)S(1)}, f32[8,128]{1,0:T(8,128)S(1)}, u32[]{:S(2)}, u32[]{:S(2)}) %collective-permute-start.12) | collective-permute-done | bytes 4128 | tf_op jit(solution)/shard_map/ppermute | solution.py:49
  72.7 1.5 %collective-permute-done.11 = f32[8,128]{1,0:T(8,128)S(1)} collective-permute-done((f32[8,128]{1,0:T(8,128)S(1)}, f32[8,128]{1,0:T(8,128)S(1)}, u32[]{:S(2)}, u32[]{:S(2)}) %collective-permute-start.11) | collective-permute-done | bytes 4128 | tf_op jit(solution)/shard_map/ppermute | solution.py:49
  75.1 1.1 %collective-permute-start.15 = (f32[8,128]{1,0:T(8,128)S(1)}, f32[8,128]{1,0:T(8,128)S(1)}, u32[]{:S(2)}, u32[]{:S(2)}) collective-permute-start(f32[8,128]{1,0:T(8,128)S(1)} %add_add_fusion.4), channel_id=1, source_target_pairs={{0,4},{4,8},{8,12},{12,0},{1,5},{5,9},{9,13},{13,1},{2,6},{6,10},{... | collective-permute-start | bytes 12296 | tf_op jit(solution)/shard_map/ppermute | solution.py:49
  76.7 1.2 %collective-permute-done.16 = f32[8,128]{1,0:T(8,128)S(1)} collective-permute-done((f32[8,128]{1,0:T(8,128)S(1)}, f32[8,128]{1,0:T(8,128)S(1)}, u32[]{:S(2)}, u32[]{:S(2)}) %collective-permute-start.16) | collective-permute-done | bytes 4128 | tf_op jit(solution)/shard_map/ppermute | solution.py:49
  77.8 2.1 %collective-permute-done.15 = f32[8,128]{1,0:T(8,128)S(1)} collective-permute-done((f32[8,128]{1,0:T(8,128)S(1)}, f32[8,128]{1,0:T(8,128)S(1)}, u32[]{:S(2)}, u32[]{:S(2)}) %collective-permute-start.15) | collective-permute-done | bytes 4128 | tf_op jit(solution)/shard_map/ppermute | solution.py:49
  79.9 1.4 %collective-permute-done.14 = f32[8,128]{1,0:T(8,128)S(1)} collective-permute-done((f32[8,128]{1,0:T(8,128)S(1)}, f32[8,128]{1,0:T(8,128)S(1)}, u32[]{:S(2)}, u32[]{:S(2)}) %collective-permute-start.14) | collective-permute-done | bytes 4128 | tf_op jit(solution)/shard_map/ppermute | solution.py:49
  81.9 1.5 %collective-permute-start.18 = (f32[8,128]{1,0:T(8,128)S(1)}, f32[8,128]{1,0:T(8,128)S(1)}, u32[]{:S(2)}, u32[]{:S(2)}) collective-permute-start(f32[8,128]{1,0:T(8,128)S(1)} %add_add_fusion.3), channel_id=1, source_target_pairs={{0,1},{1,2},{2,3},{3,0},{4,5},{5,6},{6,7},{7,4},{8,9},{9,10},{10,1... | collective-permute-start | bytes 12296 | tf_op jit(solution)/shard_map/ppermute | solution.py:49
  83.4 1.2 %collective-permute-start.17 = (f32[8,128]{1,0:T(8,128)S(1)}, f32[8,128]{1,0:T(8,128)S(1)}, u32[]{:S(2)}, u32[]{:S(2)}) collective-permute-start(f32[8,128]{1,0:T(8,128)S(1)} %add_add_fusion.3), channel_id=1, source_target_pairs={{0,2},{1,3},{2,0},{3,1},{4,6},{5,7},{6,4},{7,5},{8,10},{9,11},{10,... | collective-permute-start | bytes 12296 | tf_op jit(solution)/shard_map/ppermute | solution.py:49
  85.0 1.8 %collective-permute-done.18 = f32[8,128]{1,0:T(8,128)S(1)} collective-permute-done((f32[8,128]{1,0:T(8,128)S(1)}, f32[8,128]{1,0:T(8,128)S(1)}, u32[]{:S(2)}, u32[]{:S(2)}) %collective-permute-start.18) | collective-permute-done | bytes 4128 | tf_op jit(solution)/shard_map/ppermute | solution.py:49
  86.7 1.8 %collective-permute-done.17 = f32[8,128]{1,0:T(8,128)S(1)} collective-permute-done((f32[8,128]{1,0:T(8,128)S(1)}, f32[8,128]{1,0:T(8,128)S(1)}, u32[]{:S(2)}, u32[]{:S(2)}) %collective-permute-start.17) | collective-permute-done | bytes 4128 | tf_op jit(solution)/shard_map/ppermute | solution.py:49
  89.2 3.5 %flatten.2 = f32[16,36864]{1,0:T(8,128)} custom-call(s32[2]{0:T(128)} %pad_add_fusion.place_ref, f32[2,8,192,192]{3,2,1,0:T(8,128)} %get-tuple-element.48.square_ref), custom_call_target="tpu_custom_call" | custom-call | flops 20000000 | bytes 3000000 | tf_op jit(solution)/shard_map/flatten/pallas_call | solution.py:134
  93.2 1.1 %bitcast_dynamic-update-slice_fusion = f32[1,16,36864]{2,1,0:T(8,128)} fusion(f32[1,16,36864]{2,1,0:T(8,128)} %bitcast.28, s32[]{:T(128)S(6)} %select_n.154, f32[8,36864]{1,0:T(8,128)S(1)} %collective-permute-done.10), kind=kLoop, calls=%fused_computation.5 | loop fusion | bytes 2359300 | tf_op jit(solution)/shard_map/dynamic_update_slice | solution.py:472
  (86 shorter events, 26.5 us)
Async XLA Ops:
  1.6 5.3 %collective-permute-start.2 = (bf16[8,4608]{1,0:T(8,128)(2,1)S(1)}, bf16[8,4608]{1,0:T(8,128)(2,1)S(1)}, u32[]{:S(2)}, u32[]{:S(2)}) collective-permute-start(bf16[8,4608]{1,0:T(8,128)(2,1)S(1)} %constant_dynamic-slice_fusion), channel_id=1, source_target_pairs={{0,3},{1,0},{2,1},{3,2},{4,7},{5,4},{6,5},{7,6},{8,11},{9,8},{10,9... | collective-permute-start | bytes 221192 | tf_op jit(solution)/shard_map/ppermute | solution.py:38
  4.7 5.9 %collective-permute-start.1 = (bf16[8,4608]{1,0:T(8,128)(2,1)S(1)}, bf16[8,4608]{1,0:T(8,128)(2,1)S(1)}, u32[]{:S(2)}, u32[]{:S(2)}) collective-permute-start(bf16[8,4608]{1,0:T(8,128)(2,1)S(1)} %constant_dynamic-slice_fusion), channel_id=1, source_target_pairs={{0,2},{1,3},{2,0},{3,1},{4,6},{5,7},{6,4},{7,5},{8,10},{9,11},{10,... | collective-permute-start | bytes 221192 | tf_op jit(solution)/shard_map/ppermute | solution.py:38
  5.3 6.0 %collective-permute-start = (bf16[8,4608]{1,0:T(8,128)(2,1)S(1)}, bf16[8,4608]{1,0:T(8,128)(2,1)S(1)}, u32[]{:S(2)}, u32[]{:S(2)}) collective-permute-start(bf16[8,4608]{1,0:T(8,128)(2,1)S(1)} %constant_dynamic-slice_fusion), channel_id=1, source_target_pairs={{0,1},{1,2},{2,3},{3,0},{4,5},{5,6},{6,7},{7,4},{8,9},{9,10},{10,1... | collective-permute-start | bytes 221192 | tf_op jit(solution)/shard_map/ppermute | solution.py:38
  6.3 29.1 %copy-start.1 = (s32[512]{0:T(512)S(1)}, s32[512]{0:T(512)}, u32[]{:S(2)}) copy-start(s32[512]{0:T(512)} %param.10) | copy-start | bytes 6148
  11.3 11.5 %collective-permute-start.5 = (bf16[32,4608]{1,0:T(8,128)(2,1)S(1)}, bf16[32,4608]{1,0:T(8,128)(2,1)S(1)}, u32[]{:S(2)}, u32[]{:S(2)}) collective-permute-start(bf16[32,4608]{1,0:T(8,128)(2,1)S(1)} %pad_maximum_fusion.b0), channel_id=1, source_target_pairs={{0,12},{1,13},{2,14},{3,15},{4,0},{5,1},{6,2},{7,3},{8,4},{9,5},{1... | collective-permute-start | bytes 884744 | tf_op jit(solution)/shard_map/ppermute | solution.py:38
  15.5 8.3 %collective-permute-start.4 = (bf16[32,4608]{1,0:T(8,128)(2,1)S(1)}, bf16[32,4608]{1,0:T(8,128)(2,1)S(1)}, u32[]{:S(2)}, u32[]{:S(2)}) collective-permute-start(bf16[32,4608]{1,0:T(8,128)(2,1)S(1)} %pad_maximum_fusion.b0), channel_id=1, source_target_pairs={{0,8},{1,9},{2,10},{3,11},{4,12},{5,13},{6,14},{7,15},{8,0},{9,1},... | collective-permute-start | bytes 884744 | tf_op jit(solution)/shard_map/ppermute | solution.py:38
  15.5 11.1 %collective-permute-start.3 = (bf16[32,4608]{1,0:T(8,128)(2,1)S(1)}, bf16[32,4608]{1,0:T(8,128)(2,1)S(1)}, u32[]{:S(2)}, u32[]{:S(2)}) collective-permute-start(bf16[32,4608]{1,0:T(8,128)(2,1)S(1)} %pad_maximum_fusion.b0), channel_id=1, source_target_pairs={{0,4},{1,5},{2,6},{3,7},{4,8},{5,9},{6,10},{7,11},{8,12},{9,13},{1... | collective-permute-start | bytes 884744 | tf_op jit(solution)/shard_map/ppermute | solution.py:38
  18.2 18.6 %copy-start.3 = (f32[36864]{0:T(1024)S(1)}, f32[36864]{0:T(1024)}, u32[]{:S(2)}) copy-start(f32[36864]{0:T(1024)} %param.13) | copy-start | bytes 442372
  28.8 13.1 %copy-start.2 = (f32[16,4608]{1,0:T(8,128)S(1)}, f32[16,4608]{1,0:T(8,128)}, u32[]{:S(2)}) copy-start(f32[16,4608]{1,0:T(8,128)} %get-tuple-element.31) | copy-start | bytes 884740
  30.8 9.5 %collective-permute-start.8 = (f16[16,4608]{1,0:T(8,128)(2,1)S(1)}, f16[16,4608]{1,0:T(8,128)(2,1)S(1)}, u32[]{:S(2)}, u32[]{:S(2)}) collective-permute-start(f16[16,4608]{1,0:T(8,128)(2,1)S(1)} %convert_element_type.33), channel_id=1, source_target_pairs={{0,48},{1,49},{2,50},{3,51},{4,52},{5,53},{6,54},{7,55},{8,56},{9,... | collective-permute-start | bytes 442376 | tf_op jit(solution)/shard_map/ppermute | solution.py:38
  33.7 6.7 %collective-permute-start.7 = (f16[16,4608]{1,0:T(8,128)(2,1)S(1)}, f16[16,4608]{1,0:T(8,128)(2,1)S(1)}, u32[]{:S(2)}, u32[]{:S(2)}) collective-permute-start(f16[16,4608]{1,0:T(8,128)(2,1)S(1)} %convert_element_type.32), channel_id=1, source_target_pairs={{0,32},{1,33},{2,34},{3,35},{4,36},{5,37},{6,38},{7,39},{8,40},{9,... | collective-permute-start | bytes 442376 | tf_op jit(solution)/shard_map/ppermute | solution.py:38
  34.5 7.4 %collective-permute-start.6 = (f16[16,4608]{1,0:T(8,128)(2,1)S(1)}, f16[16,4608]{1,0:T(8,128)(2,1)S(1)}, u32[]{:S(2)}, u32[]{:S(2)}) collective-permute-start(f16[16,4608]{1,0:T(8,128)(2,1)S(1)} %convert_element_type.31), channel_id=1, source_target_pairs={{0,16},{1,17},{2,18},{3,19},{4,20},{5,21},{6,22},{7,23},{8,24},{9,... | collective-permute-start | bytes 442376 | tf_op jit(solution)/shard_map/ppermute | solution.py:38
  42.6 1.4 %collective-permute-start.9 = (f32[8,4608]{1,0:T(8,128)S(1)}, f32[8,4608]{1,0:T(8,128)S(1)}, u32[]{:S(2)}, u32[]{:S(2)}) collective-permute-start(f32[8,4608]{1,0:T(8,128)S(1)} %get-tuple-element.58), channel_id=1, source_target_pairs={{0,64},{64,0},{1,65},{65,1},{2,66},{66,2},{3,67},{67,3},{4,68},{68... | collective-permute-start | bytes 442376 | tf_op jit(solution)/shard_map/ppermute | solution.py:53
  66.9 26.2 %collective-permute-start.10 = (f32[8,36864]{1,0:T(8,128)}, f32[8,36864]{1,0:T(8,128)S(1)}, u32[]{:S(2)}, u32[]{:S(2)}) collective-permute-start(f32[8,36864]{1,0:T(8,128)} %flatten.3), channel_id=1, source_target_pairs={{0,64},{64,0},{1,65},{65,1},{2,66},{66,2},{3,67},{67,3},{4,68},{68... | collective-permute-start | bytes 3538952 | tf_op jit(solution)/shard_map/ppermute | solution.py:53
  67.1 3.6 %collective-permute-start.13 = (f32[8,128]{1,0:T(8,128)S(1)}, f32[8,128]{1,0:T(8,128)S(1)}, u32[]{:S(2)}, u32[]{:S(2)}) collective-permute-start(f32[8,128]{1,0:T(8,128)S(1)} %copy-done.4), channel_id=1, source_target_pairs={{0,48},{16,0},{32,16},{48,32},{1,49},{17,1},{33,17},{49,33},{2,50}... | collective-permute-start | bytes 12296 | tf_op jit(solution)/shard_map/ppermute | solution.py:49
  67.9 4.8 %collective-permute-start.12 = (f32[8,128]{1,0:T(8,128)S(1)}, f32[8,128]{1,0:T(8,128)S(1)}, u32[]{:S(2)}, u32[]{:S(2)}) collective-permute-start(f32[8,128]{1,0:T(8,128)S(1)} %copy-done.4), channel_id=1, source_target_pairs={{0,16},{16,32},{32,48},{48,0},{1,17},{17,33},{33,49},{49,1},{2,18}... | collective-permute-start | bytes 12296 | tf_op jit(solution)/shard_map/ppermute | solution.py:49
  69.1 5.1 %collective-permute-start.11 = (f32[8,128]{1,0:T(8,128)S(1)}, f32[8,128]{1,0:T(8,128)S(1)}, u32[]{:S(2)}, u32[]{:S(2)}) collective-permute-start(f32[8,128]{1,0:T(8,128)S(1)} %copy-done.4), channel_id=1, source_target_pairs={{0,32},{16,48},{32,0},{48,16},{1,33},{17,49},{33,1},{49,17},{2,34}... | collective-permute-start | bytes 12296 | tf_op jit(solution)/shard_map/ppermute | solution.py:49
  74.2 3.6 %collective-permute-start.16 = (f32[8,128]{1,0:T(8,128)S(1)}, f32[8,128]{1,0:T(8,128)S(1)}, u32[]{:S(2)}, u32[]{:S(2)}) collective-permute-start(f32[8,128]{1,0:T(8,128)S(1)} %add_add_fusion.4), channel_id=1, source_target_pairs={{0,12},{4,0},{8,4},{12,8},{1,13},{5,1},{9,5},{13,9},{2,14},{6,2},{... | collective-permute-start | bytes 12296 | tf_op jit(solution)/shard_map/ppermute | solution.py:49
  75.1 4.8 %collective-permute-start.15 = (f32[8,128]{1,0:T(8,128)S(1)}, f32[8,128]{1,0:T(8,128)S(1)}, u32[]{:S(2)}, u32[]{:S(2)}) collective-permute-start(f32[8,128]{1,0:T(8,128)S(1)} %add_add_fusion.4), channel_id=1, source_target_pairs={{0,4},{4,8},{8,12},{12,0},{1,5},{5,9},{9,13},{13,1},{2,6},{6,10},{... | collective-permute-start | bytes 12296 | tf_op jit(solution)/shard_map/ppermute | solution.py:49
  76.2 5.1 %collective-permute-start.14 = (f32[8,128]{1,0:T(8,128)S(1)}, f32[8,128]{1,0:T(8,128)S(1)}, u32[]{:S(2)}, u32[]{:S(2)}) collective-permute-start(f32[8,128]{1,0:T(8,128)S(1)} %add_add_fusion.4), channel_id=1, source_target_pairs={{0,8},{4,12},{8,0},{12,4},{1,9},{5,13},{9,1},{13,5},{2,10},{6,14},... | collective-permute-start | bytes 12296 | tf_op jit(solution)/shard_map/ppermute | solution.py:49
  81.4 3.6 %collective-permute-start.19 = (f32[8,128]{1,0:T(8,128)S(1)}, f32[8,128]{1,0:T(8,128)S(1)}, u32[]{:S(2)}, u32[]{:S(2)}) collective-permute-start(f32[8,128]{1,0:T(8,128)S(1)} %add_add_fusion.3), channel_id=1, source_target_pairs={{0,3},{1,0},{2,1},{3,2},{4,7},{5,4},{6,5},{7,6},{8,11},{9,8},{10,9... | collective-permute-start | bytes 12296 | tf_op jit(solution)/shard_map/ppermute | solution.py:49
  81.9 4.8 %collective-permute-start.18 = (f32[8,128]{1,0:T(8,128)S(1)}, f32[8,128]{1,0:T(8,128)S(1)}, u32[]{:S(2)}, u32[]{:S(2)}) collective-permute-start(f32[8,128]{1,0:T(8,128)S(1)} %add_add_fusion.3), channel_id=1, source_target_pairs={{0,1},{1,2},{2,3},{3,0},{4,5},{5,6},{6,7},{7,4},{8,9},{9,10},{10,1... | collective-permute-start | bytes 12296 | tf_op jit(solution)/shard_map/ppermute | solution.py:49
  83.4 5.1 %collective-permute-start.17 = (f32[8,128]{1,0:T(8,128)S(1)}, f32[8,128]{1,0:T(8,128)S(1)}, u32[]{:S(2)}, u32[]{:S(2)}) collective-permute-start(f32[8,128]{1,0:T(8,128)S(1)} %add_add_fusion.3), channel_id=1, source_target_pairs={{0,2},{1,3},{2,0},{3,1},{4,6},{5,7},{6,4},{7,5},{8,10},{9,11},{10,... | collective-permute-start | bytes 12296 | tf_op jit(solution)/shard_map/ppermute | solution.py:49
  88.5 4.1 %collective-permute-start.20 = (f32[8,128]{1,0:T(8,128)S(1)}, f32[8,128]{1,0:T(8,128)S(1)}, u32[]{:S(2)}, u32[]{:S(2)}) collective-permute-start(f32[8,128]{1,0:T(8,128)S(1)} %add_add_fusion.2), channel_id=1, source_target_pairs={{0,64},{64,0},{1,65},{65,1},{2,66},{66,2},{3,67},{67,3},{4,68},{68... | collective-permute-start | bytes 12296 | tf_op jit(solution)/shard_map/ppermute | solution.py:53
  (3 other events, 5.2 us)

commit v3 on v1

--- a/solution.py
+++ b/solution.py
@@ -9,7 +9,7 @@
 
 PURIFY = 8
 MIB = 1024 * 1024
-SINGLE = (8, 4)
+SINGLE = (8, 5)
 GRP = ("grp_0", "grp_1", "grp_2")
 ALL = ("segment", "grp_0", "grp_1", "grp_2")
 STRIDES = ((1, 4, 16), (4, 16, 1))
@@ -163,7 +163,7 @@
     return pl.pallas_call(
         partial_kernel,
         name="partial_fields",
-        out_shape=[pltpu.HBM((16, HALF), f32)] * 4,
+        out_shape=[pltpu.HBM((16, HALF), f32)] + [pltpu.VMEM((16, HALF), f32)] * 3,
         compiler_params=pltpu.CompilerParams(vmem_limit_bytes=12 * MIB),
         cost_estimate=pl.CostEstimate(flops=80000000, bytes_accessed=2400000, transcendentals=0),
     )(weights, *blocks)
@@ -325,7 +325,7 @@
         if singles > 0:
             lax.fori_loop(0, singles, single, 0)
         if singles < PURIFY:
-            lax.fori_loop(singles, PURIFY, triple, 0)
+            lax.fori_loop(singles, PURIFY, triple, 0, unroll=True)
 
     start(masked, jnp.zeros((LOCAL, BD), f32))
     purify(SINGLE[0])
@@ -347,7 +347,7 @@
         leaving[-1].start()
         both = with_diagonal(masked[d] + offset[d], extra[d : d + 1, :])
         diagonal[d : d + 1, :] = jnp.sum(solved * both, axis=0, keepdims=True)
-    energy = jnp.sum(diagonal[...], axis=1, keepdims=True) * (0.5 / count)
+    energy = jnp.sum(diagonal[...], axis=1, keepdims=True) * (0.5 / (1024.0 * count))
     energy_out[...] = jnp.broadcast_to(jnp.sum(energy, axis=0, keepdims=True), (8, 128))
     for copy in leaving:
         copy.wait()
@@ -363,7 +363,7 @@
         out_specs=[pl.BlockSpec(memory_space=pltpu.HBM), vmem],
         out_shape=[
             jax.ShapeDtypeStruct((2,) + square, f32),
-            jax.ShapeDtypeStruct((8, 128), f32),
+            pltpu.VMEM((8, 128), f32),
         ],
         scratch_shapes=[
             pltpu.VMEM((LOCAL, 2), jnp.int32),
@@ -460,7 +460,7 @@
         one, two, three = shifts(axis_shift, energy, axis)
         energy = (energy + two) + (one + three)
     energy = energy + swap_cores(energy)
-    window_energy = energy[0, 0] / 1024.0
+    window_energy = energy[0, 0]
 
     sent = flatten(jnp.stack([1 - segment, 0 * segment]).astype(jnp.int32), stack, LOCAL)
     arrived = swap_cores(sent)

time: 97.2 us -> 92.8 us (0.955)
  Pallas kernels: 30.4 us -> 28.1 us
  between operations: 2.63 us -> 0.83 us
    pallas_call x1, Pallas kernels: 19.4 us -> 17.4 us  [solve(): pl.pallas_call(solve_kernel, name='solve', in_specs=[pl.BlockSpec(memory_...]
  transfers between devices with their start and end apart: 21 -> 21, of which waited for: 15 -> 15; matrix products, arithmetic and copies ran while one was open for 10% -> 11% of each run, Pallas kernels for 7% -> 7%
where the time goes in v3:
time: 92.8 us; the launch traced here: 91.1 us
  Pallas kernels  28.1 us (30%)
  starting transfers between devices  26.6 us (29%)
  waiting for transfers between devices  22.6 us (24%)
  local copies, waits for them, and re-layouts  10.5 us (11%)
  other arithmetic  2.45 us (3%)
    pallas_call x1, Pallas kernels, solve(): pl.pallas_call(solve_kernel, name='solve', in_specs=[pl.BlockSpec(memory_...  17.4 us
    ppermute x9, starting transfers between devices, phase_shift(): return lax.ppermute(value, ALL, pairs)  15.7 us
    ppermute x9, waiting for transfers between devices, axis_shift(): return lax.ppermute(value, axis, [(i, (i + step) % 4) for i in range(4)])  11.3 us
    ppermute x9, starting transfers between devices, axis_shift(): return lax.ppermute(value, axis, [(i, (i + step) % 4) for i in range(4)])  10.7 us
    ppermute x9, waiting for transfers between devices, phase_shift(): return lax.ppermute(value, ALL, pairs)  10.6 us
    pallas_call x2, Pallas kernels, flatten(): pl.pallas_call(flatten_kernel, name='flatten', grid_spec=pltpu.PrefetchSc...  6.95 us
    pallas_call x1, Pallas kernels, unflatten(): pl.pallas_call(unflatten_kernel, name='unflatten', grid_spec=pltpu.Prefet...  2.74 us
  transfers between devices with their start and end apart: 21, of which 15 were waited for; matrix products, arithmetic and copies ran while one was open for 11% of the time, Pallas kernels for 7%

profile of v3, /device:TPU:0, one launch (start us, length us, event | category | flops | bytes accessed | tf_op | source)
XLA Modules:
  0.0 91.1 jit_solution(14088090282625657405)
XLA Ops:
  1.6 3.1 %collective-permute-start.2 = (bf16[8,4608]{1,0:T(8,128)(2,1)S(1)}, bf16[8,4608]{1,0:T(8,128)(2,1)S(1)}, u32[]{:S(2)}, u32[]{:S(2)}) collective-permute-start(bf16[8,4608]{1,0:T(8,128)(2,1)S(1)} %constant_dynamic-slice_fusion), channel_id=1, source_target_pairs={{0,3},{1,0},{2,1},{3,2},{4,7},{5,4},{6,5},{7,6},{8,11},{9,8},{10,9... | collective-permute-start | bytes 221192 | tf_op jit(solution)/shard_map/ppermute | solution.py:38
  6.9 3.7 %collective-permute-done.1 = bf16[8,4608]{1,0:T(8,128)(2,1)S(1)} collective-permute-done((bf16[8,4608]{1,0:T(8,128)(2,1)S(1)}, bf16[8,4608]{1,0:T(8,128)(2,1)S(1)}, u32[]{:S(2)}, u32[]{:S(2)}) %collective-permute-start.1) | collective-permute-done | bytes 73760 | tf_op jit(solution)/shard_map/ppermute | solution.py:38
  11.4 4.1 %collective-permute-start.5 = (bf16[32,4608]{1,0:T(8,128)(2,1)S(1)}, bf16[32,4608]{1,0:T(8,128)(2,1)S(1)}, u32[]{:S(2)}, u32[]{:S(2)}) collective-permute-start(bf16[32,4608]{1,0:T(8,128)(2,1)S(1)} %pad_maximum_fusion.b0), channel_id=1, source_target_pairs={{0,12},{1,13},{2,14},{3,15},{4,0},{5,1},{6,2},{7,3},{8,4},{9,5},{1... | collective-permute-start | bytes 884744 | tf_op jit(solution)/shard_map/ppermute | solution.py:38
  15.5 1.3 %collective-permute-start.3 = (bf16[32,4608]{1,0:T(8,128)(2,1)S(1)}, bf16[32,4608]{1,0:T(8,128)(2,1)S(1)}, u32[]{:S(2)}, u32[]{:S(2)}) collective-permute-start(bf16[32,4608]{1,0:T(8,128)(2,1)S(1)} %pad_maximum_fusion.b0), channel_id=1, source_target_pairs={{0,4},{1,5},{2,6},{3,7},{4,8},{5,9},{6,10},{7,11},{8,12},{9,13},{1... | collective-permute-start | bytes 884744 | tf_op jit(solution)/shard_map/ppermute | solution.py:38
  23.8 2.8 %collective-permute-done.3.b1 = bf16[32,4608]{1,0:T(8,128)(2,1)S(1)} collective-permute-done((bf16[32,4608]{1,0:T(8,128)(2,1)S(1)}, bf16[32,4608]{1,0:T(8,128)(2,1)S(1)}, u32[]{:S(2)}, u32[]{:S(2)}) %collective-permute-start.3) | collective-permute-done | bytes 294944 | tf_op jit(solution)/shard_map/ppermute | solution.py:38
  27.6 1.5 %collective-permute-start.6 = (f32[16,4608]{1,0:T(8,128)S(1)}, f32[16,4608]{1,0:T(8,128)S(1)}, u32[]{:S(2)}, u32[]{:S(2)}) collective-permute-start(f32[16,4608]{1,0:T(8,128)S(1)} %get-tuple-element.28), channel_id=1, source_target_pairs={{0,16},{1,17},{2,18},{3,19},{4,20},{5,21},{6,22},{7,23},{8,24},{9,... | collective-permute-start | bytes 884744 | tf_op jit(solution)/shard_map/ppermute | solution.py:38
  29.1 2.7 %collective-permute-start.7 = (f32[16,4608]{1,0:T(8,128)S(1)}, f32[16,4608]{1,0:T(8,128)S(1)}, u32[]{:S(2)}, u32[]{:S(2)}) collective-permute-start(f32[16,4608]{1,0:T(8,128)S(1)} %get-tuple-element.29), channel_id=1, source_target_pairs={{0,32},{1,33},{2,34},{3,35},{4,36},{5,37},{6,38},{7,39},{8,40},{9,... | collective-permute-start | bytes 884744 | tf_op jit(solution)/shard_map/ppermute | solution.py:38
  31.8 1.4 %collective-permute-start.8 = (f32[16,4608]{1,0:T(8,128)S(1)}, f32[16,4608]{1,0:T(8,128)S(1)}, u32[]{:S(2)}, u32[]{:S(2)}) collective-permute-start(f32[16,4608]{1,0:T(8,128)S(1)} %get-tuple-element.30), channel_id=1, source_target_pairs={{0,48},{1,49},{2,50},{3,51},{4,52},{5,53},{6,54},{7,55},{8,56},{9,... | collective-permute-start | bytes 884744 | tf_op jit(solution)/shard_map/ppermute | solution.py:38
  35.4 2.7 %unflatten.1 = (f32[1536,128]{1,0:T(8,128)}, f32[1536,128]{1,0:T(8,128)}, f32[96,192]{1,0:T(8,128)}) custom-call(s32[1]{0:T(128)} %bitcast.segment_ref, f32[16,36864]{1,0:T(8,128)} %core_ref, f32[96,192]{1,0:T(8,128)} %esp_any), custom_call_target="tpu_custom_call" | custom-call | flops 20000000 | bytes 3000000 | tf_op jit(solution)/shard_map/unflatten/pallas_call | solution.py:97
  38.2 1.5 %collective-permute-done.7 = f32[16,4608]{1,0:T(8,128)S(1)} collective-permute-done((f32[16,4608]{1,0:T(8,128)S(1)}, f32[16,4608]{1,0:T(8,128)S(1)}, u32[]{:S(2)}, u32[]{:S(2)}) %collective-permute-start.7) | collective-permute-done | bytes 294944 | tf_op jit(solution)/shard_map/ppermute | solution.py:38
  42.4 17.4 %solve.1 = (f32[2,8,192,192]{3,2,1,0:T(8,128)}, f32[8,128]{1,0:T(8,128)S(1)}) custom-call(s32[8,2]{1,0:T(8,128)} %bitcast.32, f32[8,4608]{1,0:T(8,128)} %get-tuple-element.59.mine_any, f32[8,4608]{1,0:T(8,128)} %copy-done.4, f32[1536,128]{1,0:T(8,128)} %get-tuple-element.43.first_any, f32[1536,128]{1,0:T(8,128)} %get-tuple-element.44.second_any, ...), custom_call_target="tpu_custom_call" | custom-call | flops 11000000512 | bytes 6000000 | tf_op jit(solution)/shard_map/solve/pallas_call | solution.py:359
  59.8 3.5 %flatten.3 = f32[8,36864]{1,0:T(8,128)} custom-call(s32[2]{0:T(128)} %pad_add_fusion.1.place_ref, f32[2,8,192,192]{3,2,1,0:T(8,128)} %get-tuple-element.48.square_ref), custom_call_target="tpu_custom_call" | custom-call | flops 20000000 | bytes 3000000 | tf_op jit(solution)/shard_map/flatten/pallas_call | solution.py:134
  63.5 2.5 %collective-permute-start.13 = (f32[8,128]{1,0:T(8,128)S(1)}, f32[8,128]{1,0:T(8,128)S(1)}, u32[]{:S(2)}, u32[]{:S(2)}) collective-permute-start(f32[8,128]{1,0:T(8,128)S(1)} %get-tuple-element.49), channel_id=1, source_target_pairs={{0,48},{16,0},{32,16},{48,32},{1,49},{17,1},{33,17},{49,33},{2,50}... | collective-permute-start | bytes 12296 | tf_op jit(solution)/shard_map/ppermute | solution.py:49
  66.0 2.4 %collective-permute-start.11 = (f32[8,128]{1,0:T(8,128)S(1)}, f32[8,128]{1,0:T(8,128)S(1)}, u32[]{:S(2)}, u32[]{:S(2)}) collective-permute-start(f32[8,128]{1,0:T(8,128)S(1)} %get-tuple-element.49), channel_id=1, source_target_pairs={{0,32},{16,48},{32,0},{48,16},{1,33},{17,49},{33,1},{49,17},{2,34}... | collective-permute-start | bytes 12296 | tf_op jit(solution)/shard_map/ppermute | solution.py:49
  68.4 2.4 %collective-permute-done.12 = f32[8,128]{1,0:T(8,128)S(1)} collective-permute-done((f32[8,128]{1,0:T(8,128)S(1)}, f32[8,128]{1,0:T(8,128)S(1)}, u32[]{:S(2)}, u32[]{:S(2)}) %collective-permute-start.12) | collective-permute-done | bytes 4128 | tf_op jit(solution)/shard_map/ppermute | solution.py:49
  72.0 1.1 %collective-permute-start.15 = (f32[8,128]{1,0:T(8,128)S(1)}, f32[8,128]{1,0:T(8,128)S(1)}, u32[]{:S(2)}, u32[]{:S(2)}) collective-permute-start(f32[8,128]{1,0:T(8,128)S(1)} %add_add_fusion.4), channel_id=1, source_target_pairs={{0,4},{4,8},{8,12},{12,0},{1,5},{5,9},{9,13},{13,1},{2,6},{6,10},{... | collective-permute-start | bytes 12296 | tf_op jit(solution)/shard_map/ppermute | solution.py:49
  73.6 1.2 %collective-permute-done.16 = f32[8,128]{1,0:T(8,128)S(1)} collective-permute-done((f32[8,128]{1,0:T(8,128)S(1)}, f32[8,128]{1,0:T(8,128)S(1)}, u32[]{:S(2)}, u32[]{:S(2)}) %collective-permute-start.16) | collective-permute-done | bytes 4128 | tf_op jit(solution)/shard_map/ppermute | solution.py:49
  74.7 2.1 %collective-permute-done.15 = f32[8,128]{1,0:T(8,128)S(1)} collective-permute-done((f32[8,128]{1,0:T(8,128)S(1)}, f32[8,128]{1,0:T(8,128)S(1)}, u32[]{:S(2)}, u32[]{:S(2)}) %collective-permute-start.15) | collective-permute-done | bytes 4128 | tf_op jit(solution)/shard_map/ppermute | solution.py:49
  76.8 1.4 %collective-permute-done.14 = f32[8,128]{1,0:T(8,128)S(1)} collective-permute-done((f32[8,128]{1,0:T(8,128)S(1)}, f32[8,128]{1,0:T(8,128)S(1)}, u32[]{:S(2)}, u32[]{:S(2)}) %collective-permute-start.14) | collective-permute-done | bytes 4128 | tf_op jit(solution)/shard_map/ppermute | solution.py:49
  78.8 1.5 %collective-permute-start.18 = (f32[8,128]{1,0:T(8,128)S(1)}, f32[8,128]{1,0:T(8,128)S(1)}, u32[]{:S(2)}, u32[]{:S(2)}) collective-permute-start(f32[8,128]{1,0:T(8,128)S(1)} %add_add_fusion.3), channel_id=1, source_target_pairs={{0,1},{1,2},{2,3},{3,0},{4,5},{5,6},{6,7},{7,4},{8,9},{9,10},{10,1... | collective-permute-start | bytes 12296 | tf_op jit(solution)/shard_map/ppermute | solution.py:49
  80.3 1.2 %collective-permute-start.17 = (f32[8,128]{1,0:T(8,128)S(1)}, f32[8,128]{1,0:T(8,128)S(1)}, u32[]{:S(2)}, u32[]{:S(2)}) collective-permute-start(f32[8,128]{1,0:T(8,128)S(1)} %add_add_fusion.3), channel_id=1, source_target_pairs={{0,2},{1,3},{2,0},{3,1},{4,6},{5,7},{6,4},{7,5},{8,10},{9,11},{10,... | collective-permute-start | bytes 12296 | tf_op jit(solution)/shard_map/ppermute | solution.py:49
  81.9 1.8 %collective-permute-done.18 = f32[8,128]{1,0:T(8,128)S(1)} collective-permute-done((f32[8,128]{1,0:T(8,128)S(1)}, f32[8,128]{1,0:T(8,128)S(1)}, u32[]{:S(2)}, u32[]{:S(2)}) %collective-permute-start.18) | collective-permute-done | bytes 4128 | tf_op jit(solution)/shard_map/ppermute | solution.py:49
  83.7 1.8 %collective-permute-done.17 = f32[8,128]{1,0:T(8,128)S(1)} collective-permute-done((f32[8,128]{1,0:T(8,128)S(1)}, f32[8,128]{1,0:T(8,128)S(1)}, u32[]{:S(2)}, u32[]{:S(2)}) %collective-permute-start.17) | collective-permute-done | bytes 4128 | tf_op jit(solution)/shard_map/ppermute | solution.py:49
  86.0 3.5 %flatten.2 = f32[16,36864]{1,0:T(8,128)} custom-call(s32[2]{0:T(128)} %pad_add_fusion.place_ref, f32[2,8,192,192]{3,2,1,0:T(8,128)} %get-tuple-element.48.square_ref), custom_call_target="tpu_custom_call" | custom-call | flops 20000000 | bytes 3000000 | tf_op jit(solution)/shard_map/flatten/pallas_call | solution.py:134
  (81 shorter events, 21.7 us)
Async XLA Ops:
  0.6 34.0 %copy-start.3 = (f32[36864]{0:T(1024)S(1)}, f32[36864]{0:T(1024)}, u32[]{:S(2)}) copy-start(f32[36864]{0:T(1024)} %param.13) | copy-start | bytes 442372
  0.7 32.6 %copy-start.1 = (s32[512]{0:T(512)S(1)}, s32[512]{0:T(512)}, u32[]{:S(2)}) copy-start(s32[512]{0:T(512)} %param.10) | copy-start | bytes 6148
  1.6 5.3 %collective-permute-start.2 = (bf16[8,4608]{1,0:T(8,128)(2,1)S(1)}, bf16[8,4608]{1,0:T(8,128)(2,1)S(1)}, u32[]{:S(2)}, u32[]{:S(2)}) collective-permute-start(bf16[8,4608]{1,0:T(8,128)(2,1)S(1)} %constant_dynamic-slice_fusion), channel_id=1, source_target_pairs={{0,3},{1,0},{2,1},{3,2},{4,7},{5,4},{6,5},{7,6},{8,11},{9,8},{10,9... | collective-permute-start | bytes 221192 | tf_op jit(solution)/shard_map/ppermute | solution.py:38
  4.7 5.9 %collective-permute-start.1 = (bf16[8,4608]{1,0:T(8,128)(2,1)S(1)}, bf16[8,4608]{1,0:T(8,128)(2,1)S(1)}, u32[]{:S(2)}, u32[]{:S(2)}) collective-permute-start(bf16[8,4608]{1,0:T(8,128)(2,1)S(1)} %constant_dynamic-slice_fusion), channel_id=1, source_target_pairs={{0,2},{1,3},{2,0},{3,1},{4,6},{5,7},{6,4},{7,5},{8,10},{9,11},{10,... | collective-permute-start | bytes 221192 | tf_op jit(solution)/shard_map/ppermute | solution.py:38
  5.3 6.0 %collective-permute-start = (bf16[8,4608]{1,0:T(8,128)(2,1)S(1)}, bf16[8,4608]{1,0:T(8,128)(2,1)S(1)}, u32[]{:S(2)}, u32[]{:S(2)}) collective-permute-start(bf16[8,4608]{1,0:T(8,128)(2,1)S(1)} %constant_dynamic-slice_fusion), channel_id=1, source_target_pairs={{0,1},{1,2},{2,3},{3,0},{4,5},{5,6},{6,7},{7,4},{8,9},{9,10},{10,1... | collective-permute-start | bytes 221192 | tf_op jit(solution)/shard_map/ppermute | solution.py:38
  11.4 11.5 %collective-permute-start.5 = (bf16[32,4608]{1,0:T(8,128)(2,1)S(1)}, bf16[32,4608]{1,0:T(8,128)(2,1)S(1)}, u32[]{:S(2)}, u32[]{:S(2)}) collective-permute-start(bf16[32,4608]{1,0:T(8,128)(2,1)S(1)} %pad_maximum_fusion.b0), channel_id=1, source_target_pairs={{0,12},{1,13},{2,14},{3,15},{4,0},{5,1},{6,2},{7,3},{8,4},{9,5},{1... | collective-permute-start | bytes 884744 | tf_op jit(solution)/shard_map/ppermute | solution.py:38
  15.5 8.3 %collective-permute-start.4 = (bf16[32,4608]{1,0:T(8,128)(2,1)S(1)}, bf16[32,4608]{1,0:T(8,128)(2,1)S(1)}, u32[]{:S(2)}, u32[]{:S(2)}) collective-permute-start(bf16[32,4608]{1,0:T(8,128)(2,1)S(1)} %pad_maximum_fusion.b0), channel_id=1, source_target_pairs={{0,8},{1,9},{2,10},{3,11},{4,12},{5,13},{6,14},{7,15},{8,0},{9,1},... | collective-permute-start | bytes 884744 | tf_op jit(solution)/shard_map/ppermute | solution.py:38
  15.5 11.1 %collective-permute-start.3 = (bf16[32,4608]{1,0:T(8,128)(2,1)S(1)}, bf16[32,4608]{1,0:T(8,128)(2,1)S(1)}, u32[]{:S(2)}, u32[]{:S(2)}) collective-permute-start(bf16[32,4608]{1,0:T(8,128)(2,1)S(1)} %pad_maximum_fusion.b0), channel_id=1, source_target_pairs={{0,4},{1,5},{2,6},{3,7},{4,8},{5,9},{6,10},{7,11},{8,12},{9,13},{1... | collective-permute-start | bytes 884744 | tf_op jit(solution)/shard_map/ppermute | solution.py:38
  27.6 12.1 %copy-start.2 = (f32[16,4608]{1,0:T(8,128)S(1)}, f32[16,4608]{1,0:T(8,128)}, u32[]{:S(2)}) copy-start(f32[16,4608]{1,0:T(8,128)} %get-tuple-element.31) | copy-start | bytes 884740
  27.6 10.6 %collective-permute-start.6 = (f32[16,4608]{1,0:T(8,128)S(1)}, f32[16,4608]{1,0:T(8,128)S(1)}, u32[]{:S(2)}, u32[]{:S(2)}) collective-permute-start(f32[16,4608]{1,0:T(8,128)S(1)} %get-tuple-element.28), channel_id=1, source_target_pairs={{0,16},{1,17},{2,18},{3,19},{4,20},{5,21},{6,22},{7,23},{8,24},{9,... | collective-permute-start | bytes 884744 | tf_op jit(solution)/shard_map/ppermute | solution.py:38
  29.1 10.6 %collective-permute-start.7 = (f32[16,4608]{1,0:T(8,128)S(1)}, f32[16,4608]{1,0:T(8,128)S(1)}, u32[]{:S(2)}, u32[]{:S(2)}) collective-permute-start(f32[16,4608]{1,0:T(8,128)S(1)} %get-tuple-element.29), channel_id=1, source_target_pairs={{0,32},{1,33},{2,34},{3,35},{4,36},{5,37},{6,38},{7,39},{8,40},{9,... | collective-permute-start | bytes 884744 | tf_op jit(solution)/shard_map/ppermute | solution.py:38
  31.8 7.9 %collective-permute-start.8 = (f32[16,4608]{1,0:T(8,128)S(1)}, f32[16,4608]{1,0:T(8,128)S(1)}, u32[]{:S(2)}, u32[]{:S(2)}) collective-permute-start(f32[16,4608]{1,0:T(8,128)S(1)} %get-tuple-element.30), channel_id=1, source_target_pairs={{0,48},{1,49},{2,50},{3,51},{4,52},{5,53},{6,54},{7,55},{8,56},{9,... | collective-permute-start | bytes 884744 | tf_op jit(solution)/shard_map/ppermute | solution.py:38
  40.4 1.4 %collective-permute-start.9 = (f32[8,4608]{1,0:T(8,128)S(1)}, f32[8,4608]{1,0:T(8,128)S(1)}, u32[]{:S(2)}, u32[]{:S(2)}) collective-permute-start(f32[8,4608]{1,0:T(8,128)S(1)} %get-tuple-element.58), channel_id=1, source_target_pairs={{0,64},{64,0},{1,65},{65,1},{2,66},{66,2},{3,67},{67,3},{4,68},{68... | collective-permute-start | bytes 442376 | tf_op jit(solution)/shard_map/ppermute | solution.py:53
  63.3 26.7 %collective-permute-start.10 = (f32[8,36864]{1,0:T(8,128)}, f32[8,36864]{1,0:T(8,128)S(1)}, u32[]{:S(2)}, u32[]{:S(2)}) collective-permute-start(f32[8,36864]{1,0:T(8,128)} %flatten.3), channel_id=1, source_target_pairs={{0,64},{64,0},{1,65},{65,1},{2,66},{66,2},{3,67},{67,3},{4,68},{68... | collective-permute-start | bytes 3538952 | tf_op jit(solution)/shard_map/ppermute | solution.py:53
  63.5 5.0 %collective-permute-start.13 = (f32[8,128]{1,0:T(8,128)S(1)}, f32[8,128]{1,0:T(8,128)S(1)}, u32[]{:S(2)}, u32[]{:S(2)}) collective-permute-start(f32[8,128]{1,0:T(8,128)S(1)} %get-tuple-element.49), channel_id=1, source_target_pairs={{0,48},{16,0},{32,16},{48,32},{1,49},{17,1},{33,17},{49,33},{2,50}... | collective-permute-start | bytes 12296 | tf_op jit(solution)/shard_map/ppermute | solution.py:49
  66.0 4.8 %collective-permute-start.12 = (f32[8,128]{1,0:T(8,128)S(1)}, f32[8,128]{1,0:T(8,128)S(1)}, u32[]{:S(2)}, u32[]{:S(2)}) collective-permute-start(f32[8,128]{1,0:T(8,128)S(1)} %get-tuple-element.49), channel_id=1, source_target_pairs={{0,16},{16,32},{32,48},{48,0},{1,17},{17,33},{33,49},{49,1},{2,18}... | collective-permute-start | bytes 12296 | tf_op jit(solution)/shard_map/ppermute | solution.py:49
  66.0 5.1 %collective-permute-start.11 = (f32[8,128]{1,0:T(8,128)S(1)}, f32[8,128]{1,0:T(8,128)S(1)}, u32[]{:S(2)}, u32[]{:S(2)}) collective-permute-start(f32[8,128]{1,0:T(8,128)S(1)} %get-tuple-element.49), channel_id=1, source_target_pairs={{0,32},{16,48},{32,0},{48,16},{1,33},{17,49},{33,1},{49,17},{2,34}... | collective-permute-start | bytes 12296 | tf_op jit(solution)/shard_map/ppermute | solution.py:49
  71.1 3.6 %collective-permute-start.16 = (f32[8,128]{1,0:T(8,128)S(1)}, f32[8,128]{1,0:T(8,128)S(1)}, u32[]{:S(2)}, u32[]{:S(2)}) collective-permute-start(f32[8,128]{1,0:T(8,128)S(1)} %add_add_fusion.4), channel_id=1, source_target_pairs={{0,12},{4,0},{8,4},{12,8},{1,13},{5,1},{9,5},{13,9},{2,14},{6,2},{... | collective-permute-start | bytes 12296 | tf_op jit(solution)/shard_map/ppermute | solution.py:49
  72.0 4.8 %collective-permute-start.15 = (f32[8,128]{1,0:T(8,128)S(1)}, f32[8,128]{1,0:T(8,128)S(1)}, u32[]{:S(2)}, u32[]{:S(2)}) collective-permute-start(f32[8,128]{1,0:T(8,128)S(1)} %add_add_fusion.4), channel_id=1, source_target_pairs={{0,4},{4,8},{8,12},{12,0},{1,5},{5,9},{9,13},{13,1},{2,6},{6,10},{... | collective-permute-start | bytes 12296 | tf_op jit(solution)/shard_map/ppermute | solution.py:49
  73.2 5.1 %collective-permute-start.14 = (f32[8,128]{1,0:T(8,128)S(1)}, f32[8,128]{1,0:T(8,128)S(1)}, u32[]{:S(2)}, u32[]{:S(2)}) collective-permute-start(f32[8,128]{1,0:T(8,128)S(1)} %add_add_fusion.4), channel_id=1, source_target_pairs={{0,8},{4,12},{8,0},{12,4},{1,9},{5,13},{9,1},{13,5},{2,10},{6,14},... | collective-permute-start | bytes 12296 | tf_op jit(solution)/shard_map/ppermute | solution.py:49
  78.3 3.6 %collective-permute-start.19 = (f32[8,128]{1,0:T(8,128)S(1)}, f32[8,128]{1,0:T(8,128)S(1)}, u32[]{:S(2)}, u32[]{:S(2)}) collective-permute-start(f32[8,128]{1,0:T(8,128)S(1)} %add_add_fusion.3), channel_id=1, source_target_pairs={{0,3},{1,0},{2,1},{3,2},{4,7},{5,4},{6,5},{7,6},{8,11},{9,8},{10,9... | collective-permute-start | bytes 12296 | tf_op jit(solution)/shard_map/ppermute | solution.py:49
  78.8 4.8 %collective-permute-start.18 = (f32[8,128]{1,0:T(8,128)S(1)}, f32[8,128]{1,0:T(8,128)S(1)}, u32[]{:S(2)}, u32[]{:S(2)}) collective-permute-start(f32[8,128]{1,0:T(8,128)S(1)} %add_add_fusion.3), channel_id=1, source_target_pairs={{0,1},{1,2},{2,3},{3,0},{4,5},{5,6},{6,7},{7,4},{8,9},{9,10},{10,1... | collective-permute-start | bytes 12296 | tf_op jit(solution)/shard_map/ppermute | solution.py:49
  80.3 5.1 %collective-permute-start.17 = (f32[8,128]{1,0:T(8,128)S(1)}, f32[8,128]{1,0:T(8,128)S(1)}, u32[]{:S(2)}, u32[]{:S(2)}) collective-permute-start(f32[8,128]{1,0:T(8,128)S(1)} %add_add_fusion.3), channel_id=1, source_target_pairs={{0,2},{1,3},{2,0},{3,1},{4,6},{5,7},{6,4},{7,5},{8,10},{9,11},{10,... | collective-permute-start | bytes 12296 | tf_op jit(solution)/shard_map/ppermute | solution.py:49
  85.4 4.1 %collective-permute-start.20 = (f32[8,128]{1,0:T(8,128)S(1)}, f32[8,128]{1,0:T(8,128)S(1)}, u32[]{:S(2)}, u32[]{:S(2)}) collective-permute-start(f32[8,128]{1,0:T(8,128)S(1)} %add_add_fusion.2), channel_id=1, source_target_pairs={{0,64},{64,0},{1,65},{65,1},{2,66},{66,2},{3,67},{67,3},{4,68},{68... | collective-permute-start | bytes 12296 | tf_op jit(solution)/shard_map/ppermute | solution.py:53
  (2 other events, 1.6 us)

commit v4 on v3

--- a/solution.py
+++ b/solution.py
@@ -289,7 +289,13 @@
     leaving = [pltpu.make_async_copy(fock, stack.at[0], departures.at[LOCAL])]
     leaving[0].start()
 
-    def start(source, added):
+    def prepare(d, value, exact):
+        if exact:
+            work_h[d], work_l[d] = split_two(value)
+        else:
+            work_h[d] = value.astype(bf16)
+
+    def start(source, added, exact):
         on_diagonal = diagonal[...] + added
         chemical = jnp.sum(on_diagonal, axis=1, keepdims=True) / count
         lowered = chemical * live
@@ -298,36 +304,30 @@
         scale[...] = jnp.broadcast_to(-0.5 / (radius + epsilon), (LOCAL, BD))
         shift[...] = added - lowered
         for d in range(LOCAL):
-            work[d] = with_diagonal(source[d], shift[d : d + 1, :]) * scale[d : d + 1, :]
-
-    def single(_, carry):
-        for d in range(LOCAL):
-            high = work[d].astype(bf16)
-            work_h[d] = high
-            square_h[d] = dot(high, high).astype(bf16)
-        for d in range(LOCAL):
-            work[d] = 1.5 * work[d] - 2.0 * dot(square_h[d], work_h[d])
-        return carry
-
-    def triple(_, carry):
-        for d in range(LOCAL):
-            high, low = split_two(work[d])
-            work_h[d] = high
-            work_l[d] = low
-            squared = dot_three((high, low), (high, low))
-            square_h[d], square_l[d] = split_two(squared)
-        for d in range(LOCAL):
-            cubed = dot_three((square_h[d], square_l[d]), (work_h[d], work_l[d]))
-            work[d] = 1.5 * work[d] - 2.0 * cubed
-        return carry
+            value = with_diagonal(source[d], shift[d : d + 1, :]) * scale[d : d + 1, :]
+            work[d] = value
+            prepare(d, value, exact)
 
     def purify(singles):
-        if singles > 0:
-            lax.fori_loop(0, singles, single, 0)
-        if singles < PURIFY:
-            lax.fori_loop(singles, PURIFY, triple, 0, unroll=True)
-
-    start(masked, jnp.zeros((LOCAL, BD), f32))
+        for step in range(PURIFY):
+            exact, exact_next = step >= singles, step + 1 >= singles
+            for d in range(LOCAL):
+                if exact:
+                    pair = (work_h[d], work_l[d])
+                    square_h[d], square_l[d] = split_two(dot_three(pair, pair))
+                else:
+                    square_h[d] = dot(work_h[d], work_h[d]).astype(bf16)
+            for d in range(LOCAL):
+                if exact:
+                    cubed = dot_three((square_h[d], square_l[d]), (work_h[d], work_l[d]))
+                else:
+                    cubed = dot(square_h[d], work_h[d])
+                value = 1.5 * work[d] - 2.0 * cubed
+                work[d] = value
+                if step + 1 < PURIFY:
+                    prepare(d, value, exact_next)
+
+    start(masked, jnp.zeros((LOCAL, BD), f32), SINGLE[0] == 0)
     purify(SINGLE[0])
     for d in range(LOCAL):
         occupied[d : d + 1, :] = diagonal_of(work[d])
@@ -338,7 +338,7 @@
         changed = masked[d] - half_repulsion * work[d]
         offset[d] = changed
         columns_of(changed, d)
-    start(offset, extra[...])
+    start(offset, extra[...], SINGLE[1] == 0)
     purify(SINGLE[1])
     for d in range(LOCAL):
         solved = with_diagonal(work[d], 0.5 * alive[d : d + 1, :])

time: 92.8 us -> 91 us (0.981)
  Pallas kernels: 28.1 us -> 26.3 us
    pallas_call x1, Pallas kernels: 17.4 us -> 15.7 us  [solve(): pl.pallas_call(solve_kernel, name='solve', in_specs=[pl.BlockSpec(memory_...]
where the time goes in v4:
time: 91 us; the launch traced here: 89.3 us
  starting transfers between devices  26.6 us (29%)
  Pallas kernels  26.3 us (29%)
  waiting for transfers between devices  22.6 us (25%)
  local copies, waits for them, and re-layouts  10.5 us (12%)
  other arithmetic  2.45 us (3%)
    ppermute x9, starting transfers between devices, phase_shift(): return lax.ppermute(value, ALL, pairs)  15.7 us
    pallas_call x1, Pallas kernels, solve(): pl.pallas_call(solve_kernel, name='solve', in_specs=[pl.BlockSpec(memory_...  15.7 us
    ppermute x9, waiting for transfers between devices, axis_shift(): return lax.ppermute(value, axis, [(i, (i + step) % 4) for i in range(4)])  11.3 us
    ppermute x9, starting transfers between devices, axis_shift(): return lax.ppermute(value, axis, [(i, (i + step) % 4) for i in range(4)])  10.7 us
    ppermute x9, waiting for transfers between devices, phase_shift(): return lax.ppermute(value, ALL, pairs)  10.6 us
    pallas_call x2, Pallas kernels, flatten(): pl.pallas_call(flatten_kernel, name='flatten', grid_spec=pltpu.PrefetchSc...  6.95 us
    pallas_call x1, Pallas kernels, unflatten(): pl.pallas_call(unflatten_kernel, name='unflatten', grid_spec=pltpu.Prefet...  2.74 us
  transfers between devices with their start and end apart: 21, of which 15 were waited for; matrix products, arithmetic and copies ran while one was open for 11% of the time, Pallas kernels for 7%

profile of v4, /device:TPU:0, one launch (start us, length us, event | category | flops | bytes accessed | tf_op | source)
XLA Modules:
  0.0 89.3 jit_solution(14912847945779107925)
XLA Ops:
  1.6 3.1 %collective-permute-start.2 = (bf16[8,4608]{1,0:T(8,128)(2,1)S(1)}, bf16[8,4608]{1,0:T(8,128)(2,1)S(1)}, u32[]{:S(2)}, u32[]{:S(2)}) collective-permute-start(bf16[8,4608]{1,0:T(8,128)(2,1)S(1)} %constant_dynamic-slice_fusion), channel_id=1, source_target_pairs={{0,3},{1,0},{2,1},{3,2},{4,7},{5,4},{6,5},{7,6},{8,11},{9,8},{10,9... | collective-permute-start | bytes 221192 | tf_op jit(solution)/shard_map/ppermute | solution.py:38
  6.9 3.7 %collective-permute-done.1 = bf16[8,4608]{1,0:T(8,128)(2,1)S(1)} collective-permute-done((bf16[8,4608]{1,0:T(8,128)(2,1)S(1)}, bf16[8,4608]{1,0:T(8,128)(2,1)S(1)}, u32[]{:S(2)}, u32[]{:S(2)}) %collective-permute-start.1) | collective-permute-done | bytes 73760 | tf_op jit(solution)/shard_map/ppermute | solution.py:38
  11.4 4.1 %collective-permute-start.5 = (bf16[32,4608]{1,0:T(8,128)(2,1)S(1)}, bf16[32,4608]{1,0:T(8,128)(2,1)S(1)}, u32[]{:S(2)}, u32[]{:S(2)}) collective-permute-start(bf16[32,4608]{1,0:T(8,128)(2,1)S(1)} %pad_maximum_fusion.b0), channel_id=1, source_target_pairs={{0,12},{1,13},{2,14},{3,15},{4,0},{5,1},{6,2},{7,3},{8,4},{9,5},{1... | collective-permute-start | bytes 884744 | tf_op jit(solution)/shard_map/ppermute | solution.py:38
  15.5 1.3 %collective-permute-start.3 = (bf16[32,4608]{1,0:T(8,128)(2,1)S(1)}, bf16[32,4608]{1,0:T(8,128)(2,1)S(1)}, u32[]{:S(2)}, u32[]{:S(2)}) collective-permute-start(bf16[32,4608]{1,0:T(8,128)(2,1)S(1)} %pad_maximum_fusion.b0), channel_id=1, source_target_pairs={{0,4},{1,5},{2,6},{3,7},{4,8},{5,9},{6,10},{7,11},{8,12},{9,13},{1... | collective-permute-start | bytes 884744 | tf_op jit(solution)/shard_map/ppermute | solution.py:38
  23.8 2.8 %collective-permute-done.3.b1 = bf16[32,4608]{1,0:T(8,128)(2,1)S(1)} collective-permute-done((bf16[32,4608]{1,0:T(8,128)(2,1)S(1)}, bf16[32,4608]{1,0:T(8,128)(2,1)S(1)}, u32[]{:S(2)}, u32[]{:S(2)}) %collective-permute-start.3) | collective-permute-done | bytes 294944 | tf_op jit(solution)/shard_map/ppermute | solution.py:38
  27.6 1.5 %collective-permute-start.6 = (f32[16,4608]{1,0:T(8,128)S(1)}, f32[16,4608]{1,0:T(8,128)S(1)}, u32[]{:S(2)}, u32[]{:S(2)}) collective-permute-start(f32[16,4608]{1,0:T(8,128)S(1)} %get-tuple-element.28), channel_id=1, source_target_pairs={{0,16},{1,17},{2,18},{3,19},{4,20},{5,21},{6,22},{7,23},{8,24},{9,... | collective-permute-start | bytes 884744 | tf_op jit(solution)/shard_map/ppermute | solution.py:38
  29.1 2.7 %collective-permute-start.7 = (f32[16,4608]{1,0:T(8,128)S(1)}, f32[16,4608]{1,0:T(8,128)S(1)}, u32[]{:S(2)}, u32[]{:S(2)}) collective-permute-start(f32[16,4608]{1,0:T(8,128)S(1)} %get-tuple-element.29), channel_id=1, source_target_pairs={{0,32},{1,33},{2,34},{3,35},{4,36},{5,37},{6,38},{7,39},{8,40},{9,... | collective-permute-start | bytes 884744 | tf_op jit(solution)/shard_map/ppermute | solution.py:38
  31.8 1.4 %collective-permute-start.8 = (f32[16,4608]{1,0:T(8,128)S(1)}, f32[16,4608]{1,0:T(8,128)S(1)}, u32[]{:S(2)}, u32[]{:S(2)}) collective-permute-start(f32[16,4608]{1,0:T(8,128)S(1)} %get-tuple-element.30), channel_id=1, source_target_pairs={{0,48},{1,49},{2,50},{3,51},{4,52},{5,53},{6,54},{7,55},{8,56},{9,... | collective-permute-start | bytes 884744 | tf_op jit(solution)/shard_map/ppermute | solution.py:38
  35.4 2.7 %unflatten.1 = (f32[1536,128]{1,0:T(8,128)}, f32[1536,128]{1,0:T(8,128)}, f32[96,192]{1,0:T(8,128)}) custom-call(s32[1]{0:T(128)} %bitcast.segment_ref, f32[16,36864]{1,0:T(8,128)} %core_ref, f32[96,192]{1,0:T(8,128)} %esp_any), custom_call_target="tpu_custom_call" | custom-call | flops 20000000 | bytes 3000000 | tf_op jit(solution)/shard_map/unflatten/pallas_call | solution.py:97
  38.2 1.5 %collective-permute-done.7 = f32[16,4608]{1,0:T(8,128)S(1)} collective-permute-done((f32[16,4608]{1,0:T(8,128)S(1)}, f32[16,4608]{1,0:T(8,128)S(1)}, u32[]{:S(2)}, u32[]{:S(2)}) %collective-permute-start.7) | collective-permute-done | bytes 294944 | tf_op jit(solution)/shard_map/ppermute | solution.py:38
  42.4 15.7 %solve.1 = (f32[2,8,192,192]{3,2,1,0:T(8,128)}, f32[8,128]{1,0:T(8,128)S(1)}) custom-call(s32[8,2]{1,0:T(8,128)} %bitcast.32, f32[8,4608]{1,0:T(8,128)} %get-tuple-element.59.mine_any, f32[8,4608]{1,0:T(8,128)} %copy-done.4, f32[1536,128]{1,0:T(8,128)} %get-tuple-element.43.first_any, f32[1536,128]{1,0:T(8,128)} %get-tuple-element.44.second_any, ...), custom_call_target="tpu_custom_call" | custom-call | flops 11000000512 | bytes 6000000 | tf_op jit(solution)/shard_map/solve/pallas_call | solution.py:359
  58.1 3.5 %flatten.3 = f32[8,36864]{1,0:T(8,128)} custom-call(s32[2]{0:T(128)} %pad_add_fusion.1.place_ref, f32[2,8,192,192]{3,2,1,0:T(8,128)} %get-tuple-element.48.square_ref), custom_call_target="tpu_custom_call" | custom-call | flops 20000000 | bytes 3000000 | tf_op jit(solution)/shard_map/flatten/pallas_call | solution.py:134
  61.7 2.5 %collective-permute-start.13 = (f32[8,128]{1,0:T(8,128)S(1)}, f32[8,128]{1,0:T(8,128)S(1)}, u32[]{:S(2)}, u32[]{:S(2)}) collective-permute-start(f32[8,128]{1,0:T(8,128)S(1)} %get-tuple-element.49), channel_id=1, source_target_pairs={{0,48},{16,0},{32,16},{48,32},{1,49},{17,1},{33,17},{49,33},{2,50}... | collective-permute-start | bytes 12296 | tf_op jit(solution)/shard_map/ppermute | solution.py:49
  64.2 2.4 %collective-permute-start.11 = (f32[8,128]{1,0:T(8,128)S(1)}, f32[8,128]{1,0:T(8,128)S(1)}, u32[]{:S(2)}, u32[]{:S(2)}) collective-permute-start(f32[8,128]{1,0:T(8,128)S(1)} %get-tuple-element.49), channel_id=1, source_target_pairs={{0,32},{16,48},{32,0},{48,16},{1,33},{17,49},{33,1},{49,17},{2,34}... | collective-permute-start | bytes 12296 | tf_op jit(solution)/shard_map/ppermute | solution.py:49
  66.7 2.4 %collective-permute-done.12 = f32[8,128]{1,0:T(8,128)S(1)} collective-permute-done((f32[8,128]{1,0:T(8,128)S(1)}, f32[8,128]{1,0:T(8,128)S(1)}, u32[]{:S(2)}, u32[]{:S(2)}) %collective-permute-start.12) | collective-permute-done | bytes 4128 | tf_op jit(solution)/shard_map/ppermute | solution.py:49
  70.3 1.1 %collective-permute-start.15 = (f32[8,128]{1,0:T(8,128)S(1)}, f32[8,128]{1,0:T(8,128)S(1)}, u32[]{:S(2)}, u32[]{:S(2)}) collective-permute-start(f32[8,128]{1,0:T(8,128)S(1)} %add_add_fusion.4), channel_id=1, source_target_pairs={{0,4},{4,8},{8,12},{12,0},{1,5},{5,9},{9,13},{13,1},{2,6},{6,10},{... | collective-permute-start | bytes 12296 | tf_op jit(solution)/shard_map/ppermute | solution.py:49
  71.8 1.2 %collective-permute-done.16 = f32[8,128]{1,0:T(8,128)S(1)} collective-permute-done((f32[8,128]{1,0:T(8,128)S(1)}, f32[8,128]{1,0:T(8,128)S(1)}, u32[]{:S(2)}, u32[]{:S(2)}) %collective-permute-start.16) | collective-permute-done | bytes 4128 | tf_op jit(solution)/shard_map/ppermute | solution.py:49
  73.0 2.1 %collective-permute-done.15 = f32[8,128]{1,0:T(8,128)S(1)} collective-permute-done((f32[8,128]{1,0:T(8,128)S(1)}, f32[8,128]{1,0:T(8,128)S(1)}, u32[]{:S(2)}, u32[]{:S(2)}) %collective-permute-start.15) | collective-permute-done | bytes 4128 | tf_op jit(solution)/shard_map/ppermute | solution.py:49
  75.1 1.4 %collective-permute-done.14 = f32[8,128]{1,0:T(8,128)S(1)} collective-permute-done((f32[8,128]{1,0:T(8,128)S(1)}, f32[8,128]{1,0:T(8,128)S(1)}, u32[]{:S(2)}, u32[]{:S(2)}) %collective-permute-start.14) | collective-permute-done | bytes 4128 | tf_op jit(solution)/shard_map/ppermute | solution.py:49
  77.1 1.5 %collective-permute-start.18 = (f32[8,128]{1,0:T(8,128)S(1)}, f32[8,128]{1,0:T(8,128)S(1)}, u32[]{:S(2)}, u32[]{:S(2)}) collective-permute-start(f32[8,128]{1,0:T(8,128)S(1)} %add_add_fusion.3), channel_id=1, source_target_pairs={{0,1},{1,2},{2,3},{3,0},{4,5},{5,6},{6,7},{7,4},{8,9},{9,10},{10,1... | collective-permute-start | bytes 12296 | tf_op jit(solution)/shard_map/ppermute | solution.py:49
  78.5 1.2 %collective-permute-start.17 = (f32[8,128]{1,0:T(8,128)S(1)}, f32[8,128]{1,0:T(8,128)S(1)}, u32[]{:S(2)}, u32[]{:S(2)}) collective-permute-start(f32[8,128]{1,0:T(8,128)S(1)} %add_add_fusion.3), channel_id=1, source_target_pairs={{0,2},{1,3},{2,0},{3,1},{4,6},{5,7},{6,4},{7,5},{8,10},{9,11},{10,... | collective-permute-start | bytes 12296 | tf_op jit(solution)/shard_map/ppermute | solution.py:49
  80.1 1.8 %collective-permute-done.18 = f32[8,128]{1,0:T(8,128)S(1)} collective-permute-done((f32[8,128]{1,0:T(8,128)S(1)}, f32[8,128]{1,0:T(8,128)S(1)}, u32[]{:S(2)}, u32[]{:S(2)}) %collective-permute-start.18) | collective-permute-done | bytes 4128 | tf_op jit(solution)/shard_map/ppermute | solution.py:49
  81.9 1.7 %collective-permute-done.17 = f32[8,128]{1,0:T(8,128)S(1)} collective-permute-done((f32[8,128]{1,0:T(8,128)S(1)}, f32[8,128]{1,0:T(8,128)S(1)}, u32[]{:S(2)}, u32[]{:S(2)}) %collective-permute-start.17) | collective-permute-done | bytes 4128 | tf_op jit(solution)/shard_map/ppermute | solution.py:49
  84.3 3.5 %flatten.2 = f32[16,36864]{1,0:T(8,128)} custom-call(s32[2]{0:T(128)} %pad_add_fusion.place_ref, f32[2,8,192,192]{3,2,1,0:T(8,128)} %get-tuple-element.48.square_ref), custom_call_target="tpu_custom_call" | custom-call | flops 20000000 | bytes 3000000 | tf_op jit(solution)/shard_map/flatten/pallas_call | solution.py:134
  (81 shorter events, 21.7 us)
Async XLA Ops:
  0.6 34.0 %copy-start.3 = (f32[36864]{0:T(1024)S(1)}, f32[36864]{0:T(1024)}, u32[]{:S(2)}) copy-start(f32[36864]{0:T(1024)} %param.13) | copy-start | bytes 442372
  0.7 32.6 %copy-start.1 = (s32[512]{0:T(512)S(1)}, s32[512]{0:T(512)}, u32[]{:S(2)}) copy-start(s32[512]{0:T(512)} %param.10) | copy-start | bytes 6148
  1.6 5.3 %collective-permute-start.2 = (bf16[8,4608]{1,0:T(8,128)(2,1)S(1)}, bf16[8,4608]{1,0:T(8,128)(2,1)S(1)}, u32[]{:S(2)}, u32[]{:S(2)}) collective-permute-start(bf16[8,4608]{1,0:T(8,128)(2,1)S(1)} %constant_dynamic-slice_fusion), channel_id=1, source_target_pairs={{0,3},{1,0},{2,1},{3,2},{4,7},{5,4},{6,5},{7,6},{8,11},{9,8},{10,9... | collective-permute-start | bytes 221192 | tf_op jit(solution)/shard_map/ppermute | solution.py:38
  4.7 5.9 %collective-permute-start.1 = (bf16[8,4608]{1,0:T(8,128)(2,1)S(1)}, bf16[8,4608]{1,0:T(8,128)(2,1)S(1)}, u32[]{:S(2)}, u32[]{:S(2)}) collective-permute-start(bf16[8,4608]{1,0:T(8,128)(2,1)S(1)} %constant_dynamic-slice_fusion), channel_id=1, source_target_pairs={{0,2},{1,3},{2,0},{3,1},{4,6},{5,7},{6,4},{7,5},{8,10},{9,11},{10,... | collective-permute-start | bytes 221192 | tf_op jit(solution)/shard_map/ppermute | solution.py:38
  5.3 6.0 %collective-permute-start = (bf16[8,4608]{1,0:T(8,128)(2,1)S(1)}, bf16[8,4608]{1,0:T(8,128)(2,1)S(1)}, u32[]{:S(2)}, u32[]{:S(2)}) collective-permute-start(bf16[8,4608]{1,0:T(8,128)(2,1)S(1)} %constant_dynamic-slice_fusion), channel_id=1, source_target_pairs={{0,1},{1,2},{2,3},{3,0},{4,5},{5,6},{6,7},{7,4},{8,9},{9,10},{10,1... | collective-permute-start | bytes 221192 | tf_op jit(solution)/shard_map/ppermute | solution.py:38
  11.4 11.5 %collective-permute-start.5 = (bf16[32,4608]{1,0:T(8,128)(2,1)S(1)}, bf16[32,4608]{1,0:T(8,128)(2,1)S(1)}, u32[]{:S(2)}, u32[]{:S(2)}) collective-permute-start(bf16[32,4608]{1,0:T(8,128)(2,1)S(1)} %pad_maximum_fusion.b0), channel_id=1, source_target_pairs={{0,12},{1,13},{2,14},{3,15},{4,0},{5,1},{6,2},{7,3},{8,4},{9,5},{1... | collective-permute-start | bytes 884744 | tf_op jit(solution)/shard_map/ppermute | solution.py:38
  15.5 8.3 %collective-permute-start.4 = (bf16[32,4608]{1,0:T(8,128)(2,1)S(1)}, bf16[32,4608]{1,0:T(8,128)(2,1)S(1)}, u32[]{:S(2)}, u32[]{:S(2)}) collective-permute-start(bf16[32,4608]{1,0:T(8,128)(2,1)S(1)} %pad_maximum_fusion.b0), channel_id=1, source_target_pairs={{0,8},{1,9},{2,10},{3,11},{4,12},{5,13},{6,14},{7,15},{8,0},{9,1},... | collective-permute-start | bytes 884744 | tf_op jit(solution)/shard_map/ppermute | solution.py:38
  15.5 11.1 %collective-permute-start.3 = (bf16[32,4608]{1,0:T(8,128)(2,1)S(1)}, bf16[32,4608]{1,0:T(8,128)(2,1)S(1)}, u32[]{:S(2)}, u32[]{:S(2)}) collective-permute-start(bf16[32,4608]{1,0:T(8,128)(2,1)S(1)} %pad_maximum_fusion.b0), channel_id=1, source_target_pairs={{0,4},{1,5},{2,6},{3,7},{4,8},{5,9},{6,10},{7,11},{8,12},{9,13},{1... | collective-permute-start | bytes 884744 | tf_op jit(solution)/shard_map/ppermute | solution.py:38
  27.6 12.1 %copy-start.2 = (f32[16,4608]{1,0:T(8,128)S(1)}, f32[16,4608]{1,0:T(8,128)}, u32[]{:S(2)}) copy-start(f32[16,4608]{1,0:T(8,128)} %get-tuple-element.31) | copy-start | bytes 884740
  27.6 10.6 %collective-permute-start.6 = (f32[16,4608]{1,0:T(8,128)S(1)}, f32[16,4608]{1,0:T(8,128)S(1)}, u32[]{:S(2)}, u32[]{:S(2)}) collective-permute-start(f32[16,4608]{1,0:T(8,128)S(1)} %get-tuple-element.28), channel_id=1, source_target_pairs={{0,16},{1,17},{2,18},{3,19},{4,20},{5,21},{6,22},{7,23},{8,24},{9,... | collective-permute-start | bytes 884744 | tf_op jit(solution)/shard_map/ppermute | solution.py:38
  29.1 10.6 %collective-permute-start.7 = (f32[16,4608]{1,0:T(8,128)S(1)}, f32[16,4608]{1,0:T(8,128)S(1)}, u32[]{:S(2)}, u32[]{:S(2)}) collective-permute-start(f32[16,4608]{1,0:T(8,128)S(1)} %get-tuple-element.29), channel_id=1, source_target_pairs={{0,32},{1,33},{2,34},{3,35},{4,36},{5,37},{6,38},{7,39},{8,40},{9,... | collective-permute-start | bytes 884744 | tf_op jit(solution)/shard_map/ppermute | solution.py:38
  31.8 7.9 %collective-permute-start.8 = (f32[16,4608]{1,0:T(8,128)S(1)}, f32[16,4608]{1,0:T(8,128)S(1)}, u32[]{:S(2)}, u32[]{:S(2)}) collective-permute-start(f32[16,4608]{1,0:T(8,128)S(1)} %get-tuple-element.30), channel_id=1, source_target_pairs={{0,48},{1,49},{2,50},{3,51},{4,52},{5,53},{6,54},{7,55},{8,56},{9,... | collective-permute-start | bytes 884744 | tf_op jit(solution)/shard_map/ppermute | solution.py:38
  40.4 1.4 %collective-permute-start.9 = (f32[8,4608]{1,0:T(8,128)S(1)}, f32[8,4608]{1,0:T(8,128)S(1)}, u32[]{:S(2)}, u32[]{:S(2)}) collective-permute-start(f32[8,4608]{1,0:T(8,128)S(1)} %get-tuple-element.58), channel_id=1, source_target_pairs={{0,64},{64,0},{1,65},{65,1},{2,66},{66,2},{3,67},{67,3},{4,68},{68... | collective-permute-start | bytes 442376 | tf_op jit(solution)/shard_map/ppermute | solution.py:53
  61.5 26.7 %collective-permute-start.10 = (f32[8,36864]{1,0:T(8,128)}, f32[8,36864]{1,0:T(8,128)S(1)}, u32[]{:S(2)}, u32[]{:S(2)}) collective-permute-start(f32[8,36864]{1,0:T(8,128)} %flatten.3), channel_id=1, source_target_pairs={{0,64},{64,0},{1,65},{65,1},{2,66},{66,2},{3,67},{67,3},{4,68},{68... | collective-permute-start | bytes 3538952 | tf_op jit(solution)/shard_map/ppermute | solution.py:53
  61.7 5.0 %collective-permute-start.13 = (f32[8,128]{1,0:T(8,128)S(1)}, f32[8,128]{1,0:T(8,128)S(1)}, u32[]{:S(2)}, u32[]{:S(2)}) collective-permute-start(f32[8,128]{1,0:T(8,128)S(1)} %get-tuple-element.49), channel_id=1, source_target_pairs={{0,48},{16,0},{32,16},{48,32},{1,49},{17,1},{33,17},{49,33},{2,50}... | collective-permute-start | bytes 12296 | tf_op jit(solution)/shard_map/ppermute | solution.py:49
  64.2 4.8 %collective-permute-start.12 = (f32[8,128]{1,0:T(8,128)S(1)}, f32[8,128]{1,0:T(8,128)S(1)}, u32[]{:S(2)}, u32[]{:S(2)}) collective-permute-start(f32[8,128]{1,0:T(8,128)S(1)} %get-tuple-element.49), channel_id=1, source_target_pairs={{0,16},{16,32},{32,48},{48,0},{1,17},{17,33},{33,49},{49,1},{2,18}... | collective-permute-start | bytes 12296 | tf_op jit(solution)/shard_map/ppermute | solution.py:49
  64.2 5.1 %collective-permute-start.11 = (f32[8,128]{1,0:T(8,128)S(1)}, f32[8,128]{1,0:T(8,128)S(1)}, u32[]{:S(2)}, u32[]{:S(2)}) collective-permute-start(f32[8,128]{1,0:T(8,128)S(1)} %get-tuple-element.49), channel_id=1, source_target_pairs={{0,32},{16,48},{32,0},{48,16},{1,33},{17,49},{33,1},{49,17},{2,34}... | collective-permute-start | bytes 12296 | tf_op jit(solution)/shard_map/ppermute | solution.py:49
  69.3 3.6 %collective-permute-start.16 = (f32[8,128]{1,0:T(8,128)S(1)}, f32[8,128]{1,0:T(8,128)S(1)}, u32[]{:S(2)}, u32[]{:S(2)}) collective-permute-start(f32[8,128]{1,0:T(8,128)S(1)} %add_add_fusion.4), channel_id=1, source_target_pairs={{0,12},{4,0},{8,4},{12,8},{1,13},{5,1},{9,5},{13,9},{2,14},{6,2},{... | collective-permute-start | bytes 12296 | tf_op jit(solution)/shard_map/ppermute | solution.py:49
  70.3 4.8 %collective-permute-start.15 = (f32[8,128]{1,0:T(8,128)S(1)}, f32[8,128]{1,0:T(8,128)S(1)}, u32[]{:S(2)}, u32[]{:S(2)}) collective-permute-start(f32[8,128]{1,0:T(8,128)S(1)} %add_add_fusion.4), channel_id=1, source_target_pairs={{0,4},{4,8},{8,12},{12,0},{1,5},{5,9},{9,13},{13,1},{2,6},{6,10},{... | collective-permute-start | bytes 12296 | tf_op jit(solution)/shard_map/ppermute | solution.py:49
  71.4 5.1 %collective-permute-start.14 = (f32[8,128]{1,0:T(8,128)S(1)}, f32[8,128]{1,0:T(8,128)S(1)}, u32[]{:S(2)}, u32[]{:S(2)}) collective-permute-start(f32[8,128]{1,0:T(8,128)S(1)} %add_add_fusion.4), channel_id=1, source_target_pairs={{0,8},{4,12},{8,0},{12,4},{1,9},{5,13},{9,1},{13,5},{2,10},{6,14},... | collective-permute-start | bytes 12296 | tf_op jit(solution)/shard_map/ppermute | solution.py:49
  76.5 3.6 %collective-permute-start.19 = (f32[8,128]{1,0:T(8,128)S(1)}, f32[8,128]{1,0:T(8,128)S(1)}, u32[]{:S(2)}, u32[]{:S(2)}) collective-permute-start(f32[8,128]{1,0:T(8,128)S(1)} %add_add_fusion.3), channel_id=1, source_target_pairs={{0,3},{1,0},{2,1},{3,2},{4,7},{5,4},{6,5},{7,6},{8,11},{9,8},{10,9... | collective-permute-start | bytes 12296 | tf_op jit(solution)/shard_map/ppermute | solution.py:49
  77.1 4.8 %collective-permute-start.18 = (f32[8,128]{1,0:T(8,128)S(1)}, f32[8,128]{1,0:T(8,128)S(1)}, u32[]{:S(2)}, u32[]{:S(2)}) collective-permute-start(f32[8,128]{1,0:T(8,128)S(1)} %add_add_fusion.3), channel_id=1, source_target_pairs={{0,1},{1,2},{2,3},{3,0},{4,5},{5,6},{6,7},{7,4},{8,9},{9,10},{10,1... | collective-permute-start | bytes 12296 | tf_op jit(solution)/shard_map/ppermute | solution.py:49
  78.5 5.1 %collective-permute-start.17 = (f32[8,128]{1,0:T(8,128)S(1)}, f32[8,128]{1,0:T(8,128)S(1)}, u32[]{:S(2)}, u32[]{:S(2)}) collective-permute-start(f32[8,128]{1,0:T(8,128)S(1)} %add_add_fusion.3), channel_id=1, source_target_pairs={{0,2},{1,3},{2,0},{3,1},{4,6},{5,7},{6,4},{7,5},{8,10},{9,11},{10,... | collective-permute-start | bytes 12296 | tf_op jit(solution)/shard_map/ppermute | solution.py:49
  83.6 4.1 %collective-permute-start.20 = (f32[8,128]{1,0:T(8,128)S(1)}, f32[8,128]{1,0:T(8,128)S(1)}, u32[]{:S(2)}, u32[]{:S(2)}) collective-permute-start(f32[8,128]{1,0:T(8,128)S(1)} %add_add_fusion.2), channel_id=1, source_target_pairs={{0,64},{64,0},{1,65},{65,1},{2,66},{66,2},{3,67},{67,3},{4,68},{68... | collective-permute-start | bytes 12296 | tf_op jit(solution)/shard_map/ppermute | solution.py:53
  (2 other events, 1.6 us)

commit v5 on v4

--- a/solution.py
+++ b/solution.py
@@ -33,7 +33,7 @@
         stride = STRIDES[core][phase]
         for chip in range(64):
             place = (chip // stride) % 4
-            target = chip + (((place + step) % 4) - place) * stride
+            target = chip + ((place ^ step) - place) * stride
             pairs.append((core * 64 + chip, core * 64 + target))
     return lax.ppermute(value, ALL, pairs)
 
@@ -46,7 +46,7 @@
 
 
 def axis_shift(value, axis, step):
-    return lax.ppermute(value, axis, [(i, (i + step) % 4) for i in range(4)])
+    return lax.ppermute(value, axis, [(i, i ^ step) for i in range(4)])
 
 
 def swap_cores(value):
@@ -427,13 +427,13 @@
     places = [(chip // strides[p]) % 4 for p in range(3)]
 
     def moved(chips, phase, step):
-        return chips + ((places[phase] + step + 4) % 4 - places[phase]) * strides[phase]
+        return chips + ((places[phase] ^ step) - places[phase]) * strides[phase]
 
     steps = jnp.arange(4, dtype=jnp.int32)
     targets = moved(chip, 2, steps)
     rows = (jnp.arange(16, dtype=jnp.int32) + 8 * segment) % 16
     dimers = (targets[:, None] * 16 + rows[None, :]).reshape(64)
-    sources = moved(moved(chip, 0, -steps)[None, :], 1, -steps[:, None])
+    sources = moved(moved(chip, 0, steps)[None, :], 1, steps[:, None])
     labels = (sources[:, :, None] * 8 + jnp.arange(8, dtype=jnp.int32)).reshape(128)
     pairs = pair_ids[:, dimers]
     weights = esp_weights(pairs[0], pairs[1], centers, labels).astype(bf16)

time: 91 us -> 90.9 us (level)
  waiting for transfers between devices: 22.6 us -> 20.9 us
  starting transfers between devices: 26.6 us -> 28.1 us
    ppermute x9, waiting for transfers between devices: 11.3 us -> 7.53 us  [axis_shift(): return lax.ppermute(value, axis, [(i, i ^ step) for i in range(4)])]
    ppermute x9, starting transfers between devices: 10.7 us -> 14.1 us  [axis_shift(): return lax.ppermute(value, axis, [(i, i ^ step) for i in range(4)])]
    ppermute x9, waiting for transfers between devices: 10.6 us -> 12.7 us  [phase_shift(): return lax.ppermute(value, ALL, pairs)]
    ppermute x9, starting transfers between devices: 15.7 us -> 13.9 us  [phase_shift(): return lax.ppermute(value, ALL, pairs)]
  transfers between devices with their start and end apart: 21 -> 21, of which waited for: 15 -> 16; matrix products, arithmetic and copies ran while one was open for 11% -> 11% of each run, Pallas kernels for 7% -> 7%
where the time goes in v5:
time: 90.9 us; the launch traced here: 89.2 us
  starting transfers between devices  28.1 us (31%)
  Pallas kernels  26.4 us (29%)
  waiting for transfers between devices  20.9 us (23%)
  local copies, waits for them, and re-layouts  10.5 us (12%)
  other arithmetic  2.44 us (3%)
    pallas_call x1, Pallas kernels, solve(): pl.pallas_call(solve_kernel, name='solve', in_specs=[pl.BlockSpec(memory_...  15.6 us
    ppermute x9, starting transfers between devices, axis_shift(): return lax.ppermute(value, axis, [(i, i ^ step) for i in range(4)])  14.1 us
    ppermute x9, starting transfers between devices, phase_shift(): return lax.ppermute(value, ALL, pairs)  13.9 us
    ppermute x9, waiting for transfers between devices, phase_shift(): return lax.ppermute(value, ALL, pairs)  12.7 us
    ppermute x9, waiting for transfers between devices, axis_shift(): return lax.ppermute(value, axis, [(i, i ^ step) for i in range(4)])  7.53 us
    pallas_call x2, Pallas kernels, flatten(): pl.pallas_call(flatten_kernel, name='flatten', grid_spec=pltpu.PrefetchSc...  6.95 us
    pallas_call x1, Pallas kernels, unflatten(): pl.pallas_call(unflatten_kernel, name='unflatten', grid_spec=pltpu.Prefet...  2.74 us
  transfers between devices with their start and end apart: 21, of which 16 were waited for; matrix products, arithmetic and copies ran while one was open for 11% of the time, Pallas kernels for 7%

profile of v5, /device:TPU:0, one launch (start us, length us, event | category | flops | bytes accessed | tf_op | source)
XLA Modules:
  0.0 89.2 jit_solution(5728028156161843915)
XLA Ops:
  1.6 3.1 %collective-permute-start.2 = (bf16[8,4608]{1,0:T(8,128)(2,1)S(1)}, bf16[8,4608]{1,0:T(8,128)(2,1)S(1)}, u32[]{:S(2)}, u32[]{:S(2)}) collective-permute-start(bf16[8,4608]{1,0:T(8,128)(2,1)S(1)} %constant_dynamic-slice_fusion), channel_id=1, source_target_pairs={{0,3},{1,2},{2,1},{3,0},{4,7},{5,6},{6,5},{7,4},{8,11},{9,10},{10,... | collective-permute-start | bytes 221192 | tf_op jit(solution)/shard_map/ppermute | solution.py:38
  6.3 1.1 %collective-permute-done.2 = bf16[8,4608]{1,0:T(8,128)(2,1)S(1)} collective-permute-done((bf16[8,4608]{1,0:T(8,128)(2,1)S(1)}, bf16[8,4608]{1,0:T(8,128)(2,1)S(1)}, u32[]{:S(2)}, u32[]{:S(2)}) %collective-permute-start.2) | collective-permute-done | bytes 73760 | tf_op jit(solution)/shard_map/ppermute | solution.py:38
  7.4 3.2 %collective-permute-done.1 = bf16[8,4608]{1,0:T(8,128)(2,1)S(1)} collective-permute-done((bf16[8,4608]{1,0:T(8,128)(2,1)S(1)}, bf16[8,4608]{1,0:T(8,128)(2,1)S(1)}, u32[]{:S(2)}, u32[]{:S(2)}) %collective-permute-start.1) | collective-permute-done | bytes 73760 | tf_op jit(solution)/shard_map/ppermute | solution.py:38
  10.6 4.1 %collective-permute-start.5 = (bf16[32,4608]{1,0:T(8,128)(2,1)S(1)}, bf16[32,4608]{1,0:T(8,128)(2,1)S(1)}, u32[]{:S(2)}, u32[]{:S(2)}) collective-permute-start(bf16[32,4608]{1,0:T(8,128)(2,1)S(1)} %pad_maximum_fusion.b0), channel_id=1, source_target_pairs={{0,12},{1,13},{2,14},{3,15},{4,8},{5,9},{6,10},{7,11},{8,4},{9,5},... | collective-permute-start | bytes 884744 | tf_op jit(solution)/shard_map/ppermute | solution.py:38
  20.8 1.3 %collective-permute-done.5.b3 = bf16[32,4608]{1,0:T(8,128)(2,1)S(1)} collective-permute-done((bf16[32,4608]{1,0:T(8,128)(2,1)S(1)}, bf16[32,4608]{1,0:T(8,128)(2,1)S(1)}, u32[]{:S(2)}, u32[]{:S(2)}) %collective-permute-start.5) | collective-permute-done | bytes 294944 | tf_op jit(solution)/shard_map/ppermute | solution.py:38
  23.6 1.0 %partial_fields.1 = (f32[16,4608]{1,0:T(8,128)}, f32[16,4608]{1,0:T(8,128)S(1)}, f32[16,4608]{1,0:T(8,128)S(1)}, f32[16,4608]{1,0:T(8,128)S(1)}) custom-call(bf16[64,128]{1,0:T(8,128)(2,1)S(1)} %select_convert_fusion.weight_ref, bf16[32,4608]{1,0:T(8,128)(2,1)S(1)} %pad_maximum_fusion.b0, bf16[32,4608]{1,0:T(8,128)(2,1)S(1)} %collective-permute-done.3.b1, ...), custom_call_target="tpu_custom_call" | custom-call | flops 80000000 | bytes 2400000 | tf_op jit(solution)/shard_map/partial_fields/pallas_call | solution.py:163
  24.6 1.5 %collective-permute-start.6 = (f32[16,4608]{1,0:T(8,128)S(1)}, f32[16,4608]{1,0:T(8,128)S(1)}, u32[]{:S(2)}, u32[]{:S(2)}) collective-permute-start(f32[16,4608]{1,0:T(8,128)S(1)} %get-tuple-element.28), channel_id=1, source_target_pairs={{0,16},{1,17},{2,18},{3,19},{4,20},{5,21},{6,22},{7,23},{8,24},{9,... | collective-permute-start | bytes 884744 | tf_op jit(solution)/shard_map/ppermute | solution.py:38
  26.0 2.7 %collective-permute-start.7 = (f32[16,4608]{1,0:T(8,128)S(1)}, f32[16,4608]{1,0:T(8,128)S(1)}, u32[]{:S(2)}, u32[]{:S(2)}) collective-permute-start(f32[16,4608]{1,0:T(8,128)S(1)} %get-tuple-element.29), channel_id=1, source_target_pairs={{0,32},{1,33},{2,34},{3,35},{4,36},{5,37},{6,38},{7,39},{8,40},{9,... | collective-permute-start | bytes 884744 | tf_op jit(solution)/shard_map/ppermute | solution.py:38
  31.5 2.7 %unflatten.1 = (f32[1536,128]{1,0:T(8,128)}, f32[1536,128]{1,0:T(8,128)}, f32[96,192]{1,0:T(8,128)}) custom-call(s32[1]{0:T(128)} %bitcast.segment_ref, f32[16,36864]{1,0:T(8,128)} %core_ref, f32[96,192]{1,0:T(8,128)} %esp_any), custom_call_target="tpu_custom_call" | custom-call | flops 20000000 | bytes 3000000 | tf_op jit(solution)/shard_map/unflatten/pallas_call | solution.py:97
  34.2 2.5 %collective-permute-done.7 = f32[16,4608]{1,0:T(8,128)S(1)} collective-permute-done((f32[16,4608]{1,0:T(8,128)S(1)}, f32[16,4608]{1,0:T(8,128)S(1)}, u32[]{:S(2)}, u32[]{:S(2)}) %collective-permute-start.7) | collective-permute-done | bytes 294944 | tf_op jit(solution)/shard_map/ppermute | solution.py:38
  36.7 3.1 %collective-permute-done.8 = f32[16,4608]{1,0:T(8,128)S(1)} collective-permute-done((f32[16,4608]{1,0:T(8,128)S(1)}, f32[16,4608]{1,0:T(8,128)S(1)}, u32[]{:S(2)}, u32[]{:S(2)}) %collective-permute-start.8) | collective-permute-done | bytes 294944 | tf_op jit(solution)/shard_map/ppermute | solution.py:38
  42.5 15.6 %solve.1 = (f32[2,8,192,192]{3,2,1,0:T(8,128)}, f32[8,128]{1,0:T(8,128)S(1)}) custom-call(s32[8,2]{1,0:T(8,128)} %bitcast.32, f32[8,4608]{1,0:T(8,128)} %get-tuple-element.59.mine_any, f32[8,4608]{1,0:T(8,128)} %copy-done.4, f32[1536,128]{1,0:T(8,128)} %get-tuple-element.43.first_any, f32[1536,128]{1,0:T(8,128)} %get-tuple-element.44.second_any, ...), custom_call_target="tpu_custom_call" | custom-call | flops 11000000512 | bytes 6000000 | tf_op jit(solution)/shard_map/solve/pallas_call | solution.py:359
  58.2 3.5 %flatten.3 = f32[8,36864]{1,0:T(8,128)} custom-call(s32[2]{0:T(128)} %pad_add_fusion.1.place_ref, f32[2,8,192,192]{3,2,1,0:T(8,128)} %get-tuple-element.48.square_ref), custom_call_target="tpu_custom_call" | custom-call | flops 20000000 | bytes 3000000 | tf_op jit(solution)/shard_map/flatten/pallas_call | solution.py:134
  62.3 4.2 %collective-permute-start.11 = (f32[8,128]{1,0:T(8,128)S(1)}, f32[8,128]{1,0:T(8,128)S(1)}, u32[]{:S(2)}, u32[]{:S(2)}) collective-permute-start(f32[8,128]{1,0:T(8,128)S(1)} %get-tuple-element.49), channel_id=1, source_target_pairs={{0,32},{16,48},{32,0},{48,16},{1,33},{17,49},{33,1},{49,17},{2,34}... | collective-permute-start | bytes 12296 | tf_op jit(solution)/shard_map/ppermute | solution.py:49
  66.7 1.5 %collective-permute-done.11 = f32[8,128]{1,0:T(8,128)S(1)} collective-permute-done((f32[8,128]{1,0:T(8,128)S(1)}, f32[8,128]{1,0:T(8,128)S(1)}, u32[]{:S(2)}, u32[]{:S(2)}) %collective-permute-start.11) | collective-permute-done | bytes 4128 | tf_op jit(solution)/shard_map/ppermute | solution.py:49
  68.2 3.1 %collective-permute-start.16 = (f32[8,128]{1,0:T(8,128)S(1)}, f32[8,128]{1,0:T(8,128)S(1)}, u32[]{:S(2)}, u32[]{:S(2)}) collective-permute-start(f32[8,128]{1,0:T(8,128)S(1)} %add_add_fusion.4), channel_id=1, source_target_pairs={{0,12},{4,8},{8,4},{12,0},{1,13},{5,9},{9,5},{13,1},{2,14},{6,10},... | collective-permute-start | bytes 12296 | tf_op jit(solution)/shard_map/ppermute | solution.py:49
  71.3 1.6 %collective-permute-start.14 = (f32[8,128]{1,0:T(8,128)S(1)}, f32[8,128]{1,0:T(8,128)S(1)}, u32[]{:S(2)}, u32[]{:S(2)}) collective-permute-start(f32[8,128]{1,0:T(8,128)S(1)} %add_add_fusion.4), channel_id=1, source_target_pairs={{0,8},{4,12},{8,0},{12,4},{1,9},{5,13},{9,1},{13,5},{2,10},{6,14},... | collective-permute-start | bytes 12296 | tf_op jit(solution)/shard_map/ppermute | solution.py:49
  73.0 1.9 %collective-permute-done.15 = f32[8,128]{1,0:T(8,128)S(1)} collective-permute-done((f32[8,128]{1,0:T(8,128)S(1)}, f32[8,128]{1,0:T(8,128)S(1)}, u32[]{:S(2)}, u32[]{:S(2)}) %collective-permute-start.15) | collective-permute-done | bytes 4128 | tf_op jit(solution)/shard_map/ppermute | solution.py:49
  74.9 1.5 %collective-permute-done.14 = f32[8,128]{1,0:T(8,128)S(1)} collective-permute-done((f32[8,128]{1,0:T(8,128)S(1)}, f32[8,128]{1,0:T(8,128)S(1)}, u32[]{:S(2)}, u32[]{:S(2)}) %collective-permute-start.14) | collective-permute-done | bytes 4128 | tf_op jit(solution)/shard_map/ppermute | solution.py:49
  76.4 1.3 %collective-permute-start.19 = (f32[8,128]{1,0:T(8,128)S(1)}, f32[8,128]{1,0:T(8,128)S(1)}, u32[]{:S(2)}, u32[]{:S(2)}) collective-permute-start(f32[8,128]{1,0:T(8,128)S(1)} %add_add_fusion.3), channel_id=1, source_target_pairs={{0,3},{1,2},{2,1},{3,0},{4,7},{5,6},{6,5},{7,4},{8,11},{9,10},{10,... | collective-permute-start | bytes 12296 | tf_op jit(solution)/shard_map/ppermute | solution.py:49
  78.4 2.7 %collective-permute-start.17 = (f32[8,128]{1,0:T(8,128)S(1)}, f32[8,128]{1,0:T(8,128)S(1)}, u32[]{:S(2)}, u32[]{:S(2)}) collective-permute-start(f32[8,128]{1,0:T(8,128)S(1)} %add_add_fusion.3), channel_id=1, source_target_pairs={{0,2},{1,3},{2,0},{3,1},{4,6},{5,7},{6,4},{7,5},{8,10},{9,11},{10,... | collective-permute-start | bytes 12296 | tf_op jit(solution)/shard_map/ppermute | solution.py:49
  81.3 2.1 %collective-permute-done.17 = f32[8,128]{1,0:T(8,128)S(1)} collective-permute-done((f32[8,128]{1,0:T(8,128)S(1)}, f32[8,128]{1,0:T(8,128)S(1)}, u32[]{:S(2)}, u32[]{:S(2)}) %collective-permute-start.17) | collective-permute-done | bytes 4128 | tf_op jit(solution)/shard_map/ppermute | solution.py:49
  84.1 3.5 %flatten.2 = f32[16,36864]{1,0:T(8,128)} custom-call(s32[2]{0:T(128)} %pad_add_fusion.place_ref, f32[2,8,192,192]{3,2,1,0:T(8,128)} %get-tuple-element.48.square_ref), custom_call_target="tpu_custom_call" | custom-call | flops 20000000 | bytes 3000000 | tf_op jit(solution)/shard_map/flatten/pallas_call | solution.py:134
  88.1 1.1 %bitcast_dynamic-update-slice_fusion = f32[1,16,36864]{2,1,0:T(8,128)} fusion(f32[1,16,36864]{2,1,0:T(8,128)} %bitcast.28, s32[]{:T(128)S(6)} %select_n.122, f32[8,36864]{1,0:T(8,128)S(1)} %collective-permute-done.10), kind=kLoop, calls=%fused_computation.5 | loop fusion | bytes 2359300 | tf_op jit(solution)/shard_map/dynamic_update_slice | solution.py:468
  (81 shorter events, 18.3 us)
Async XLA Ops:
  0.6 30.1 %copy-start.3 = (f32[36864]{0:T(1024)S(1)}, f32[36864]{0:T(1024)}, u32[]{:S(2)}) copy-start(f32[36864]{0:T(1024)} %param.13) | copy-start | bytes 442372
  0.7 28.6 %copy-start.1 = (s32[512]{0:T(512)S(1)}, s32[512]{0:T(512)}, u32[]{:S(2)}) copy-start(s32[512]{0:T(512)} %param.10) | copy-start | bytes 6148
  1.6 5.8 %collective-permute-start.2 = (bf16[8,4608]{1,0:T(8,128)(2,1)S(1)}, bf16[8,4608]{1,0:T(8,128)(2,1)S(1)}, u32[]{:S(2)}, u32[]{:S(2)}) collective-permute-start(bf16[8,4608]{1,0:T(8,128)(2,1)S(1)} %constant_dynamic-slice_fusion), channel_id=1, source_target_pairs={{0,3},{1,2},{2,1},{3,0},{4,7},{5,6},{6,5},{7,4},{8,11},{9,10},{10,... | collective-permute-start | bytes 221192 | tf_op jit(solution)/shard_map/ppermute | solution.py:38
  4.7 5.9 %collective-permute-start.1 = (bf16[8,4608]{1,0:T(8,128)(2,1)S(1)}, bf16[8,4608]{1,0:T(8,128)(2,1)S(1)}, u32[]{:S(2)}, u32[]{:S(2)}) collective-permute-start(bf16[8,4608]{1,0:T(8,128)(2,1)S(1)} %constant_dynamic-slice_fusion), channel_id=1, source_target_pairs={{0,2},{1,3},{2,0},{3,1},{4,6},{5,7},{6,4},{7,5},{8,10},{9,11},{10,... | collective-permute-start | bytes 221192 | tf_op jit(solution)/shard_map/ppermute | solution.py:38
  5.3 5.2 %collective-permute-start = (bf16[8,4608]{1,0:T(8,128)(2,1)S(1)}, bf16[8,4608]{1,0:T(8,128)(2,1)S(1)}, u32[]{:S(2)}, u32[]{:S(2)}) collective-permute-start(bf16[8,4608]{1,0:T(8,128)(2,1)S(1)} %constant_dynamic-slice_fusion), channel_id=1, source_target_pairs={{0,1},{1,0},{2,3},{3,2},{4,5},{5,4},{6,7},{7,6},{8,9},{9,8},{10,11... | collective-permute-start | bytes 221192 | tf_op jit(solution)/shard_map/ppermute | solution.py:38
  10.6 11.5 %collective-permute-start.5 = (bf16[32,4608]{1,0:T(8,128)(2,1)S(1)}, bf16[32,4608]{1,0:T(8,128)(2,1)S(1)}, u32[]{:S(2)}, u32[]{:S(2)}) collective-permute-start(bf16[32,4608]{1,0:T(8,128)(2,1)S(1)} %pad_maximum_fusion.b0), channel_id=1, source_target_pairs={{0,12},{1,13},{2,14},{3,15},{4,8},{5,9},{6,10},{7,11},{8,4},{9,5},... | collective-permute-start | bytes 884744 | tf_op jit(solution)/shard_map/ppermute | solution.py:38
  14.7 8.2 %collective-permute-start.4 = (bf16[32,4608]{1,0:T(8,128)(2,1)S(1)}, bf16[32,4608]{1,0:T(8,128)(2,1)S(1)}, u32[]{:S(2)}, u32[]{:S(2)}) collective-permute-start(bf16[32,4608]{1,0:T(8,128)(2,1)S(1)} %pad_maximum_fusion.b0), channel_id=1, source_target_pairs={{0,8},{1,9},{2,10},{3,11},{4,12},{5,13},{6,14},{7,15},{8,0},{9,1},... | collective-permute-start | bytes 884744 | tf_op jit(solution)/shard_map/ppermute | solution.py:38
  14.7 8.8 %collective-permute-start.3 = (bf16[32,4608]{1,0:T(8,128)(2,1)S(1)}, bf16[32,4608]{1,0:T(8,128)(2,1)S(1)}, u32[]{:S(2)}, u32[]{:S(2)}) collective-permute-start(bf16[32,4608]{1,0:T(8,128)(2,1)S(1)} %pad_maximum_fusion.b0), channel_id=1, source_target_pairs={{0,4},{1,5},{2,6},{3,7},{4,0},{5,1},{6,2},{7,3},{8,12},{9,13},{10,... | collective-permute-start | bytes 884744 | tf_op jit(solution)/shard_map/ppermute | solution.py:38
  24.6 15.2 %copy-start.2 = (f32[16,4608]{1,0:T(8,128)S(1)}, f32[16,4608]{1,0:T(8,128)}, u32[]{:S(2)}) copy-start(f32[16,4608]{1,0:T(8,128)} %get-tuple-element.31) | copy-start | bytes 884740
  24.6 9.7 %collective-permute-start.6 = (f32[16,4608]{1,0:T(8,128)S(1)}, f32[16,4608]{1,0:T(8,128)S(1)}, u32[]{:S(2)}, u32[]{:S(2)}) collective-permute-start(f32[16,4608]{1,0:T(8,128)S(1)} %get-tuple-element.28), channel_id=1, source_target_pairs={{0,16},{1,17},{2,18},{3,19},{4,20},{5,21},{6,22},{7,23},{8,24},{9,... | collective-permute-start | bytes 884744 | tf_op jit(solution)/shard_map/ppermute | solution.py:38
  26.0 10.7 %collective-permute-start.7 = (f32[16,4608]{1,0:T(8,128)S(1)}, f32[16,4608]{1,0:T(8,128)S(1)}, u32[]{:S(2)}, u32[]{:S(2)}) collective-permute-start(f32[16,4608]{1,0:T(8,128)S(1)} %get-tuple-element.29), channel_id=1, source_target_pairs={{0,32},{1,33},{2,34},{3,35},{4,36},{5,37},{6,38},{7,39},{8,40},{9,... | collective-permute-start | bytes 884744 | tf_op jit(solution)/shard_map/ppermute | solution.py:38
  28.8 11.0 %collective-permute-start.8 = (f32[16,4608]{1,0:T(8,128)S(1)}, f32[16,4608]{1,0:T(8,128)S(1)}, u32[]{:S(2)}, u32[]{:S(2)}) collective-permute-start(f32[16,4608]{1,0:T(8,128)S(1)} %get-tuple-element.30), channel_id=1, source_target_pairs={{0,48},{1,49},{2,50},{3,51},{4,52},{5,53},{6,54},{7,55},{8,56},{9,... | collective-permute-start | bytes 884744 | tf_op jit(solution)/shard_map/ppermute | solution.py:38
  40.5 1.4 %collective-permute-start.9 = (f32[8,4608]{1,0:T(8,128)S(1)}, f32[8,4608]{1,0:T(8,128)S(1)}, u32[]{:S(2)}, u32[]{:S(2)}) collective-permute-start(f32[8,4608]{1,0:T(8,128)S(1)} %get-tuple-element.58), channel_id=1, source_target_pairs={{0,64},{64,0},{1,65},{65,1},{2,66},{66,2},{3,67},{67,3},{4,68},{68... | collective-permute-start | bytes 442376 | tf_op jit(solution)/shard_map/ppermute | solution.py:53
  61.7 26.4 %collective-permute-start.10 = (f32[8,36864]{1,0:T(8,128)}, f32[8,36864]{1,0:T(8,128)S(1)}, u32[]{:S(2)}, u32[]{:S(2)}) collective-permute-start(f32[8,36864]{1,0:T(8,128)} %flatten.3), channel_id=1, source_target_pairs={{0,64},{64,0},{1,65},{65,1},{2,66},{66,2},{3,67},{67,3},{4,68},{68... | collective-permute-start | bytes 3538952 | tf_op jit(solution)/shard_map/ppermute | solution.py:53
  61.8 4.8 %collective-permute-start.13 = (f32[8,128]{1,0:T(8,128)S(1)}, f32[8,128]{1,0:T(8,128)S(1)}, u32[]{:S(2)}, u32[]{:S(2)}) collective-permute-start(f32[8,128]{1,0:T(8,128)S(1)} %get-tuple-element.49), channel_id=1, source_target_pairs={{0,48},{16,32},{32,16},{48,0},{1,49},{17,33},{33,17},{49,1},{2,50}... | collective-permute-start | bytes 12296 | tf_op jit(solution)/shard_map/ppermute | solution.py:49
  62.3 4.3 %collective-permute-start.12 = (f32[8,128]{1,0:T(8,128)S(1)}, f32[8,128]{1,0:T(8,128)S(1)}, u32[]{:S(2)}, u32[]{:S(2)}) collective-permute-start(f32[8,128]{1,0:T(8,128)S(1)} %get-tuple-element.49), channel_id=1, source_target_pairs={{0,16},{16,0},{32,48},{48,32},{1,17},{17,1},{33,49},{49,33},{2,18}... | collective-permute-start | bytes 12296 | tf_op jit(solution)/shard_map/ppermute | solution.py:49
  62.3 5.8 %collective-permute-start.11 = (f32[8,128]{1,0:T(8,128)S(1)}, f32[8,128]{1,0:T(8,128)S(1)}, u32[]{:S(2)}, u32[]{:S(2)}) collective-permute-start(f32[8,128]{1,0:T(8,128)S(1)} %get-tuple-element.49), channel_id=1, source_target_pairs={{0,32},{16,48},{32,0},{48,16},{1,33},{17,49},{33,1},{49,17},{2,34}... | collective-permute-start | bytes 12296 | tf_op jit(solution)/shard_map/ppermute | solution.py:49
  68.2 4.8 %collective-permute-start.16 = (f32[8,128]{1,0:T(8,128)S(1)}, f32[8,128]{1,0:T(8,128)S(1)}, u32[]{:S(2)}, u32[]{:S(2)}) collective-permute-start(f32[8,128]{1,0:T(8,128)S(1)} %add_add_fusion.4), channel_id=1, source_target_pairs={{0,12},{4,8},{8,4},{12,0},{1,13},{5,9},{9,5},{13,1},{2,14},{6,10},... | collective-permute-start | bytes 12296 | tf_op jit(solution)/shard_map/ppermute | solution.py:49
  71.3 3.6 %collective-permute-start.15 = (f32[8,128]{1,0:T(8,128)S(1)}, f32[8,128]{1,0:T(8,128)S(1)}, u32[]{:S(2)}, u32[]{:S(2)}) collective-permute-start(f32[8,128]{1,0:T(8,128)S(1)} %add_add_fusion.4), channel_id=1, source_target_pairs={{0,4},{4,0},{8,12},{12,8},{1,5},{5,1},{9,13},{13,9},{2,6},{6,2},{1... | collective-permute-start | bytes 12296 | tf_op jit(solution)/shard_map/ppermute | solution.py:49
  71.3 5.1 %collective-permute-start.14 = (f32[8,128]{1,0:T(8,128)S(1)}, f32[8,128]{1,0:T(8,128)S(1)}, u32[]{:S(2)}, u32[]{:S(2)}) collective-permute-start(f32[8,128]{1,0:T(8,128)S(1)} %add_add_fusion.4), channel_id=1, source_target_pairs={{0,8},{4,12},{8,0},{12,4},{1,9},{5,13},{9,1},{13,5},{2,10},{6,14},... | collective-permute-start | bytes 12296 | tf_op jit(solution)/shard_map/ppermute | solution.py:49
  76.4 4.8 %collective-permute-start.19 = (f32[8,128]{1,0:T(8,128)S(1)}, f32[8,128]{1,0:T(8,128)S(1)}, u32[]{:S(2)}, u32[]{:S(2)}) collective-permute-start(f32[8,128]{1,0:T(8,128)S(1)} %add_add_fusion.3), channel_id=1, source_target_pairs={{0,3},{1,2},{2,1},{3,0},{4,7},{5,6},{6,5},{7,4},{8,11},{9,10},{10,... | collective-permute-start | bytes 12296 | tf_op jit(solution)/shard_map/ppermute | solution.py:49
  77.7 3.6 %collective-permute-start.18 = (f32[8,128]{1,0:T(8,128)S(1)}, f32[8,128]{1,0:T(8,128)S(1)}, u32[]{:S(2)}, u32[]{:S(2)}) collective-permute-start(f32[8,128]{1,0:T(8,128)S(1)} %add_add_fusion.3), channel_id=1, source_target_pairs={{0,1},{1,0},{2,3},{3,2},{4,5},{5,4},{6,7},{7,6},{8,9},{9,8},{10,11... | collective-permute-start | bytes 12296 | tf_op jit(solution)/shard_map/ppermute | solution.py:49
  78.4 5.1 %collective-permute-start.17 = (f32[8,128]{1,0:T(8,128)S(1)}, f32[8,128]{1,0:T(8,128)S(1)}, u32[]{:S(2)}, u32[]{:S(2)}) collective-permute-start(f32[8,128]{1,0:T(8,128)S(1)} %add_add_fusion.3), channel_id=1, source_target_pairs={{0,2},{1,3},{2,0},{3,1},{4,6},{5,7},{6,4},{7,5},{8,10},{9,11},{10,... | collective-permute-start | bytes 12296 | tf_op jit(solution)/shard_map/ppermute | solution.py:49
  83.5 4.1 %collective-permute-start.20 = (f32[8,128]{1,0:T(8,128)S(1)}, f32[8,128]{1,0:T(8,128)S(1)}, u32[]{:S(2)}, u32[]{:S(2)}) collective-permute-start(f32[8,128]{1,0:T(8,128)S(1)} %add_add_fusion.2), channel_id=1, source_target_pairs={{0,64},{64,0},{1,65},{65,1},{2,66},{66,2},{3,67},{67,3},{4,68},{68... | collective-permute-start | bytes 12296 | tf_op jit(solution)/shard_map/ppermute | solution.py:53
  (2 other events, 1.6 us)
